TPU v7x, 128 devices: a whole 4x4x4 slice. The times are simulated.
128 devices in a mesh: py: 4 (over y), px: 8 (over z_lo, x), pz: 4 (over z_hi, core).
Axes of the slice: x: 4, y: 4, z: 4 (z_hi: 2, z_lo: 2; z = z_hi * 2 + z_lo), core: 2. Of those that a mesh axis runs over, the one named last changes fastest.
Arguments:
- starting_state: float32 [512, 32, 128, 128], P('py', 'px', 'pz'), may hold values from 0.5 to 2
- scaled_conductivity: float32 [512, 32, 128, 128], P('py', 'px', 'pz'), may hold values from 0.03 to 0.15
- scaled_heat_supply: float32 [512, 32, 128, 128], P('py', 'px', 'pz'), may hold values from -0.2 to 0.2
Outputs:
- normalised_result: float32 [512, 32, 128, 128], P('py', 'px', 'pz')
- temperature_end: float32 [512, 32, 128, 128], P('py', 'px', 'pz')
All inputs are finite; a program needn't handle non-finite values.
Results may differ from a plain program's by a relative error of at most 0.00002.
Values sent between devices are 32-bit elements; how exact they have to be, the bound alone decides.
No kernel may reach another device: no remote copies, remote signals or barrier semaphores. Data moves between devices by JAX's collectives and lax.ppermute only.
A program may use at most 128 MiB of HBM per device.

v0:
```python
import jax
import jax.numpy as jnp
from jax import lax
from jax.sharding import PartitionSpec as P

STEPS = 4


def extended(array, sides, width):
    edges = {}
    for axis, dim in sides:
        devices, length = (lax.axis_size(axis), array.shape[dim])
        up = [(i, (i + 1) % devices) for i in range(devices - 1)]
        last = lax.slice_in_dim(array, length - width, length, axis=dim)
        initial = lax.slice_in_dim(array, 0, width, axis=dim)
        edges[dim] = (
            lax.ppermute(last, axis, up),
            lax.ppermute(initial, axis, [(b, a) for a, b in up]),
        )
    done = []
    for _, dim in sides:
        low, high = edges[dim]
        around = [(width, width) if d in done else (0, 0) for d in range(array.ndim)]
        array = jnp.concatenate([jnp.pad(low, around), array, jnp.pad(high, around)], axis=dim)
        done.append(dim)
    return array


def interior_points(values, dims):
    for coordinate_axis in dims:
        values = lax.slice_in_dim(
            values, 1, values.shape[coordinate_axis] - 1, axis=coordinate_axis
        )
    return values


def boundary_layer(values, coordinate_axis, start, dims):
    others = [other for other in dims if other != coordinate_axis]
    values = interior_points(values, others)
    return lax.slice_in_dim(
        values, start, start + values.shape[coordinate_axis] - 2, axis=coordinate_axis
    )


def conduction_timestep(framed_thermal_lattice, scaled_conductivity, scaled_heat_supply):
    central_point = interior_points(framed_thermal_lattice, (0, 1, 2))
    preceding_neighbour = [
        boundary_layer(framed_thermal_lattice, coordinate_axis, 0, (0, 1, 2))
        for coordinate_axis in (0, 1, 2)
    ]
    following_neighbour = [
        boundary_layer(framed_thermal_lattice, coordinate_axis, 2, (0, 1, 2))
        for coordinate_axis in (0, 1, 2)
    ]
    spread = (
        preceding_neighbour[0]
        + following_neighbour[0]
        + preceding_neighbour[1]
        + following_neighbour[1]
        + preceding_neighbour[2]
        + following_neighbour[2]
        - 6.0 * central_point
    )
    return central_point + scaled_conductivity * spread + scaled_heat_supply


def body(starting_state, scaled_conductivity, scaled_heat_supply):
    for step in range(STEPS):
        framed_thermal_lattice = extended(starting_state, (("py", 0), ("px", 1), ("pz", 2)), 1)
        starting_state = conduction_timestep(
            framed_thermal_lattice, scaled_conductivity, scaled_heat_supply
        )
    row_number_total = starting_state.shape[1] * lax.axis_size("px")
    guess = 1.0
    moved = starting_state - guess
    totals, squares = lax.psum(
        (jnp.sum(moved, axis=1, keepdims=True), jnp.sum(moved * moved, axis=1, keepdims=True)), "px"
    )
    row_average = guess + totals / row_number_total
    deviation_rows = starting_state - row_average
    line_variance = squares / row_number_total - totals / row_number_total * (
        totals / row_number_total
    )
    normalised_result = deviation_rows * lax.rsqrt(line_variance + 0.0001)
    return (normalised_result, starting_state)


def solution(mesh):
    placed = (P("py", "px", "pz", None), P("py", "px", "pz", None), P("py", "px", "pz", None))
    return jax.shard_map(
        body,
        mesh=mesh,
        in_specs=placed,
        out_specs=(P("py", "px", "pz", None), P("py", "px", "pz", None)),
        check_vma=False,
    )
```

profile of v0, /device:TPU:1, one launch (start us, length us, event | category | flops | bytes accessed | tf_op | source)
XLA Modules:
  0.0 497.5 jit_solution(4713084273634273184)
XLA Ops:
  7.2 8.2 %copy.16 = f32[128,4,32,128]{3,0,2,1:T(8,128)S(1)} copy(f32[128,4,32,128]{3,2,1,0:T(8,128)} %param.3) | data formatting | bytes 16777216 | tf_op args[0]
  16.0 4.1 collective-permute-start.2
  21.4 6.3 %collective-permute-start.4 = (f32[128,4,1,128]{3,0,2,1:T(8,128)S(1)}, f32[128,4,1,128]{3,0,2,1:T(8,128)S(1)}, u32[]{:S(2)}, u32[]{:S(2)}) collective-permute-start(f32[128,4,1,128]{3,0,2,1:T(8,128)S(1)} %get-tuple-element.27), channel_id=1, source_target_pairs={{0,1},{1,2},{2,3},{4,5},{5,6},{6,7},{8,9},{9,10},{10,11},{12,13},{... | collective-permute-start | bytes 786440 | tf_op jit(solution)/shard_map/ppermute | solution.py:17
  27.7 1.9 collective-permute-start.5
  30.5 1.3 collective-permute-start.1
  31.8 32.3 %collective-permute-done.2 = f32[128,1,32,128]{3,0,2,1:T(8,128)S(1)} collective-permute-done((f32[128,1,32,128]{3,0,2,1:T(8,128)S(1)}, f32[128,1,32,128]{3,0,2,1:T(8,128)S(1)}, u32[]{:S(2)}, u32[]{:S(2)}) %collective-permute-start.2) | collective-permute-done | bytes 2097184 | tf_op jit(solution)/shard_map/ppermute | solution.py:17
  64.2 3.4 collective-permute-start
  68.7 2.0 collective-permute-done.4
  70.7 3.7 collective-permute-done.5
  74.4 29.5 %fusion.38 = f32[128,4,32,128]{3,0,2,1:T(8,128)} fusion(f32[128,4,32,128]{3,0,2,1:T(8,128)} %copy-done, f32[128,4,1,128]{3,0,2,1:T(8,128)S(1)} %collective-permute-done.5, f32[130,1,32,128]{3,0,2,1:T(8,128)S(1)} %pad.51, f32[130,1,32,128]{3,0,2,1:T(8,128)S(1)} %pad.50, f32[1,4,32,128]{3,0,2,1:T(1,128)S(1)} %collective-permute-done.1, ...), kind=kLoop, calls=%fused_computation.93 | loop fusion | flops 71303168 | bytes 38469632 | tf_op jit(solution)/shard_map/add | solution.py:64
  104.0 2.5 fusion.53
  106.5 1.4 collective-permute-start.8
  110.3 5.2 %collective-permute-start.10 = (f32[128,4,1,128]{3,0,2,1:T(8,128)S(1)}, f32[128,4,1,128]{3,0,2,1:T(8,128)S(1)}, u32[]{:S(2)}, u32[]{:S(2)}) collective-permute-start(f32[128,4,1,128]{3,0,2,1:T(8,128)S(1)} %get-tuple-element.21), channel_id=1, source_target_pairs={{0,1},{1,2},{2,3},{4,5},{5,6},{6,7},{8,9},{9,10},{10,11},{12,13},{... | collective-permute-start | bytes 786440 | tf_op jit(solution)/shard_map/ppermute | solution.py:17
  115.4 1.9 collective-permute-start.11
  117.4 1.3 fusion.52
  118.7 4.0 collective-permute-start.6
  122.7 30.5 %collective-permute-done.8 = f32[128,1,32,128]{3,0,2,1:T(8,128)S(1)} collective-permute-done((f32[128,1,32,128]{3,0,2,1:T(8,128)S(1)}, f32[128,1,32,128]{3,0,2,1:T(8,128)S(1)}, u32[]{:S(2)}, u32[]{:S(2)}) %collective-permute-start.8) | collective-permute-done | bytes 2097184 | tf_op jit(solution)/shard_map/ppermute | solution.py:17
  154.7 2.5 collective-permute-done.9
  158.2 3.4 collective-permute-done.11
  161.5 29.5 %fusion.27 = f32[128,4,32,128]{3,0,2,1:T(8,128)} fusion(f32[128,4,32,128]{3,0,2,1:T(8,128)} %fusion.38, f32[128,4,1,128]{3,0,2,1:T(8,128)S(1)} %collective-permute-done.11, f32[130,1,32,128]{3,0,2,1:T(8,128)S(1)} %pad.55, f32[130,1,32,128]{3,0,2,1:T(8,128)S(1)} %pad.54, f32[1,4,32,128]{3,0,2,1:T(1,128)S(1)} %collective-permute-done.7, ...), kind=kLoop, calls=%fused_computation.64 | loop fusion | flops 71303168 | bytes 38469632 | tf_op jit(solution)/shard_map/add | solution.py:64
  191.1 2.5 fusion.50
  193.6 1.8 collective-permute-start.14
  195.4 1.3 collective-permute-start.15
  197.8 3.9 collective-permute-start.16
  201.6 1.9 collective-permute-start.17
  203.6 1.3 fusion.49
  204.9 3.6 collective-permute-start.12
  208.5 30.4 %collective-permute-done.14 = f32[128,1,32,128]{3,0,2,1:T(8,128)S(1)} collective-permute-done((f32[128,1,32,128]{3,0,2,1:T(8,128)S(1)}, f32[128,1,32,128]{3,0,2,1:T(8,128)S(1)}, u32[]{:S(2)}, u32[]{:S(2)}) %collective-permute-start.14) | collective-permute-done | bytes 2097184 | tf_op jit(solution)/shard_map/ppermute | solution.py:17
  240.4 2.9 collective-permute-done.15
  243.5 1.5 collective-permute-done.13
  244.9 2.5 collective-permute-done.17
  247.4 29.5 %fusion.16 = f32[128,4,32,128]{3,0,2,1:T(8,128)} fusion(f32[128,4,32,128]{3,0,2,1:T(8,128)} %fusion.27, f32[128,4,1,128]{3,0,2,1:T(8,128)S(1)} %collective-permute-done.17, f32[130,1,32,128]{3,0,2,1:T(8,128)S(1)} %pad.59, f32[130,1,32,128]{3,0,2,1:T(8,128)S(1)} %pad.58, f32[1,4,32,128]{3,0,2,1:T(1,128)S(1)} %collective-permute-done.13, ...), kind=kLoop, calls=%fused_computation.35 | loop fusion | flops 71303168 | bytes 38469632 | tf_op jit(solution)/shard_map/add | solution.py:64
  276.9 2.5 fusion.46
  279.4 1.5 collective-permute-start.20
  283.3 2.1 collective-permute-start.22
  285.4 3.6 collective-permute-start.23
  289.1 1.3 fusion.47
  290.4 3.6 collective-permute-start.18
  294.0 29.5 %collective-permute-done.20 = f32[128,1,32,128]{3,0,2,1:T(8,128)S(1)} collective-permute-done((f32[128,1,32,128]{3,0,2,1:T(8,128)S(1)}, f32[128,1,32,128]{3,0,2,1:T(8,128)S(1)}, u32[]{:S(2)}, u32[]{:S(2)}) %collective-permute-start.20) | collective-permute-done | bytes 2097184 | tf_op jit(solution)/shard_map/ppermute | solution.py:17
  325.0 2.5 collective-permute-done.21
  327.5 1.5 pad.63
  329.0 2.3 collective-permute-done.23
  331.3 32.9 %add_reduce_fusion = (f32[128,32,128]{2,0,1:T(8,128)}, f32[128,32,128]{2,0,1:T(8,128)}, f32[128,4,32,128]{3,0,2,1:T(8,128)}) fusion(f32[128,4,32,128]{3,2,1,0:T(8,128)} %param.5, f32[128,4,32,128]{3,0,2,1:T(8,128)} %fusion.16, f32[128,4,1,128]{3,0,2,1:T(8,128)S(1)} %collective-permute-done.23, f32[130,1,32,128]{3,0,2,1:T(8,128)} %pad.63, ...), kind=kLoop, calls=%fused_computation.120 | loop fusion | flops 78643200 | bytes 42663936 | tf_op jit(solution)/shard_map/reduce_sum | solution.py:77
  364.2 11.6 %copy.25 = f32[128,4,32,128]{3,2,1,0:T(8,128)} copy(f32[128,4,32,128]{3,0,2,1:T(8,128)} %get-tuple-element.8) | data formatting | bytes 16777216
  375.9 95.2 %all-reduce.19.cloned.1.call-done = (f32[128,1,32,128]{3,0,2,1:T(8,128)}, f32[128,1,32,128]{3,0,2,1:T(8,128)}) async-done(((f32[128,1,32,128]{3,0,2,1:T(8,128)}, f32[128,1,32,128]{3,0,2,1:T(8,128)}), (f32[128,1,32,128]{3,0,2,1:T(8,128)}, f32[128,1,32,128]{3,0,2,1:T(8,128)})) %all-reduce.19.cloned.1.call-update) | async-done | bytes 4194320 | tf_op jit(solution)/shard_map/psum | solution.py:76
  471.0 5.1 %add_bitcast_fusion = (f32[128,32,128]{2,0,1:T(8,128)}, f32[128,32,128]{2,0,1:T(8,128)}) fusion(f32[128,1,32,128]{3,0,2,1:T(8,128)} %get-tuple-element.7, f32[128,1,32,128]{3,0,2,1:T(8,128)} %get-tuple-element.6), kind=kLoop, calls=%fused_computation.122 | loop fusion | flops 3145728 | bytes 8388608 | tf_op jit(solution)/shard_map/sub | solution.py:80
  476.1 6.1 %subtract_multiply_fusion = f32[128,4,32,128]{3,0,2,1:T(8,128)S(1)} fusion(f32[128,4,32,128]{3,0,2,1:T(8,128)} %get-tuple-element.8, f32[128,32,128]{2,0,1:T(8,128)} %get-tuple-element.34, f32[128,32,128]{2,0,1:T(8,128)} %get-tuple-element.33), kind=kLoop, calls=%fused_computation.119 | loop fusion | flops 4194304 | bytes 20971520 | tf_op jit(solution)/shard_map/mul | solution.py:84
  482.2 8.3 %copy.24 = f32[128,4,32,128]{3,2,1,0:T(8,128)} copy(f32[128,4,32,128]{3,0,2,1:T(8,128)S(1)} %subtract_multiply_fusion) | data formatting | bytes 16777216
  (34 shorter events, 15.2 us)
Async XLA Ops:
  7.2 463.9 %all-reduce.19.cloned.1.call-start = ((), (), s32[]{:S(2)}) async-start(), calls=%async_computation | async-start | bytes 8388608 | tf_op jit(solution)/shard_map/psum | solution.py:76
  15.4 52.9 %copy-start = (f32[128,4,32,128]{3,0,2,1:T(8,128)}, f32[128,4,32,128]{3,0,2,1:T(8,128)S(1)}, u32[]{:S(2)}) copy-start(f32[128,4,32,128]{3,0,2,1:T(8,128)S(1)} %copy.16) | copy-start | bytes 25165828
  16.0 48.2 %collective-permute-start.2 = (f32[128,1,32,128]{3,0,2,1:T(8,128)S(1)}, f32[128,1,32,128]{3,0,2,1:T(8,128)S(1)}, u32[]{:S(2)}, u32[]{:S(2)}) collective-permute-start(f32[128,1,32,128]{3,0,2,1:T(8,128)S(1)} %get-tuple-element.31), channel_id=1, source_target_pairs={{0,4},{4,8},{8,12},{12,16},{16,20},{20,24},{24,28},{1,5},{5,9},{9,... | collective-permute-start | bytes 6291464 | tf_op jit(solution)/shard_map/ppermute | solution.py:17
  20.0 48.1 %collective-permute-start.3 = (f32[128,1,32,128]{3,0,2,1:T(8,128)S(1)}, f32[128,1,32,128]{3,0,2,1:T(8,128)S(1)}, u32[]{:S(2)}, u32[]{:S(2)}) collective-permute-start(f32[128,1,32,128]{3,0,2,1:T(8,128)S(1)} %get-tuple-element.32), channel_id=1, source_target_pairs={{4,0},{8,4},{12,8},{16,12},{20,16},{24,20},{28,24},{5,1},{9,5},{13... | collective-permute-start | bytes 6291464 | tf_op jit(solution)/shard_map/ppermute | solution.py:18
  21.4 49.3 %collective-permute-start.4 = (f32[128,4,1,128]{3,0,2,1:T(8,128)S(1)}, f32[128,4,1,128]{3,0,2,1:T(8,128)S(1)}, u32[]{:S(2)}, u32[]{:S(2)}) collective-permute-start(f32[128,4,1,128]{3,0,2,1:T(8,128)S(1)} %get-tuple-element.27), channel_id=1, source_target_pairs={{0,1},{1,2},{2,3},{4,5},{5,6},{6,7},{8,9},{9,10},{10,11},{12,13},{... | collective-permute-start | bytes 786440 | tf_op jit(solution)/shard_map/ppermute | solution.py:17
  27.7 46.7 %collective-permute-start.5 = (f32[128,4,1,128]{3,0,2,1:T(8,128)S(1)}, f32[128,4,1,128]{3,0,2,1:T(8,128)S(1)}, u32[]{:S(2)}, u32[]{:S(2)}) collective-permute-start(f32[128,4,1,128]{3,0,2,1:T(8,128)S(1)} %get-tuple-element.28), channel_id=1, source_target_pairs={{1,0},{2,1},{3,2},{5,4},{6,5},{7,6},{9,8},{10,9},{11,10},{13,12},{... | collective-permute-start | bytes 786440 | tf_op jit(solution)/shard_map/ppermute | solution.py:18
  30.5 37.8 %collective-permute-start.1 = (f32[1,4,32,128]{3,0,2,1:T(1,128)S(1)}, f32[1,4,32,128]{3,0,2,1:T(1,128)S(1)}, u32[]{:S(2)}, u32[]{:S(2)}) collective-permute-start(f32[1,4,32,128]{3,0,2,1:T(1,128)S(1)} %bitcast.11), channel_id=1, source_target_pairs={{32,0},{64,32},{96,64},{33,1},{65,33},{97,65},{34,2},{66,34},{98,6... | collective-permute-start | bytes 196616 | tf_op jit(solution)/shard_map/ppermute | solution.py:18
  64.2 4.5 collective-permute-start
  106.5 46.7 %collective-permute-start.8 = (f32[128,1,32,128]{3,0,2,1:T(8,128)S(1)}, f32[128,1,32,128]{3,0,2,1:T(8,128)S(1)}, u32[]{:S(2)}, u32[]{:S(2)}) collective-permute-start(f32[128,1,32,128]{3,0,2,1:T(8,128)S(1)} %get-tuple-element.25), channel_id=1, source_target_pairs={{0,4},{4,8},{8,12},{12,16},{16,20},{20,24},{24,28},{1,5},{5,9},{9,... | collective-permute-start | bytes 6291464 | tf_op jit(solution)/shard_map/ppermute | solution.py:17
  107.9 49.3 %collective-permute-start.9 = (f32[128,1,32,128]{3,0,2,1:T(8,128)S(1)}, f32[128,1,32,128]{3,0,2,1:T(8,128)S(1)}, u32[]{:S(2)}, u32[]{:S(2)}) collective-permute-start(f32[128,1,32,128]{3,0,2,1:T(8,128)S(1)} %get-tuple-element.26), channel_id=1, source_target_pairs={{4,0},{8,4},{12,8},{16,12},{20,16},{24,20},{28,24},{5,1},{9,5},{13... | collective-permute-start | bytes 6291464 | tf_op jit(solution)/shard_map/ppermute | solution.py:18
  110.3 47.9 %collective-permute-start.10 = (f32[128,4,1,128]{3,0,2,1:T(8,128)S(1)}, f32[128,4,1,128]{3,0,2,1:T(8,128)S(1)}, u32[]{:S(2)}, u32[]{:S(2)}) collective-permute-start(f32[128,4,1,128]{3,0,2,1:T(8,128)S(1)} %get-tuple-element.21), channel_id=1, source_target_pairs={{0,1},{1,2},{2,3},{4,5},{5,6},{6,7},{8,9},{9,10},{10,11},{12,13},{... | collective-permute-start | bytes 786440 | tf_op jit(solution)/shard_map/ppermute | solution.py:17
  115.4 46.1 %collective-permute-start.11 = (f32[128,4,1,128]{3,0,2,1:T(8,128)S(1)}, f32[128,4,1,128]{3,0,2,1:T(8,128)S(1)}, u32[]{:S(2)}, u32[]{:S(2)}) collective-permute-start(f32[128,4,1,128]{3,0,2,1:T(8,128)S(1)} %get-tuple-element.22), channel_id=1, source_target_pairs={{1,0},{2,1},{3,2},{5,4},{6,5},{7,6},{9,8},{10,9},{11,10},{13,12},{... | collective-permute-start | bytes 786440 | tf_op jit(solution)/shard_map/ppermute | solution.py:18
  118.7 38.7 %collective-permute-start.6 = (f32[1,4,32,128]{3,0,2,1:T(1,128)S(1)}, f32[1,4,32,128]{3,0,2,1:T(1,128)S(1)}, u32[]{:S(2)}, u32[]{:S(2)}) collective-permute-start(f32[1,4,32,128]{3,0,2,1:T(1,128)S(1)} %get-tuple-element.23), channel_id=1, source_target_pairs={{0,32},{32,64},{64,96},{1,33},{33,65},{65,97},{2,34},{34,66},{66,9... | collective-permute-start | bytes 196616 | tf_op jit(solution)/shard_map/ppermute | solution.py:17
  153.2 5.0 %collective-permute-start.7 = (f32[1,4,32,128]{3,0,2,1:T(1,128)S(1)}, f32[1,4,32,128]{3,0,2,1:T(1,128)S(1)}, u32[]{:S(2)}, u32[]{:S(2)}) collective-permute-start(f32[1,4,32,128]{3,0,2,1:T(1,128)S(1)} %get-tuple-element.24), channel_id=1, source_target_pairs={{32,0},{64,32},{96,64},{33,1},{65,33},{97,65},{34,2},{66,34},{98,6... | collective-permute-start | bytes 196616 | tf_op jit(solution)/shard_map/ppermute | solution.py:18
  193.6 45.3 %collective-permute-start.14 = (f32[128,1,32,128]{3,0,2,1:T(8,128)S(1)}, f32[128,1,32,128]{3,0,2,1:T(8,128)S(1)}, u32[]{:S(2)}, u32[]{:S(2)}) collective-permute-start(f32[128,1,32,128]{3,0,2,1:T(8,128)S(1)} %get-tuple-element.19), channel_id=1, source_target_pairs={{0,4},{4,8},{8,12},{12,16},{16,20},{20,24},{24,28},{1,5},{5,9},{9,... | collective-permute-start | bytes 6291464 | tf_op jit(solution)/shard_map/ppermute | solution.py:17
  195.4 47.9 %collective-permute-start.15 = (f32[128,1,32,128]{3,0,2,1:T(8,128)S(1)}, f32[128,1,32,128]{3,0,2,1:T(8,128)S(1)}, u32[]{:S(2)}, u32[]{:S(2)}) collective-permute-start(f32[128,1,32,128]{3,0,2,1:T(8,128)S(1)} %get-tuple-element.20), channel_id=1, source_target_pairs={{4,0},{8,4},{12,8},{16,12},{20,16},{24,20},{28,24},{5,1},{9,5},{13... | collective-permute-start | bytes 6291464 | tf_op jit(solution)/shard_map/ppermute | solution.py:18
  197.8 47.1 %collective-permute-start.16 = (f32[128,4,1,128]{3,0,2,1:T(8,128)S(1)}, f32[128,4,1,128]{3,0,2,1:T(8,128)S(1)}, u32[]{:S(2)}, u32[]{:S(2)}) collective-permute-start(f32[128,4,1,128]{3,0,2,1:T(8,128)S(1)} %get-tuple-element.15), channel_id=1, source_target_pairs={{0,1},{1,2},{2,3},{4,5},{5,6},{6,7},{8,9},{9,10},{10,11},{12,13},{... | collective-permute-start | bytes 786440 | tf_op jit(solution)/shard_map/ppermute | solution.py:17
  201.6 45.8 %collective-permute-start.17 = (f32[128,4,1,128]{3,0,2,1:T(8,128)S(1)}, f32[128,4,1,128]{3,0,2,1:T(8,128)S(1)}, u32[]{:S(2)}, u32[]{:S(2)}) collective-permute-start(f32[128,4,1,128]{3,0,2,1:T(8,128)S(1)} %get-tuple-element.16), channel_id=1, source_target_pairs={{1,0},{2,1},{3,2},{5,4},{6,5},{7,6},{9,8},{10,9},{11,10},{13,12},{... | collective-permute-start | bytes 786440 | tf_op jit(solution)/shard_map/ppermute | solution.py:18
  204.9 38.6 %collective-permute-start.12 = (f32[1,4,32,128]{3,0,2,1:T(1,128)S(1)}, f32[1,4,32,128]{3,0,2,1:T(1,128)S(1)}, u32[]{:S(2)}, u32[]{:S(2)}) collective-permute-start(f32[1,4,32,128]{3,0,2,1:T(1,128)S(1)} %get-tuple-element.17), channel_id=1, source_target_pairs={{0,32},{32,64},{64,96},{1,33},{33,65},{65,97},{2,34},{34,66},{66,9... | collective-permute-start | bytes 196616 | tf_op jit(solution)/shard_map/ppermute | solution.py:17
  238.9 6.0 %collective-permute-start.13 = (f32[1,4,32,128]{3,0,2,1:T(1,128)S(1)}, f32[1,4,32,128]{3,0,2,1:T(1,128)S(1)}, u32[]{:S(2)}, u32[]{:S(2)}) collective-permute-start(f32[1,4,32,128]{3,0,2,1:T(1,128)S(1)} %get-tuple-element.18), channel_id=1, source_target_pairs={{32,0},{64,32},{96,64},{33,1},{65,33},{97,65},{34,2},{66,34},{98,6... | collective-permute-start | bytes 196616 | tf_op jit(solution)/shard_map/ppermute | solution.py:18
  279.4 44.1 %collective-permute-start.20 = (f32[128,1,32,128]{3,0,2,1:T(8,128)S(1)}, f32[128,1,32,128]{3,0,2,1:T(8,128)S(1)}, u32[]{:S(2)}, u32[]{:S(2)}) collective-permute-start(f32[128,1,32,128]{3,0,2,1:T(8,128)S(1)} %get-tuple-element.11), channel_id=1, source_target_pairs={{0,4},{4,8},{8,12},{12,16},{16,20},{20,24},{24,28},{1,5},{5,9},{9,... | collective-permute-start | bytes 6291464 | tf_op jit(solution)/shard_map/ppermute | solution.py:17
  280.9 46.5 %collective-permute-start.21 = (f32[128,1,32,128]{3,0,2,1:T(8,128)S(1)}, f32[128,1,32,128]{3,0,2,1:T(8,128)S(1)}, u32[]{:S(2)}, u32[]{:S(2)}) collective-permute-start(f32[128,1,32,128]{3,0,2,1:T(8,128)S(1)} %get-tuple-element.12), channel_id=1, source_target_pairs={{4,0},{8,4},{12,8},{16,12},{20,16},{24,20},{28,24},{5,1},{9,5},{13... | collective-permute-start | bytes 6291464 | tf_op jit(solution)/shard_map/ppermute | solution.py:18
  283.3 45.7 %collective-permute-start.22 = (f32[128,4,1,128]{3,0,2,1:T(8,128)S(1)}, f32[128,4,1,128]{3,0,2,1:T(8,128)S(1)}, u32[]{:S(2)}, u32[]{:S(2)}) collective-permute-start(f32[128,4,1,128]{3,0,2,1:T(8,128)S(1)} %get-tuple-element.9), channel_id=1, source_target_pairs={{0,1},{1,2},{2,3},{4,5},{5,6},{6,7},{8,9},{9,10},{10,11},{12,13},{... | collective-permute-start | bytes 786440 | tf_op jit(solution)/shard_map/ppermute | solution.py:17
  285.4 45.9 %collective-permute-start.23 = (f32[128,4,1,128]{3,0,2,1:T(8,128)S(1)}, f32[128,4,1,128]{3,0,2,1:T(8,128)S(1)}, u32[]{:S(2)}, u32[]{:S(2)}) collective-permute-start(f32[128,4,1,128]{3,0,2,1:T(8,128)S(1)} %get-tuple-element.10), channel_id=1, source_target_pairs={{1,0},{2,1},{3,2},{5,4},{6,5},{7,6},{9,8},{10,9},{11,10},{13,12},{... | collective-permute-start | bytes 786440 | tf_op jit(solution)/shard_map/ppermute | solution.py:18
  290.4 38.6 %collective-permute-start.18 = (f32[1,4,32,128]{3,0,2,1:T(1,128)S(1)}, f32[1,4,32,128]{3,0,2,1:T(1,128)S(1)}, u32[]{:S(2)}, u32[]{:S(2)}) collective-permute-start(f32[1,4,32,128]{3,0,2,1:T(1,128)S(1)} %get-tuple-element.13), channel_id=1, source_target_pairs={{0,32},{32,64},{64,96},{1,33},{33,65},{65,97},{2,34},{34,66},{66,9... | collective-permute-start | bytes 196616 | tf_op jit(solution)/shard_map/ppermute | solution.py:17
  323.5 5.5 %collective-permute-start.19 = (f32[1,4,32,128]{3,0,2,1:T(1,128)S(1)}, f32[1,4,32,128]{3,0,2,1:T(1,128)S(1)}, u32[]{:S(2)}, u32[]{:S(2)}) collective-permute-start(f32[1,4,32,128]{3,0,2,1:T(1,128)S(1)} %get-tuple-element.14), channel_id=1, source_target_pairs={{32,0},{64,32},{96,64},{33,1},{65,33},{97,65},{34,2},{66,34},{98,6... | collective-permute-start | bytes 196616 | tf_op jit(solution)/shard_map/ppermute | solution.py:18
Sparse Core Ops, SparseCore 0:
  364.4 106.6 all-reduce.18
where the time goes:
time: 504 us; the launch traced here: 497 us
  waiting for transfers between devices  243 us (48%)
  other arithmetic  133 us (26%)
  starting transfers between devices  60.7 us (12%)
  local copies, waits for them, and re-layouts  47 us (9%)
  between operations  14.6 us (3%)
    ppermute x12, waiting for transfers between devices, extended(): lax.ppermute(last, axis, up)  125 us
    psum x1, waiting for transfers between devices, body(): lax.psum((jnp.sum(moved, axis=1, keepdims=True), jnp.sum(moved * moved, a...  95.2 us
    add x3, other arithmetic, conduction_timestep(): return central_point + scaled_conductivity * spread + scaled_heat_supply  88.6 us
    ppermute x12, starting transfers between devices, extended(): lax.ppermute(last, axis, up)  40.9 us
    reduce_sum x1, other arithmetic, body(): jnp.sum(moved, axis=1, keepdims=True)  32.9 us
    unnamed x5, local copies, waits for them, and re-layouts  28.1 us
    ppermute x12, waiting for transfers between devices, extended(): lax.ppermute(initial, axis, [(b, a) for a, b in up])  22.4 us
    ppermute x12, starting transfers between devices, extended(): lax.ppermute(initial, axis, [(b, a) for a, b in up])  19.7 us
  transfers between devices with their start and end apart: 25, of which 17 were waited for; matrix products, arithmetic and copies ran while one was open for 5% of the time, Pallas kernels for 0%

commit v1 on v0

v1 whole, which is shorter than its diff:
```python
import functools

import jax
import jax.numpy as jnp
from jax import lax
from jax.experimental import pallas as pl
from jax.experimental.pallas import tpu as pltpu
from jax.sharding import PartitionSpec as P


STEPS = 4


def ring(value, axis, shift):
    devices = lax.axis_size(axis)
    return lax.ppermute(value, axis, [(i, (i + shift) % devices) for i in range(devices)])


def send_up(value, axis):
    return ring(value, axis, 1)


def send_down(value, axis):
    return ring(value, axis, -1)


def swap(value, mask):
    return lax.ppermute(value, "px", [(i, i ^ mask) for i in range(lax.axis_size("px"))])


def pair_swap(value, axis, odd):
    devices = lax.axis_size(axis)
    return lax.ppermute(value, axis, [(i, ((i - odd) ^ 1) + odd) for i in range(odd, devices - odd)])


def exchange(faces, axis):
    even = pair_swap(faces[0], axis, 0)
    odd = pair_swap(faces[1], axis, 1)
    return even, odd


def z_exchange(faces):
    last_x, last_z = lax.axis_size("px") - 1, lax.axis_size("pz") - 1
    flat = lambda x, z: x * (last_z + 1) + z
    direct = [(flat(x, a), flat(x, b)) for x in range(1, last_x) for a, b in ((1, 2), (2, 1))]
    out, back = [], []
    for x, over in ((0, last_x // 2 + 1), (last_x, last_x // 2)):
        out += [(flat(x, 1), flat(over, last_z)), (flat(x, 2), flat(over, 0))]
        back += [(flat(over, last_z), flat(x, 2)), (flat(over, 0), flat(x, 1))]
    even = pair_swap(faces[0], "pz", 0)
    odd = lax.ppermute(faces[1], ("px", "pz"), direct + out)
    over = lax.ppermute(odd, ("px", "pz"), back)
    return even, odd, over


def by_parity(axis, low, high):
    even = lax.axis_index(axis) % 2 == 0
    return jnp.where(even, high, low), jnp.where(even, low, high)


def inside(axis):
    at = lax.axis_index(axis)
    below = jnp.where(at > 0, 1.0, 0.0).astype(jnp.float32)
    above = jnp.where(at < lax.axis_size(axis) - 1, 1.0, 0.0).astype(jnp.float32)
    return below, above


def update_rows(refs, store, block, width, height, is_first, is_last, outer):
    u, before, after, low, high, xe, xo, ze, zo, zo_over, k, s = refs
    x_at, z_at = lax.axis_index("px"), lax.axis_index("pz")
    x_outer = (x_at == 0) | (x_at == lax.axis_size("px") - 1)
    z_inner = ((z_at > 0) & (z_at < lax.axis_size("pz") - 1)).astype(jnp.float32)
    x_even = lax.axis_index("px") % 2 == 0
    z_even = lax.axis_index("pz") % 2 == 0
    y_below, y_above = inside("py")
    sub = lax.broadcasted_iota(jnp.int32, (height, u.shape[-1]), 0)
    at_low = sub == 0
    at_high = sub == height - 1

    def one_row(r, below, above):
        for x in range(width):
            c = u[r, x]
            left = jnp.where(x_even, xo[r], xe[r]) if x == 0 else u[r, x - 1]
            right = jnp.where(x_even, xe[r], xo[r]) if x == width - 1 else u[r, x + 1]
            line = r * width + x
            z_first = ze[pl.ds(line, 1), :]
            z_second = jnp.where(x_outer, zo_over[pl.ds(line, 1), :], zo[pl.ds(line, 1), :]) * z_inner
            zd = jnp.where(at_low, jnp.where(z_even, z_second, z_first), pltpu.roll(c, 1, 0))
            zu = jnp.where(at_high, jnp.where(z_even, z_first, z_second), pltpu.roll(c, height - 1, 0))
            spread = below(x) + above(x) + left + right + zd + zu - 6.0 * c
            store(r, x, c + k[r, x] * spread + s[r, x])

    def lowest(x):
        return jnp.where(is_first, low[0, x] * y_below if outer[0] else low[0, x], before[0, x])

    def highest(x):
        return jnp.where(is_last, high[0, x] * y_above if outer[1] else high[0, x], after[0, x])

    one_row(0, lowest, lambda x: u[1, x])

    def middle(r, carry):
        one_row(r, lambda x: u[r - 1, x], lambda x: u[r + 1, x])
        return carry

    lax.fori_loop(1, block - 1, middle, 0)
    one_row(block - 1, lambda x: u[block - 2, x], highest)


def pick_body(low, high, even_face, odd_face):
    even_face[...], odd_face[...] = by_parity("px", low[:, 0], high[:, 0])


def pick(u, row0, count):
    _, width, height, lanes = u.shape
    block = min(16, count)
    first = row0 // block
    face = jax.ShapeDtypeStruct((count, height, lanes), jnp.float32)
    return pl.pallas_call(
        pick_body,
        grid=(count // block,),
        in_specs=[
            pl.BlockSpec((block, 1, height, lanes), lambda i: (first + i, 0, 0, 0)),
            pl.BlockSpec((block, 1, height, lanes), lambda i: (first + i, width - 1, 0, 0)),
        ],
        out_specs=[pl.BlockSpec((block, height, lanes), lambda i: (i, 0, 0))] * 2,
        out_shape=[face, face],
        compiler_params=pltpu.CompilerParams(dimension_semantics=("arbitrary",)),
        name="pick",
    )(u, u)


def step_body(*refs, block, blocks, extra, y_face, outer):
    ins, outs = refs[:12], refs[12 + extra :]
    width, height = ins[0].shape[1:3]
    i = pl.program_id(0)
    kept = {}

    def store(r, x, value):
        outs[0][r, x] = value
        if x == 0:
            kept["low"] = value
        if x == width - 1:
            outs[3][r], outs[4][r] = by_parity("px", kept["low"], value)
        line = pl.ds(r * width + x, 1)
        outs[1][line, :], outs[2][line, :] = by_parity("pz", value[0:1], value[height - 1 : height])

    update_rows(ins, store, block, width, height, i == 0, i == blocks - 1, outer)
    if y_face == "low":

        @pl.when(i == 0)
        def _():
            outs[5][0] = outs[0][0]

    if y_face == "high":

        @pl.when(i == blocks - 1)
        def _():
            outs[5][0] = outs[0][block - 1]


def field_specs(row0, offset, rows, block, width, height, lanes, low, high, at):
    full = (block, width, height, lanes)
    one = (1, width, height, lanes)
    first = row0 // block
    extra = offset // block
    return [
        pl.BlockSpec(full, lambda *g: (first + at(*g), 0, 0, 0)),
        pl.BlockSpec(one, lambda *g: (jnp.maximum(row0 + at(*g) * block - 1, 0), 0, 0, 0)),
        pl.BlockSpec(one, lambda *g: (jnp.minimum(row0 + (at(*g) + 1) * block, rows - 1), 0, 0, 0)),
        pl.BlockSpec(one, lambda *g: (low, 0, 0, 0)),
        pl.BlockSpec(one, lambda *g: (high, 0, 0, 0)),
        pl.BlockSpec((block, height, lanes), lambda *g: (extra + at(*g), 0, 0)),
        pl.BlockSpec((block, height, lanes), lambda *g: (extra + at(*g), 0, 0)),
        pl.BlockSpec((block * width, lanes), lambda *g: (first + at(*g), 0)),
        pl.BlockSpec((block * width, lanes), lambda *g: (first + at(*g), 0)),
        pl.BlockSpec((block * width, lanes), lambda *g: (first + at(*g), 0)),
        pl.BlockSpec(full, lambda *g: (first + at(*g), 0, 0, 0)),
        pl.BlockSpec(full, lambda *g: (first + at(*g), 0, 0, 0)),
    ]


def advance(u, halos, low, high, k, s, row0, count, offset, targets, block):
    rows, width, height, lanes = u.shape
    block = min(block, count)
    blocks = count // block
    first = row0 // block
    y_face = "low" if row0 == 0 else "high" if row0 + count == rows else None
    specs = field_specs(row0, offset, rows, block, width, height, lanes, low[1], high[1], lambda i: i)
    operands = [u, u, u, low[0], high[0], *halos, k, s]
    aliases = {}
    for number, target in enumerate(targets):
        aliases[len(operands)] = number
        operands.append(target)
        specs.append(pl.BlockSpec(memory_space=pl.ANY))
    face = pl.BlockSpec((block, height, lanes), lambda i: (i, 0, 0))
    edge = pl.BlockSpec((block * width, lanes), lambda i: (first + i, 0))
    out_specs = [pl.BlockSpec((block, width, height, lanes), lambda i: (first + i, 0, 0, 0)), edge, edge, face, face]
    shapes = [u.shape] + [(rows * width, lanes)] * 2 + [(count, height, lanes)] * 2
    if y_face:
        out_specs.append(pl.BlockSpec((1, width, height, lanes), lambda i: (0, 0, 0, 0)))
        shapes.append((1, width, height, lanes))
    return pl.pallas_call(
        functools.partial(
            step_body,
            block=block,
            blocks=blocks,
            extra=len(targets),
            y_face=y_face,
            outer=(row0 == 0, row0 + count == rows),
        ),
        grid=(blocks,),
        in_specs=specs,
        out_specs=out_specs,
        out_shape=[jax.ShapeDtypeStruct(shape, jnp.float32) for shape in shapes],
        input_output_aliases=aliases,
        compiler_params=pltpu.CompilerParams(dimension_semantics=("arbitrary",)),
        name="advance",
    )(*operands)


def final_body(bits, *refs, block, per_part, extra, outer):
    ins, outs = refs[:12], refs[12 + extra :]
    width, height = ins[0].shape[1:3]
    p, i = pl.program_id(0), pl.program_id(1)
    at = jnp.where(p == 0, 1 - bits[0], bits[0]) * per_part + i
    result, send, keep = outs
    totals = {}

    def stats_to(target):
        def store(r, x, value):
            result[r, x] = value
            moved = value - 1.0
            totals["sum"] = moved if x == 0 else totals["sum"] + moved
            totals["square"] = moved * moved if x == 0 else totals["square"] + moved * moved
            if x == width - 1:
                target[0, r] = totals["sum"]
                target[1, r] = totals["square"]

        update_rows(ins, store, block, width, height, at == 0, at == 2 * per_part - 1, outer)

    @pl.when(p == 0)
    def _():
        stats_to(send)

    @pl.when(p == 1)
    def _():
        stats_to(keep)


def finish(u, halos, low, high, k, s, row0, count, offset, target, after, bits, block):
    rows, width, height, lanes = u.shape
    block = min(block, count // 2)
    per_part = count // 2 // block
    first = row0 // block

    def at(p, i, bits):
        return jnp.where(p == 0, 1 - bits[0], bits[0]) * per_part + i

    specs = field_specs(row0, offset, rows, block, width, height, lanes, low[1], high[1], at)
    operands = [bits, u, u, u, low[0], high[0], *halos, k, s]
    aliases = {}
    extra = list(after)
    if target is not None:
        aliases = {len(operands) + len(extra): 0}
        extra.append(target)
    operands += extra
    specs += [pl.BlockSpec(memory_space=pl.ANY)] * len(extra)
    part = (2, block, height, lanes)
    out_specs = [
        pl.BlockSpec((block, width, height, lanes), lambda *g: (first + at(*g), 0, 0, 0)),
        pl.BlockSpec(part, lambda p, i, m: (0, jnp.where(p == 0, i, per_part - 1), 0, 0)),
        pl.BlockSpec(part, lambda p, i, m: (0, jnp.where(p == 0, 0, i), 0, 0)),
    ]
    sums = (2, count // 2, height, lanes)
    return pl.pallas_call(
        functools.partial(
            final_body, block=block, per_part=per_part, extra=len(extra), outer=(row0 == 0, row0 + count == rows)
        ),
        grid_spec=pltpu.PrefetchScalarGridSpec(
            num_scalar_prefetch=1, grid=(2, per_part), in_specs=specs, out_specs=out_specs
        ),
        out_shape=[jax.ShapeDtypeStruct(shape, jnp.float32) for shape in (u.shape, sums, sums)],
        input_output_aliases=aliases,
        compiler_params=pltpu.CompilerParams(dimension_semantics=("arbitrary", "arbitrary")),
        name="finish",
    )(*operands)


def scale_body(bits, u, own, other, *refs, inverse):
    result = refs[-1]
    width = u.shape[1]

    def scaled(sums):
        def one_row(r, carry):
            mean = sums[0, 0, r] * inverse
            factor = lax.rsqrt(sums[0, 1, r] * inverse - mean * mean + 0.0001)
            mean = mean + 1.0
            for x in range(width):
                result[r, x] = (u[r, x] - mean) * factor
            return carry

        lax.fori_loop(0, u.shape[0], one_row, 0)

    @pl.when(pl.program_id(0) == 0)
    def _():
        scaled(own)

    @pl.when(pl.program_id(0) == 1)
    def _():
        scaled(other)


def scale(u, own, other, bits, row0, target, line_length):
    _, width, height, lanes = u.shape
    pieces, _, block = own.shape[:3]
    first = row0 // block

    def at(p, i, bits):
        return first + jnp.where(p == 0, bits[0], 1 - bits[0]) * pieces + (bits[1] ^ i if pieces > 1 else 0)

    full = pl.BlockSpec((block, width, height, lanes), lambda *g: (at(*g), 0, 0, 0))
    part = (1, 2, block, height, lanes)
    specs = [
        full,
        pl.BlockSpec(part, lambda p, i, m: (jnp.where(p == 0, i, pieces - 1), 0, 0, 0, 0)),
        pl.BlockSpec(part, lambda p, i, m: (jnp.where(p == 0, 0, i), 0, 0, 0, 0)),
    ]
    operands = [bits, u, own, other]
    aliases = {}
    if target is not None:
        aliases = {len(operands): 0}
        operands.append(target)
        specs.append(pl.BlockSpec(memory_space=pl.ANY))
    return pl.pallas_call(
        functools.partial(scale_body, inverse=1.0 / line_length),
        grid_spec=pltpu.PrefetchScalarGridSpec(num_scalar_prefetch=1, grid=(2, pieces), in_specs=specs, out_specs=full),
        out_shape=jax.ShapeDtypeStruct(u.shape, jnp.float32),
        input_output_aliases=aliases,
        compiler_params=pltpu.CompilerParams(dimension_semantics=("arbitrary", "arbitrary")),
        name="scale",
    )(*operands)


def body(u, k, s):
    rows, width, height, lanes = u.shape
    half, quarter = rows // 2, rows // 4
    place = lax.axis_index("px").astype(jnp.int32)
    column = place & 3
    right = column >> 1
    middle = (column ^ right) & 1
    by_near = jnp.stack([middle, right])
    by_far = jnp.stack([right, middle])

    x_halos = {row0: (exchange(pick(u, row0, half), "px"), half) for row0 in (0, half)}
    edges = by_parity("pz", u[:, :, 0].reshape(-1, lanes), u[:, :, height - 1].reshape(-1, lanes))
    z_halos = z_exchange(edges)
    y_low = (send_up(u[rows - 1 :], "py"), 0)
    y_high = (send_down(u[:1], "py"), 0)
    for step in range(1, STEPS):
        count = half if step < STEPS - 1 else quarter
        targets = ()
        arrived = {}
        for row0 in range(0, rows, count):
            received, length = x_halos[row0 // half * half]
            low = y_low if row0 == 0 else (u, row0 - 1)
            high = y_high if row0 + count == rows else (u, row0 + count)
            out = advance(u, (*received, *z_halos), low, high, k, s, row0, count, row0 % length, targets, 16)
            targets = out[:3]
            arrived[row0] = (exchange(out[3:5], "px"), count)
            if row0 == 0:
                next_high = (send_down(out[5], "py"), 0)
            if row0 + count == rows:
                next_low = (send_up(out[5], "py"), 0)
        u = targets[0]
        z_halos = z_exchange(targets[1:])
        x_halos, y_low, y_high = arrived, next_low, next_high

    def x_first(total, masks, bit):
        rows_left = total.shape[1] // 2
        part = lambda b: lax.dynamic_slice_in_dim(total, b * rows_left, rows_left, axis=1)
        total = part(bit) + swap(part(1 - bit), masks[1])
        total = total + swap(total, 4)
        total = jnp.stack([total, swap(total, masks[1])])
        return total, swap(total, masks[0])

    end = None
    sums = []
    for number, row0 in enumerate(range(0, rows, quarter)):
        masks, bits = ((3, 1), by_far) if number % 2 else ((1, 3), by_near)
        low = y_low if row0 == 0 else (u, row0 - 1)
        high = y_high if row0 + quarter == rows else (u, row0 + quarter)
        end, send, keep = finish(u, (*x_halos[row0][0], *z_halos), low, high, k, s, row0, quarter, 0, end, (), bits, 8)
        sums.append((*x_first(keep + swap(send, masks[0]), masks, bits[1]), bits))
    result = None
    for number, (own, other, bits) in enumerate(sums):
        result = scale(end, own, other, bits, number * quarter, result, width * lax.axis_size("px"))
    return result, end


def solution(mesh):
    placed = P("py", "px", "pz", None)
    return jax.shard_map(
        body, mesh=mesh, in_specs=(placed, placed, placed), out_specs=(placed, placed), check_vma=False
    )
```

time: 504 us -> 341 us (0.68)
  other arithmetic: 133 us -> 6.92 us
  waiting for transfers between devices: 243 us -> 119 us
  Pallas kernels: 0 us -> 118 us
  local copies, waits for them, and re-layouts: 47 us -> 10.1 us
  starting transfers between devices: 60.7 us -> 80.8 us
  between operations: 14.6 us -> 1.42 us
    pallas_call x0 -> x18, Pallas kernels: none -> 118 us  [the longest x8 62.8 us: advance(): pl.pallas_call(functools.partial(step_body, block=block, blocks=blocks, e...]
    psum x1 -> x0, waiting for transfers between devices: 95.2 us -> none  [body(): lax.psum((jnp.sum(moved, axis=1, keepdims=True), jnp.sum(moved * moved, a...]
    add x3 -> x12, other arithmetic: 88.6 us -> 2.86 us  [the longest x4 2.56 us: body(): sums.append((*x_first(keep + swap(send, masks[0]), masks, bits[1]), bits))]
    reduce_sum x1 -> x0, other arithmetic: 32.9 us -> none  [body(): jnp.sum(moved, axis=1, keepdims=True)]
    ppermute x24 -> x60, waiting for transfers between devices: 147 us -> 119 us  [the longest x20 50.9 us: swap(): lax.ppermute(value, 'px', [(i, i ^ mask) for i in range(lax.axis_size('px...]
    ppermute x24 -> x60, starting transfers between devices: 60.6 us -> 80.8 us  [the longest x24 28.4 us: pair_swap(): lax.ppermute(value, axis, [(i, (i - odd ^ 1) + odd) for i in range(odd, d...]
    unnamed x5 -> x86, local copies, waits for them, and re-layouts: 28.1 us -> 9.15 us
    slice x12 -> x1, local copies, waits for them, and re-layouts: 16 us -> 0.88 us  [body(): y_low = (send_up(u[rows - 1:], 'py'), 0)]
  transfers between devices with their start and end apart: 25 -> 60, of which waited for: 17 -> 26; matrix products, arithmetic and copies ran while one was open for 5% -> 2% of each run, Pallas kernels for 0% -> 33%
where the time goes in v1:
time: 341 us; the launch traced here: 337 us
  waiting for transfers between devices  119 us (35%)
  Pallas kernels  118 us (35%)
  starting transfers between devices  80.8 us (24%)
  local copies, waits for them, and re-layouts  10.1 us (3%)
  other arithmetic  6.92 us (2%)
    pallas_call x8, Pallas kernels, advance(): pl.pallas_call(functools.partial(step_body, block=block, blocks=blocks, e...  62.8 us
    ppermute x20, waiting for transfers between devices, swap(): lax.ppermute(value, 'px', [(i, i ^ mask) for i in range(lax.axis_size('px...  50.9 us
    ppermute x4, waiting for transfers between devices, z_exchange(): over = lax.ppermute(odd, ('px', 'pz'), back)  35.5 us
    ppermute x24, starting transfers between devices, pair_swap(): lax.ppermute(value, axis, [(i, (i - odd ^ 1) + odd) for i in range(odd, d...  28.4 us
    pallas_call x4, Pallas kernels, finish(): pl.pallas_call(functools.partial(final_body, block=block, per_part=per_pa...  28.4 us
    ppermute x4, starting transfers between devices, z_exchange(): odd = lax.ppermute(faces[1], ('px', 'pz'), direct + out)  24.9 us
    pallas_call x4, Pallas kernels, scale(): pl.pallas_call(functools.partial(scale_body, inverse=1.0 / line_length),...  19.5 us
    ppermute x8, waiting for transfers between devices, ring(): lax.ppermute(value, axis, [(i, (i + shift) % devices) for i in range(devi...  14.1 us
  transfers between devices with their start and end apart: 60, of which 26 were waited for; matrix products, arithmetic and copies ran while one was open for 2% of the time, Pallas kernels for 33%

profile of v1, /device:TPU:1, one launch (start us, length us, event | category | flops | bytes accessed | tf_op | source)
XLA Modules:
  0.0 336.9 jit_solution(6190694569985414231)
XLA Ops:
  0.6 3.8 %pick.3 = (f32[64,32,128]{2,1,0:T(8,128)}, f32[64,32,128]{2,1,0:T(8,128)}) custom-call(f32[128,4,32,128]{3,2,1,0:T(8,128)} %refs_3_.1, f32[128,4,32,128]{3,2,1,0:T(8,128)} %refs_3_.1), custom_call_target="tpu_custom_call" | custom-call | tf_op jit(solution)/shard_map/pick/pallas_call | solution.py:118
  4.4 2.0 collective-permute-start.7
  10.3 3.8 %pick.2 = (f32[64,32,128]{2,1,0:T(8,128)}, f32[64,32,128]{2,1,0:T(8,128)}) custom-call(f32[128,4,32,128]{3,2,1,0:T(8,128)} %refs_3_.1, f32[128,4,32,128]{3,2,1,0:T(8,128)} %refs_3_.1), custom_call_target="tpu_custom_call" | custom-call | tf_op jit(solution)/shard_map/pick/pallas_call | solution.py:118
  14.1 2.4 collective-permute-start.1
  17.3 2.8 broadcast_select_fusion
  20.0 8.3 %collective-permute-start.4 = (f32[512,128]{1,0:T(8,128)S(1)}, f32[512,128]{1,0:T(8,128)S(1)}, u32[]{:S(2)}, u32[]{:S(2)}) collective-permute-start(f32[512,128]{1,0:T(8,128)S(1)} %bitcast.21), channel_id=1, source_target_pairs={{5,6},{6,5},{9,10},{10,9},{13,14},{14,13},{17,18},{18,17},{21,22},... | collective-permute-start | bytes 786440 | tf_op jit(solution)/shard_map/ppermute | solution.py:51
  28.4 6.1 %collective-permute-done.4.refs_8_ = f32[512,128]{1,0:T(8,128)S(1)} collective-permute-done((f32[512,128]{1,0:T(8,128)S(1)}, f32[512,128]{1,0:T(8,128)S(1)}, u32[]{:S(2)}, u32[]{:S(2)}) %collective-permute-start.4) | collective-permute-done | bytes 262176 | tf_op jit(solution)/shard_map/ppermute | solution.py:51
  37.3 6.9 %collective-permute-done.5.refs_9_ = f32[512,128]{1,0:T(8,128)S(1)} collective-permute-done((f32[512,128]{1,0:T(8,128)S(1)}, f32[512,128]{1,0:T(8,128)S(1)}, u32[]{:S(2)}, u32[]{:S(2)}) %collective-permute-start.5) | collective-permute-done | bytes 262176 | tf_op jit(solution)/shard_map/ppermute | solution.py:52
  44.9 9.5 %advance.8 = (f32[128,4,32,128]{3,2,1,0:T(8,128)}, f32[512,128]{1,0:T(8,128)}, f32[512,128]{1,0:T(8,128)}, f32[64,32,128]{2,1,0:T(8,128)}, f32[64,32,128]{2,1,0:T(8,128)}, /*index=5*/f32[1,4,32,128]{3,2,1,0:T(8,128)}) custom-call(f32[128,4,32,128]{3,2,1,0:T(8,128)} %refs_3_.1, f32[128,4,32,128]{3,2,1,0:T(8,128)} %refs_3_.1, f32[128,4,32,128]{3,2,1,0:T(8,128)} %refs_3_.1, ...), custom_call_target="tpu_custom_call" | custom-call | tf_op jit(solution)/shard_map/advance/pallas_call | solution.py:202
  57.6 2.1 collective-permute-done.refs_4_
  61.1 10.2 %advance.9 = (f32[128,4,32,128]{3,2,1,0:T(8,128)}, f32[512,128]{1,0:T(8,128)}, f32[512,128]{1,0:T(8,128)}, f32[64,32,128]{2,1,0:T(8,128)}, f32[64,32,128]{2,1,0:T(8,128)}, /*index=5*/f32[1,4,32,128]{3,2,1,0:T(8,128)}) custom-call(f32[128,4,32,128]{3,2,1,0:T(8,128)} %refs_3_.1, ...), custom_call_target="tpu_custom_call", output_to_operand_aliasing={{0}: (12, {}), {1}: (13, {}), {2}: (14, {})} | custom-call | tf_op jit(solution)/shard_map/advance/pallas_call | solution.py:202
  75.3 3.2 collective-permute-done.15.refs_3_
  78.6 6.0 %collective-permute-start.13 = (f32[512,128]{1,0:T(8,128)}, f32[512,128]{1,0:T(8,128)S(1)}, u32[]{:S(2)}, u32[]{:S(2)}) collective-permute-start(f32[512,128]{1,0:T(8,128)} %get-tuple-element.76), channel_id=1, source_target_pairs={{5,6},{6,5},{9,10},{10,9},{13,14},{14,13},{17,18},{18,17},{21,22},... | collective-permute-start | bytes 786440 | tf_op jit(solution)/shard_map/ppermute | solution.py:51
  84.5 3.6 %collective-permute-done.13.refs_8_ = f32[512,128]{1,0:T(8,128)S(1)} collective-permute-done((f32[512,128]{1,0:T(8,128)}, f32[512,128]{1,0:T(8,128)S(1)}, u32[]{:S(2)}, u32[]{:S(2)}) %collective-permute-start.13) | collective-permute-done | bytes 262176 | tf_op jit(solution)/shard_map/ppermute | solution.py:51
  91.2 12.8 %collective-permute-done.14.refs_9_ = f32[512,128]{1,0:T(8,128)S(1)} collective-permute-done((f32[512,128]{1,0:T(8,128)S(1)}, f32[512,128]{1,0:T(8,128)S(1)}, u32[]{:S(2)}, u32[]{:S(2)}) %collective-permute-start.14) | collective-permute-done | bytes 262176 | tf_op jit(solution)/shard_map/ppermute | solution.py:52
  104.7 9.5 %advance.10 = (f32[128,4,32,128]{3,2,1,0:T(8,128)}, f32[512,128]{1,0:T(8,128)}, f32[512,128]{1,0:T(8,128)}, f32[64,32,128]{2,1,0:T(8,128)}, f32[64,32,128]{2,1,0:T(8,128)}, /*index=5*/f32[1,4,32,128]{3,2,1,0:T(8,128)}) custom-call(f32[128,4,32,128]{3,2,1,0:T(8,128)} %get-tuple-element.71.refs_0_.refs_1_.refs_2_.refs_4_.refs_3_, ...), custom_call_target="tpu_custom_call" | custom-call | tf_op jit(solution)/shard_map/advance/pallas_call | solution.py:202
  120.5 10.2 %advance.11 = (f32[128,4,32,128]{3,2,1,0:T(8,128)}, f32[512,128]{1,0:T(8,128)}, f32[512,128]{1,0:T(8,128)}, f32[64,32,128]{2,1,0:T(8,128)}, f32[64,32,128]{2,1,0:T(8,128)}, /*index=5*/f32[1,4,32,128]{3,2,1,0:T(8,128)}) custom-call(f32[128,4,32,128]{3,2,1,0:T(8,128)} %get-tuple-element.71.refs_0_.refs_1_, ...), custom_call_target="tpu_custom_call", output_to_operand_aliasing={{0}: (12, {}), {1}: (13, {}), {2}: (14, {})} | custom-call | tf_op jit(solution)/shard_map/advance/pallas_call | solution.py:202
  130.8 2.3 collective-permute-start.19
  133.9 4.5 %collective-permute-done.26.refs_3_ = f32[1,4,32,128]{3,2,1,0:T(8,128)S(1)} collective-permute-done((f32[1,4,32,128]{3,2,1,0:T(8,128)}, f32[1,4,32,128]{3,2,1,0:T(8,128)S(1)}, u32[]{:S(2)}, u32[]{:S(2)}) %collective-permute-start.26) | collective-permute-done | bytes 65568 | tf_op jit(solution)/shard_map/ppermute | solution.py:16
  138.4 5.6 %collective-permute-start.22 = (f32[512,128]{1,0:T(8,128)}, f32[512,128]{1,0:T(8,128)S(1)}, u32[]{:S(2)}, u32[]{:S(2)}) collective-permute-start(f32[512,128]{1,0:T(8,128)} %get-tuple-element.88), channel_id=1, source_target_pairs={{5,6},{6,5},{9,10},{10,9},{13,14},{14,13},{17,18},{18,17},{21,22},... | collective-permute-start | bytes 786440 | tf_op jit(solution)/shard_map/ppermute | solution.py:51
  144.0 3.6 %collective-permute-done.22.refs_8_ = f32[512,128]{1,0:T(8,128)S(1)} collective-permute-done((f32[512,128]{1,0:T(8,128)}, f32[512,128]{1,0:T(8,128)S(1)}, u32[]{:S(2)}, u32[]{:S(2)}) %collective-permute-start.22) | collective-permute-done | bytes 262176 | tf_op jit(solution)/shard_map/ppermute | solution.py:51
  150.7 13.4 %collective-permute-done.23.refs_9_ = f32[512,128]{1,0:T(8,128)S(1)} collective-permute-done((f32[512,128]{1,0:T(8,128)S(1)}, f32[512,128]{1,0:T(8,128)S(1)}, u32[]{:S(2)}, u32[]{:S(2)}) %collective-permute-start.23) | collective-permute-done | bytes 262176 | tf_op jit(solution)/shard_map/ppermute | solution.py:52
  164.8 5.5 %advance.12 = (f32[128,4,32,128]{3,2,1,0:T(8,128)}, f32[512,128]{1,0:T(8,128)}, f32[512,128]{1,0:T(8,128)}, f32[32,32,128]{2,1,0:T(8,128)}, f32[32,32,128]{2,1,0:T(8,128)}, /*index=5*/f32[1,4,32,128]{3,2,1,0:T(8,128)}) custom-call(f32[128,4,32,128]{3,2,1,0:T(8,128)} %get-tuple-element.83.refs_0_.refs_1_.refs_2_.refs_4_.refs_3_, ...), custom_call_target="tpu_custom_call" | custom-call | tf_op jit(solution)/shard_map/advance/pallas_call | solution.py:202
  172.4 6.0 %advance.13 = (f32[128,4,32,128]{3,2,1,0:T(8,128)}, f32[512,128]{1,0:T(8,128)}, f32[512,128]{1,0:T(8,128)}, f32[32,32,128]{2,1,0:T(8,128)}, f32[32,32,128]{2,1,0:T(8,128)}) custom-call(f32[128,4,32,128]{3,2,1,0:T(8,128)} %get-tuple-element.83.refs_0_.refs_1_.refs_2_.refs_4_.refs_3_, ...), custom_call_target="tpu_custom_call", output_to_operand_aliasing={{0}: (12, {}), {1}: (13, {}), {2}: (14, {})} | custom-call | tf_op jit(solution)/shard_map/advance/pallas_call | solution.py:202
  179.7 5.9 %advance.14 = (f32[128,4,32,128]{3,2,1,0:T(8,128)}, f32[512,128]{1,0:T(8,128)}, f32[512,128]{1,0:T(8,128)}, f32[32,32,128]{2,1,0:T(8,128)}, f32[32,32,128]{2,1,0:T(8,128)}) custom-call(f32[128,4,32,128]{3,2,1,0:T(8,128)} %get-tuple-element.83.refs_0_.refs_1_.refs_2_.refs_4_.refs_3_, ...), custom_call_target="tpu_custom_call", output_to_operand_aliasing={{0}: (12, {}), {1}: (13, {}), {2}: (14, {})} | custom-call | tf_op jit(solution)/shard_map/advance/pallas_call | solution.py:202
  186.3 5.9 %advance.15 = (f32[128,4,32,128]{3,2,1,0:T(8,128)}, f32[512,128]{1,0:T(8,128)}, f32[512,128]{1,0:T(8,128)}, f32[32,32,128]{2,1,0:T(8,128)}, f32[32,32,128]{2,1,0:T(8,128)}, /*index=5*/f32[1,4,32,128]{3,2,1,0:T(8,128)}) custom-call(f32[128,4,32,128]{3,2,1,0:T(8,128)} %get-tuple-element.83.refs_0_.refs_1_, ...), custom_call_target="tpu_custom_call", output_to_operand_aliasing={{0}: (12, {}), {1}: (13, {}), {2}: (14, {})} | custom-call | tf_op jit(solution)/shard_map/advance/pallas_call | solution.py:202
  192.2 5.0 %collective-permute-start.31 = (f32[512,128]{1,0:T(8,128)}, f32[512,128]{1,0:T(8,128)S(1)}, u32[]{:S(2)}, u32[]{:S(2)}) collective-permute-start(f32[512,128]{1,0:T(8,128)} %get-tuple-element.106), channel_id=1, source_target_pairs={{5,6},{6,5},{9,10},{10,9},{13,14},{14,13},{17,18},{18,17},{21,22},... | collective-permute-start | bytes 786440 | tf_op jit(solution)/shard_map/ppermute | solution.py:51
  199.3 2.5 collective-permute-done.37.refs_3_
  204.9 3.6 %collective-permute-start.33 = (f32[32,32,128]{2,1,0:T(8,128)}, f32[32,32,128]{2,1,0:T(8,128)}, u32[]{:S(2)}, u32[]{:S(2)}) collective-permute-start(f32[32,32,128]{2,1,0:T(8,128)} %get-tuple-element.107), channel_id=1, source_target_pairs={{0,4},{4,0},{8,12},{12,8},{16,20},{20,16},{24,28},{28,24},{1,5},{5... | collective-permute-start | bytes 1572872 | tf_op jit(solution)/shard_map/ppermute | solution.py:33
  210.3 2.1 collective-permute-start.28
  212.4 2.3 collective-permute-done.32.refs_9_
  216.8 7.1 %finish.4 = (f32[128,4,32,128]{3,2,1,0:T(8,128)}, f32[2,16,32,128]{3,2,1,0:T(8,128)}, f32[2,16,32,128]{3,2,1,0:T(8,128)}) custom-call(s32[2]{0:T(128)} %pad_add_fusion.1.bits, f32[128,4,32,128]{3,2,1,0:T(8,128)} %get-tuple-element.101.refs_0_.refs_1_.refs_2_.refs_4_.refs_3_, f32[128,4,32,128]{3,2,1,0:T(8,128)} %get-tuple-element.101.refs_0_.refs_1_.refs_2_.refs_4_.refs_3_, ...), custom_call_target="tpu_custom_call" | custom-call | tf_op jit(solution)/shard_map/finish/pallas_call | solution.py:275
  225.2 7.2 %finish.5 = (f32[128,4,32,128]{3,2,1,0:T(8,128)}, f32[2,16,32,128]{3,2,1,0:T(8,128)}, f32[2,16,32,128]{3,2,1,0:T(8,128)}) custom-call(s32[2]{0:T(128)} %pad_add_fusion.bits, f32[128,4,32,128]{3,2,1,0:T(8,128)} %get-tuple-element.101.refs_0_.refs_1_.refs_2_.refs_4_.refs_3_, ...), custom_call_target="tpu_custom_call", output_to_operand_aliasing={{0}: (13, {})} | custom-call | tf_op jit(solution)/shard_map/finish/pallas_call | solution.py:275
  233.5 3.6 %collective-permute-start.27 = (f32[1,4,32,128]{3,2,1,0:T(8,128)S(1)}, f32[1,4,32,128]{3,2,1,0:T(8,128)S(1)}, u32[]{:S(2)}, u32[]{:S(2)}) collective-permute-start(f32[1,4,32,128]{3,2,1,0:T(8,128)S(1)} %copy-done.40), channel_id=1, source_target_pairs={{0,96},{32,0},{64,32},{96,64},{1,97},{33,1},{65,33},{97,65},{2,98}... | collective-permute-start | bytes 196616 | tf_op jit(solution)/shard_map/ppermute | solution.py:16
  237.1 7.0 %finish.6 = (f32[128,4,32,128]{3,2,1,0:T(8,128)}, f32[2,16,32,128]{3,2,1,0:T(8,128)}, f32[2,16,32,128]{3,2,1,0:T(8,128)}) custom-call(s32[2]{0:T(128)} %pad_add_fusion.1.bits, f32[128,4,32,128]{3,2,1,0:T(8,128)} %get-tuple-element.101.refs_0_.refs_1_.refs_2_.refs_4_.refs_3_, ...), custom_call_target="tpu_custom_call", output_to_operand_aliasing={{0}: (13, {})} | custom-call | tf_op jit(solution)/shard_map/finish/pallas_call | solution.py:275
  246.0 7.0 %finish.7 = (f32[128,4,32,128]{3,2,1,0:T(8,128)}, f32[2,16,32,128]{3,2,1,0:T(8,128)}, f32[2,16,32,128]{3,2,1,0:T(8,128)}) custom-call(s32[2]{0:T(128)} %pad_add_fusion.bits, f32[128,4,32,128]{3,2,1,0:T(8,128)} %get-tuple-element.101.refs_0_.refs_1_.refs_2_.refs_4_.refs_3_, ...), custom_call_target="tpu_custom_call", output_to_operand_aliasing={{0}: (13, {})} | custom-call | tf_op jit(solution)/shard_map/finish/pallas_call | solution.py:275
  259.4 9.1 %collective-permute-done.40 = f32[2,16,32,128]{3,2,1,0:T(8,128)} collective-permute-done((f32[2,16,32,128]{3,2,1,0:T(8,128)}, f32[2,16,32,128]{3,2,1,0:T(8,128)}, u32[]{:S(2)}, u32[]{:S(2)}) %collective-permute-start.40) | collective-permute-done | bytes 524320 | tf_op jit(solution)/shard_map/ppermute | solution.py:28
  269.8 4.1 %collective-permute-done.56 = f32[2,8,32,128]{3,2,1,0:T(8,128)S(1)} collective-permute-done((f32[2,8,32,128]{3,2,1,0:T(8,128)S(1)}, f32[2,8,32,128]{3,2,1,0:T(8,128)S(1)}, u32[]{:S(2)}, u32[]{:S(2)}) %collective-permute-start.56) | collective-permute-done | bytes 262176 | tf_op jit(solution)/shard_map/ppermute | solution.py:28
  275.7 3.9 %collective-permute-done.46 = f32[2,8,32,128]{3,2,1,0:T(8,128)S(1)} collective-permute-done((f32[2,8,32,128]{3,2,1,0:T(8,128)S(1)}, f32[2,8,32,128]{3,2,1,0:T(8,128)S(1)}, u32[]{:S(2)}, u32[]{:S(2)}) %collective-permute-start.46) | collective-permute-done | bytes 262176 | tf_op jit(solution)/shard_map/ppermute | solution.py:28
  281.4 5.5 %collective-permute-done.52 = f32[2,8,32,128]{3,2,1,0:T(8,128)S(1)} collective-permute-done((f32[2,8,32,128]{3,2,1,0:T(8,128)S(1)}, f32[2,8,32,128]{3,2,1,0:T(8,128)S(1)}, u32[]{:S(2)}, u32[]{:S(2)}) %collective-permute-start.52) | collective-permute-done | bytes 262176 | tf_op jit(solution)/shard_map/ppermute | solution.py:28
  287.1 5.5 %collective-permute-done.47 = f32[2,8,32,128]{3,2,1,0:T(8,128)S(1)} collective-permute-done((f32[2,8,32,128]{3,2,1,0:T(8,128)S(1)}, f32[2,8,32,128]{3,2,1,0:T(8,128)S(1)}, u32[]{:S(2)}, u32[]{:S(2)}) %collective-permute-start.47) | collective-permute-done | bytes 262176 | tf_op jit(solution)/shard_map/ppermute | solution.py:28
  292.6 5.5 %collective-permute-done.42 = f32[2,8,32,128]{3,2,1,0:T(8,128)S(1)} collective-permute-done((f32[2,8,32,128]{3,2,1,0:T(8,128)S(1)}, f32[2,8,32,128]{3,2,1,0:T(8,128)S(1)}, u32[]{:S(2)}, u32[]{:S(2)}) %collective-permute-start.42) | collective-permute-done | bytes 262176 | tf_op jit(solution)/shard_map/ppermute | solution.py:28
  300.2 4.4 %collective-permute-done.43 = f32[2,8,32,128]{3,2,1,0:T(8,128)S(1)} collective-permute-done((f32[2,8,32,128]{3,2,1,0:T(8,128)S(1)}, f32[2,8,32,128]{3,2,1,0:T(8,128)S(1)}, u32[]{:S(2)}, u32[]{:S(2)}) %collective-permute-start.43) | collective-permute-done | bytes 262176 | tf_op jit(solution)/shard_map/ppermute | solution.py:28
  304.7 11.1 %collective-permute-done.59.other = f32[2,2,8,32,128]{4,3,2,1,0:T(8,128)S(1)} collective-permute-done((f32[2,2,8,32,128]{4,3,2,1,0:T(8,128)S(1)}, f32[2,2,8,32,128]{4,3,2,1,0:T(8,128)S(1)}, u32[]{:S(2)}, u32[]{:S(2)}) %collective-permute-start.59) | collective-permute-done | bytes 524320 | tf_op jit(solution)/shard_map/ppermute | solution.py:28
  316.6 4.9 %scale.4.refs_0_ = f32[128,4,32,128]{3,2,1,0:T(8,128)} custom-call(s32[2]{0:T(128)} %pad_add_fusion.1.bits, f32[128,4,32,128]{3,2,1,0:T(8,128)} %get-tuple-element.63.u, f32[2,2,8,32,128]{4,3,2,1,0:T(8,128)} %copy-done.8, f32[2,2,8,32,128]{4,3,2,1,0:T(8,128)} %copy-done.29), custom_call_target="tpu_custom_call" | custom-call | tf_op jit(solution)/shard_map/scale/pallas_call | solution.py:334
  322.3 4.9 %scale.5.refs_0_ = f32[128,4,32,128]{3,2,1,0:T(8,128)} custom-call(s32[2]{0:T(128)} %pad_add_fusion.bits, f32[128,4,32,128]{3,2,1,0:T(8,128)} %get-tuple-element.63.u, f32[2,2,8,32,128]{4,3,2,1,0:T(8,128)} %copy-done.9, f32[2,2,8,32,128]{4,3,2,1,0:T(8,128)} %copy-done.30, f32[128,4,32,128]{3,2,1,0:T(8,128)} %scale.4.refs_0_), custom_call_target="tpu_custom_call", output_to_operand_aliasing={{}: (4, {})} | custom-call | tf_op jit(solution)/shard_map/scale/pallas_call | solution.py:334
  327.2 4.9 %scale.6.refs_0_ = f32[128,4,32,128]{3,2,1,0:T(8,128)} custom-call(s32[2]{0:T(128)} %pad_add_fusion.1.bits, f32[128,4,32,128]{3,2,1,0:T(8,128)} %get-tuple-element.63.u, f32[2,2,8,32,128]{4,3,2,1,0:T(8,128)} %copy-done.10, f32[2,2,8,32,128]{4,3,2,1,0:T(8,128)} %collective-permute-done.49.other, ...), custom_call_target="tpu_custom_call", output_to_operand_aliasing={{}: (4, {})} | custom-call | tf_op jit(solution)/shard_map/scale/pallas_call | solution.py:334
  332.1 4.9 %scale.7 = f32[128,4,32,128]{3,2,1,0:T(8,128)} custom-call(s32[2]{0:T(128)} %pad_add_fusion.bits, f32[128,4,32,128]{3,2,1,0:T(8,128)} %get-tuple-element.63.u, f32[2,2,8,32,128]{4,3,2,1,0:T(8,128)} %copy-done.11, f32[2,2,8,32,128]{4,3,2,1,0:T(8,128)} %collective-permute-done.44.other, f32[128,4,32,128]{3,2,1,0:T(8,128)} %scale.6.refs_0_), custom_call_target="tpu_custom_call", output_to_operand_aliasing={{}: (4, {})} | custom-call | tf_op jit(solution)/shard_map/scale/pallas_call | solution.py:334
  (200 shorter events, 63.5 us)
Async XLA Ops:
  4.4 39.8 %collective-permute-start.7 = (f32[64,32,128]{2,1,0:T(8,128)}, f32[64,32,128]{2,1,0:T(8,128)}, u32[]{:S(2)}, u32[]{:S(2)}) collective-permute-start(f32[64,32,128]{2,1,0:T(8,128)} %get-tuple-element.66), channel_id=1, source_target_pairs={{0,4},{4,0},{8,12},{12,8},{16,20},{20,16},{24,28},{28,24},{1,5},{5... | collective-permute-start | bytes 3145736 | tf_op jit(solution)/shard_map/ppermute | solution.py:33
  6.5 37.8 %collective-permute-start.8 = (f32[64,32,128]{2,1,0:T(8,128)}, f32[64,32,128]{2,1,0:T(8,128)}, u32[]{:S(2)}, u32[]{:S(2)}) collective-permute-start(f32[64,32,128]{2,1,0:T(8,128)} %get-tuple-element.67), channel_id=1, source_target_pairs={{4,8},{8,4},{12,16},{16,12},{20,24},{24,20},{5,9},{9,5},{13,17},{1... | collective-permute-start | bytes 3145736 | tf_op jit(solution)/shard_map/ppermute | solution.py:33
  9.0 11.1 %collective-permute-start.6 = (f32[1,4,32,128]{3,2,1,0:T(8,128)S(1)}, f32[1,4,32,128]{3,2,1,0:T(8,128)S(1)}, u32[]{:S(2)}, u32[]{:S(2)}) collective-permute-start(f32[1,4,32,128]{3,2,1,0:T(8,128)S(1)} %get-tuple-element.126), channel_id=1, source_target_pairs={{0,32},{32,64},{64,96},{96,0},{1,33},{33,65},{65,97},{97,1},{2,34}... | collective-permute-start | bytes 196616 | tf_op jit(solution)/shard_map/ppermute | solution.py:16
  14.1 45.6 %collective-permute-start.1 = (f32[64,32,128]{2,1,0:T(8,128)}, f32[64,32,128]{2,1,0:T(8,128)S(1)}, u32[]{:S(2)}, u32[]{:S(2)}) collective-permute-start(f32[64,32,128]{2,1,0:T(8,128)} %get-tuple-element.64), channel_id=1, source_target_pairs={{0,4},{4,0},{8,12},{12,8},{16,20},{20,16},{24,28},{28,24},{1,5},{5... | collective-permute-start | bytes 3145736 | tf_op jit(solution)/shard_map/ppermute | solution.py:33
  16.5 43.2 %collective-permute-start.2 = (f32[64,32,128]{2,1,0:T(8,128)}, f32[64,32,128]{2,1,0:T(8,128)S(1)}, u32[]{:S(2)}, u32[]{:S(2)}) collective-permute-start(f32[64,32,128]{2,1,0:T(8,128)} %get-tuple-element.65), channel_id=1, source_target_pairs={{4,8},{8,4},{12,16},{16,12},{20,24},{24,20},{5,9},{9,5},{13,17},{1... | collective-permute-start | bytes 3145736 | tf_op jit(solution)/shard_map/ppermute | solution.py:33
  20.0 14.4 %collective-permute-start.4 = (f32[512,128]{1,0:T(8,128)S(1)}, f32[512,128]{1,0:T(8,128)S(1)}, u32[]{:S(2)}, u32[]{:S(2)}) collective-permute-start(f32[512,128]{1,0:T(8,128)S(1)} %bitcast.21), channel_id=1, source_target_pairs={{5,6},{6,5},{9,10},{10,9},{13,14},{14,13},{17,18},{18,17},{21,22},... | collective-permute-start | bytes 786440 | tf_op jit(solution)/shard_map/ppermute | solution.py:51
  36.0 8.2 %collective-permute-start.5 = (f32[512,128]{1,0:T(8,128)S(1)}, f32[512,128]{1,0:T(8,128)S(1)}, u32[]{:S(2)}, u32[]{:S(2)}) collective-permute-start(f32[512,128]{1,0:T(8,128)S(1)} %collective-permute-done.4.refs_8_), channel_id=1, source_target_pairs={{19,2},{16,1},{15,30},{12,29},{51,34},{48,33},{47,62},{44,61},{83,... | collective-permute-start | bytes 786440 | tf_op jit(solution)/shard_map/ppermute | solution.py:52
  54.4 49.5 %collective-permute-start.16 = (f32[64,32,128]{2,1,0:T(8,128)}, f32[64,32,128]{2,1,0:T(8,128)}, u32[]{:S(2)}, u32[]{:S(2)}) collective-permute-start(f32[64,32,128]{2,1,0:T(8,128)} %get-tuple-element.78), channel_id=1, source_target_pairs={{0,4},{4,0},{8,12},{12,8},{16,20},{20,16},{24,28},{28,24},{1,5},{5... | collective-permute-start | bytes 3145736 | tf_op jit(solution)/shard_map/ppermute | solution.py:33
  54.5 49.5 %collective-permute-start.17 = (f32[64,32,128]{2,1,0:T(8,128)}, f32[64,32,128]{2,1,0:T(8,128)}, u32[]{:S(2)}, u32[]{:S(2)}) collective-permute-start(f32[64,32,128]{2,1,0:T(8,128)} %get-tuple-element.79), channel_id=1, source_target_pairs={{4,8},{8,4},{12,16},{16,12},{20,24},{24,20},{5,9},{9,5},{13,17},{1... | collective-permute-start | bytes 3145736 | tf_op jit(solution)/shard_map/ppermute | solution.py:33
  71.3 47.8 %collective-permute-start.10 = (f32[64,32,128]{2,1,0:T(8,128)}, f32[64,32,128]{2,1,0:T(8,128)S(1)}, u32[]{:S(2)}, u32[]{:S(2)}) collective-permute-start(f32[64,32,128]{2,1,0:T(8,128)} %get-tuple-element.73), channel_id=1, source_target_pairs={{0,4},{4,0},{8,12},{12,8},{16,20},{20,16},{24,28},{28,24},{1,5},{5... | collective-permute-start | bytes 3145736 | tf_op jit(solution)/shard_map/ppermute | solution.py:33
  73.2 45.9 %collective-permute-start.11 = (f32[64,32,128]{2,1,0:T(8,128)}, f32[64,32,128]{2,1,0:T(8,128)S(1)}, u32[]{:S(2)}, u32[]{:S(2)}) collective-permute-start(f32[64,32,128]{2,1,0:T(8,128)} %get-tuple-element.74), channel_id=1, source_target_pairs={{4,8},{8,4},{12,16},{16,12},{20,24},{24,20},{5,9},{9,5},{13,17},{1... | collective-permute-start | bytes 3145736 | tf_op jit(solution)/shard_map/ppermute | solution.py:33
  78.6 9.6 %collective-permute-start.13 = (f32[512,128]{1,0:T(8,128)}, f32[512,128]{1,0:T(8,128)S(1)}, u32[]{:S(2)}, u32[]{:S(2)}) collective-permute-start(f32[512,128]{1,0:T(8,128)} %get-tuple-element.76), channel_id=1, source_target_pairs={{5,6},{6,5},{9,10},{10,9},{13,14},{14,13},{17,18},{18,17},{21,22},... | collective-permute-start | bytes 786440 | tf_op jit(solution)/shard_map/ppermute | solution.py:51
  89.9 14.1 %collective-permute-start.14 = (f32[512,128]{1,0:T(8,128)S(1)}, f32[512,128]{1,0:T(8,128)S(1)}, u32[]{:S(2)}, u32[]{:S(2)}) collective-permute-start(f32[512,128]{1,0:T(8,128)S(1)} %collective-permute-done.13.refs_8_), channel_id=1, source_target_pairs={{19,2},{16,1},{15,30},{12,29},{51,34},{48,33},{47,62},{44,61},{83,... | collective-permute-start | bytes 786440 | tf_op jit(solution)/shard_map/ppermute | solution.py:52
  114.3 49.8 %collective-permute-start.24 = (f32[64,32,128]{2,1,0:T(8,128)}, f32[64,32,128]{2,1,0:T(8,128)}, u32[]{:S(2)}, u32[]{:S(2)}) collective-permute-start(f32[64,32,128]{2,1,0:T(8,128)} %get-tuple-element.89), channel_id=1, source_target_pairs={{0,4},{4,0},{8,12},{12,8},{16,20},{20,16},{24,28},{28,24},{1,5},{5... | collective-permute-start | bytes 3145736 | tf_op jit(solution)/shard_map/ppermute | solution.py:33
  114.3 49.7 %collective-permute-start.25 = (f32[64,32,128]{2,1,0:T(8,128)}, f32[64,32,128]{2,1,0:T(8,128)}, u32[]{:S(2)}, u32[]{:S(2)}) collective-permute-start(f32[64,32,128]{2,1,0:T(8,128)} %get-tuple-element.90), channel_id=1, source_target_pairs={{4,8},{8,4},{12,16},{16,12},{20,24},{24,20},{5,9},{9,5},{13,17},{1... | collective-permute-start | bytes 3145736 | tf_op jit(solution)/shard_map/ppermute | solution.py:33
  130.8 47.6 %collective-permute-start.19 = (f32[64,32,128]{2,1,0:T(8,128)}, f32[64,32,128]{2,1,0:T(8,128)S(1)}, u32[]{:S(2)}, u32[]{:S(2)}) collective-permute-start(f32[64,32,128]{2,1,0:T(8,128)} %get-tuple-element.85), channel_id=1, source_target_pairs={{0,4},{4,0},{8,12},{12,8},{16,20},{20,16},{24,28},{28,24},{1,5},{5... | collective-permute-start | bytes 3145736 | tf_op jit(solution)/shard_map/ppermute | solution.py:33
  133.0 45.4 %collective-permute-start.20 = (f32[64,32,128]{2,1,0:T(8,128)}, f32[64,32,128]{2,1,0:T(8,128)S(1)}, u32[]{:S(2)}, u32[]{:S(2)}) collective-permute-start(f32[64,32,128]{2,1,0:T(8,128)} %get-tuple-element.86), channel_id=1, source_target_pairs={{4,8},{8,4},{12,16},{16,12},{20,24},{24,20},{5,9},{9,5},{13,17},{1... | collective-permute-start | bytes 3145736 | tf_op jit(solution)/shard_map/ppermute | solution.py:33
  138.4 9.2 %collective-permute-start.22 = (f32[512,128]{1,0:T(8,128)}, f32[512,128]{1,0:T(8,128)S(1)}, u32[]{:S(2)}, u32[]{:S(2)}) collective-permute-start(f32[512,128]{1,0:T(8,128)} %get-tuple-element.88), channel_id=1, source_target_pairs={{5,6},{6,5},{9,10},{10,9},{13,14},{14,13},{17,18},{18,17},{21,22},... | collective-permute-start | bytes 786440 | tf_op jit(solution)/shard_map/ppermute | solution.py:51
  149.4 14.7 %collective-permute-start.23 = (f32[512,128]{1,0:T(8,128)S(1)}, f32[512,128]{1,0:T(8,128)S(1)}, u32[]{:S(2)}, u32[]{:S(2)}) collective-permute-start(f32[512,128]{1,0:T(8,128)S(1)} %collective-permute-done.22.refs_8_), channel_id=1, source_target_pairs={{19,2},{16,1},{15,30},{12,29},{51,34},{48,33},{47,62},{44,61},{83,... | collective-permute-start | bytes 786440 | tf_op jit(solution)/shard_map/ppermute | solution.py:52
  170.2 34.6 %collective-permute-start.38 = (f32[32,32,128]{2,1,0:T(8,128)}, f32[32,32,128]{2,1,0:T(8,128)S(1)}, u32[]{:S(2)}, u32[]{:S(2)}) collective-permute-start(f32[32,32,128]{2,1,0:T(8,128)} %get-tuple-element.112), channel_id=1, source_target_pairs={{0,4},{4,0},{8,12},{12,8},{16,20},{20,16},{24,28},{28,24},{1,5},{5... | collective-permute-start | bytes 1572872 | tf_op jit(solution)/shard_map/ppermute | solution.py:33
  170.3 38.1 %collective-permute-start.39 = (f32[32,32,128]{2,1,0:T(8,128)}, f32[32,32,128]{2,1,0:T(8,128)S(1)}, u32[]{:S(2)}, u32[]{:S(2)}) collective-permute-start(f32[32,32,128]{2,1,0:T(8,128)} %get-tuple-element.113), channel_id=1, source_target_pairs={{4,8},{8,4},{12,16},{16,12},{20,24},{24,20},{5,9},{9,5},{13,17},{1... | collective-permute-start | bytes 1572872 | tf_op jit(solution)/shard_map/ppermute | solution.py:33
  171.0 14.6 %collective-permute-start.18 = (f32[1,4,32,128]{3,2,1,0:T(8,128)S(1)}, f32[1,4,32,128]{3,2,1,0:T(8,128)S(1)}, u32[]{:S(2)}, u32[]{:S(2)}) collective-permute-start(f32[1,4,32,128]{3,2,1,0:T(8,128)S(1)} %copy-done.41), channel_id=1, source_target_pairs={{0,96},{32,0},{64,32},{96,64},{1,97},{33,1},{65,33},{97,65},{2,98}... | collective-permute-start | bytes 196616 | tf_op jit(solution)/shard_map/ppermute | solution.py:16
  192.2 9.6 %collective-permute-start.31 = (f32[512,128]{1,0:T(8,128)}, f32[512,128]{1,0:T(8,128)S(1)}, u32[]{:S(2)}, u32[]{:S(2)}) collective-permute-start(f32[512,128]{1,0:T(8,128)} %get-tuple-element.106), channel_id=1, source_target_pairs={{5,6},{6,5},{9,10},{10,9},{13,14},{14,13},{17,18},{18,17},{21,22},... | collective-permute-start | bytes 786440 | tf_op jit(solution)/shard_map/ppermute | solution.py:51
  197.7 12.6 %collective-permute-start.35 = (f32[32,32,128]{2,1,0:T(8,128)S(1)}, f32[32,32,128]{2,1,0:T(8,128)S(1)}, u32[]{:S(2)}, u32[]{:S(2)}) collective-permute-start(f32[32,32,128]{2,1,0:T(8,128)S(1)} %copy-done.39), channel_id=1, source_target_pairs={{0,4},{4,0},{8,12},{12,8},{16,20},{20,16},{24,28},{28,24},{1,5},{5... | collective-permute-start | bytes 1572872 | tf_op jit(solution)/shard_map/ppermute | solution.py:33
  201.8 22.1 %collective-permute-start.36 = (f32[32,32,128]{2,1,0:T(8,128)}, f32[32,32,128]{2,1,0:T(8,128)}, u32[]{:S(2)}, u32[]{:S(2)}) collective-permute-start(f32[32,32,128]{2,1,0:T(8,128)} %get-tuple-element.110), channel_id=1, source_target_pairs={{4,8},{8,4},{12,16},{16,12},{20,24},{24,20},{5,9},{9,5},{13,17},{1... | collective-permute-start | bytes 1572872 | tf_op jit(solution)/shard_map/ppermute | solution.py:33
  203.6 11.2 %collective-permute-start.32 = (f32[512,128]{1,0:T(8,128)S(1)}, f32[512,128]{1,0:T(8,128)S(1)}, u32[]{:S(2)}, u32[]{:S(2)}) collective-permute-start(f32[512,128]{1,0:T(8,128)S(1)} %collective-permute-done.31.refs_8_), channel_id=1, source_target_pairs={{19,2},{16,1},{15,30},{12,29},{51,34},{48,33},{47,62},{44,61},{83,... | collective-permute-start | bytes 786440 | tf_op jit(solution)/shard_map/ppermute | solution.py:52
  204.9 27.5 %collective-permute-start.33 = (f32[32,32,128]{2,1,0:T(8,128)}, f32[32,32,128]{2,1,0:T(8,128)}, u32[]{:S(2)}, u32[]{:S(2)}) collective-permute-start(f32[32,32,128]{2,1,0:T(8,128)} %get-tuple-element.107), channel_id=1, source_target_pairs={{0,4},{4,0},{8,12},{12,8},{16,20},{20,16},{24,28},{28,24},{1,5},{5... | collective-permute-start | bytes 1572872 | tf_op jit(solution)/shard_map/ppermute | solution.py:33
  208.4 25.1 %collective-permute-start.34 = (f32[32,32,128]{2,1,0:T(8,128)}, f32[32,32,128]{2,1,0:T(8,128)}, u32[]{:S(2)}, u32[]{:S(2)}) collective-permute-start(f32[32,32,128]{2,1,0:T(8,128)} %get-tuple-element.108), channel_id=1, source_target_pairs={{4,8},{8,4},{12,16},{16,12},{20,24},{24,20},{5,9},{9,5},{13,17},{1... | collective-permute-start | bytes 1572872 | tf_op jit(solution)/shard_map/ppermute | solution.py:33
  210.3 34.9 %collective-permute-start.28 = (f32[32,32,128]{2,1,0:T(8,128)}, f32[32,32,128]{2,1,0:T(8,128)S(1)}, u32[]{:S(2)}, u32[]{:S(2)}) collective-permute-start(f32[32,32,128]{2,1,0:T(8,128)} %get-tuple-element.103), channel_id=1, source_target_pairs={{0,4},{4,0},{8,12},{12,8},{16,20},{20,16},{24,28},{28,24},{1,5},{5... | collective-permute-start | bytes 1572872 | tf_op jit(solution)/shard_map/ppermute | solution.py:33
  214.7 30.5 %collective-permute-start.29 = (f32[32,32,128]{2,1,0:T(8,128)}, f32[32,32,128]{2,1,0:T(8,128)}, u32[]{:S(2)}, u32[]{:S(2)}) collective-permute-start(f32[32,32,128]{2,1,0:T(8,128)} %get-tuple-element.104), channel_id=1, source_target_pairs={{4,8},{8,4},{12,16},{16,12},{20,24},{24,20},{5,9},{9,5},{13,17},{1... | collective-permute-start | bytes 1572872 | tf_op jit(solution)/shard_map/ppermute | solution.py:33
  223.9 30.1 %collective-permute-start.55 = (f32[2,16,32,128]{3,2,1,0:T(8,128)}, f32[2,16,32,128]{3,2,1,0:T(8,128)S(1)}, u32[]{:S(2)}, u32[]{:S(2)}) collective-permute-start(f32[2,16,32,128]{3,2,1,0:T(8,128)} %get-tuple-element.125), channel_id=1, source_target_pairs={{0,4},{4,0},{8,12},{12,8},{16,20},{20,16},{24,28},{28,24},{1,5},{5... | collective-permute-start | bytes 1572872 | tf_op jit(solution)/shard_map/ppermute | solution.py:28
  232.4 23.6 %collective-permute-start.50 = (f32[2,16,32,128]{3,2,1,0:T(8,128)}, f32[2,16,32,128]{3,2,1,0:T(8,128)S(1)}, u32[]{:S(2)}, u32[]{:S(2)}) collective-permute-start(f32[2,16,32,128]{3,2,1,0:T(8,128)} %get-tuple-element.123), channel_id=1, source_target_pairs={{0,12},{4,8},{8,4},{12,0},{16,28},{20,24},{24,20},{28,16},{1,13},{... | collective-permute-start | bytes 1572872 | tf_op jit(solution)/shard_map/ppermute | solution.py:28
  233.5 10.7 %collective-permute-start.27 = (f32[1,4,32,128]{3,2,1,0:T(8,128)S(1)}, f32[1,4,32,128]{3,2,1,0:T(8,128)S(1)}, u32[]{:S(2)}, u32[]{:S(2)}) collective-permute-start(f32[1,4,32,128]{3,2,1,0:T(8,128)S(1)} %copy-done.40), channel_id=1, source_target_pairs={{0,96},{32,0},{64,32},{96,64},{1,97},{33,1},{65,33},{97,65},{2,98}... | collective-permute-start | bytes 196616 | tf_op jit(solution)/shard_map/ppermute | solution.py:16
  244.2 13.9 %collective-permute-start.45 = (f32[2,16,32,128]{3,2,1,0:T(8,128)}, f32[2,16,32,128]{3,2,1,0:T(8,128)}, u32[]{:S(2)}, u32[]{:S(2)}) collective-permute-start(f32[2,16,32,128]{3,2,1,0:T(8,128)} %get-tuple-element.121), channel_id=1, source_target_pairs={{0,4},{4,0},{8,12},{12,8},{16,20},{20,16},{24,28},{28,24},{1,5},{5... | collective-permute-start | bytes 1572872 | tf_op jit(solution)/shard_map/ppermute | solution.py:28
  253.0 15.4 %collective-permute-start.40 = (f32[2,16,32,128]{3,2,1,0:T(8,128)}, f32[2,16,32,128]{3,2,1,0:T(8,128)}, u32[]{:S(2)}, u32[]{:S(2)}) collective-permute-start(f32[2,16,32,128]{3,2,1,0:T(8,128)} %get-tuple-element.119), channel_id=1, source_target_pairs={{0,12},{4,8},{8,4},{12,0},{16,28},{20,24},{24,20},{28,16},{1,13},{... | collective-permute-start | bytes 1572872 | tf_op jit(solution)/shard_map/ppermute | solution.py:28
  254.2 19.8 %collective-permute-start.56 = (f32[2,8,32,128]{3,2,1,0:T(8,128)S(1)}, f32[2,8,32,128]{3,2,1,0:T(8,128)S(1)}, u32[]{:S(2)}, u32[]{:S(2)}) collective-permute-start(f32[2,8,32,128]{3,2,1,0:T(8,128)S(1)} %constant_dynamic-slice_fusion), channel_id=1, source_target_pairs={{0,12},{4,8},{8,4},{12,0},{16,28},{20,24},{24,20},{28,16},{1,13},{... | collective-permute-start | bytes 786440 | tf_op jit(solution)/shard_map/ppermute | solution.py:28
  256.1 18.0 %collective-permute-start.51 = (f32[2,8,32,128]{3,2,1,0:T(8,128)S(1)}, f32[2,8,32,128]{3,2,1,0:T(8,128)S(1)}, u32[]{:S(2)}, u32[]{:S(2)}) collective-permute-start(f32[2,8,32,128]{3,2,1,0:T(8,128)S(1)} %constant_dynamic-slice_fusion.1), channel_id=1, source_target_pairs={{0,4},{4,0},{8,12},{12,8},{16,20},{20,16},{24,28},{28,24},{1,5},{5... | collective-permute-start | bytes 786440 | tf_op jit(solution)/shard_map/ppermute | solution.py:28
  259.3 20.3 %collective-permute-start.46 = (f32[2,8,32,128]{3,2,1,0:T(8,128)S(1)}, f32[2,8,32,128]{3,2,1,0:T(8,128)S(1)}, u32[]{:S(2)}, u32[]{:S(2)}) collective-permute-start(f32[2,8,32,128]{3,2,1,0:T(8,128)S(1)} %constant_dynamic-slice_fusion.2), channel_id=1, source_target_pairs={{0,12},{4,8},{8,4},{12,0},{16,28},{20,24},{24,20},{28,16},{1,13},{... | collective-permute-start | bytes 786440 | tf_op jit(solution)/shard_map/ppermute | solution.py:28
  269.8 9.9 %collective-permute-start.41 = (f32[2,8,32,128]{3,2,1,0:T(8,128)S(1)}, f32[2,8,32,128]{3,2,1,0:T(8,128)S(1)}, u32[]{:S(2)}, u32[]{:S(2)}) collective-permute-start(f32[2,8,32,128]{3,2,1,0:T(8,128)S(1)} %constant_dynamic-slice_fusion.3), channel_id=1, source_target_pairs={{0,4},{4,0},{8,12},{12,8},{16,20},{20,16},{24,28},{28,24},{1,5},{5... | collective-permute-start | bytes 786440 | tf_op jit(solution)/shard_map/ppermute | solution.py:28
  274.1 12.7 %collective-permute-start.52 = (f32[2,8,32,128]{3,2,1,0:T(8,128)S(1)}, f32[2,8,32,128]{3,2,1,0:T(8,128)S(1)}, u32[]{:S(2)}, u32[]{:S(2)}) collective-permute-start(f32[2,8,32,128]{3,2,1,0:T(8,128)S(1)} %dynamic-slice_add_fusion.1), channel_id=1, source_target_pairs={{0,16},{4,20},{8,24},{12,28},{16,0},{20,4},{24,8},{28,12},{1,17},{... | collective-permute-start | bytes 786440 | tf_op jit(solution)/shard_map/ppermute | solution.py:28
  279.6 12.9 %collective-permute-start.47 = (f32[2,8,32,128]{3,2,1,0:T(8,128)S(1)}, f32[2,8,32,128]{3,2,1,0:T(8,128)S(1)}, u32[]{:S(2)}, u32[]{:S(2)}) collective-permute-start(f32[2,8,32,128]{3,2,1,0:T(8,128)S(1)} %dynamic-slice_add_fusion.2), channel_id=1, source_target_pairs={{0,16},{4,20},{8,24},{12,28},{16,0},{20,4},{24,8},{28,12},{1,17},{... | collective-permute-start | bytes 786440 | tf_op jit(solution)/shard_map/ppermute | solution.py:28
  279.8 18.4 %collective-permute-start.42 = (f32[2,8,32,128]{3,2,1,0:T(8,128)S(1)}, f32[2,8,32,128]{3,2,1,0:T(8,128)S(1)}, u32[]{:S(2)}, u32[]{:S(2)}) collective-permute-start(f32[2,8,32,128]{3,2,1,0:T(8,128)S(1)} %dynamic-slice_add_fusion.3), channel_id=1, source_target_pairs={{0,16},{4,20},{8,24},{12,28},{16,0},{20,4},{24,8},{28,12},{1,17},{... | collective-permute-start | bytes 786440 | tf_op jit(solution)/shard_map/ppermute | solution.py:28
  281.3 17.0 %collective-permute-start.58 = (f32[2,8,32,128]{3,2,1,0:T(8,128)S(1)}, f32[2,8,32,128]{3,2,1,0:T(8,128)S(1)}, u32[]{:S(2)}, u32[]{:S(2)}) collective-permute-start(f32[2,8,32,128]{3,2,1,0:T(8,128)S(1)} %add.72), channel_id=1, source_target_pairs={{0,12},{4,8},{8,4},{12,0},{16,28},{20,24},{24,20},{28,16},{1,13},{... | collective-permute-start | bytes 786440 | tf_op jit(solution)/shard_map/ppermute | solution.py:28
  286.9 12.9 %collective-permute-start.53 = (f32[2,8,32,128]{3,2,1,0:T(8,128)S(1)}, f32[2,8,32,128]{3,2,1,0:T(8,128)S(1)}, u32[]{:S(2)}, u32[]{:S(2)}) collective-permute-start(f32[2,8,32,128]{3,2,1,0:T(8,128)S(1)} %add.69), channel_id=1, source_target_pairs={{0,4},{4,0},{8,12},{12,8},{16,20},{20,16},{24,28},{28,24},{1,5},{5... | collective-permute-start | bytes 786440 | tf_op jit(solution)/shard_map/ppermute | solution.py:28
  298.3 17.5 %collective-permute-start.59 = (f32[2,2,8,32,128]{4,3,2,1,0:T(8,128)S(1)}, f32[2,2,8,32,128]{4,3,2,1,0:T(8,128)S(1)}, u32[]{:S(2)}, u32[]{:S(2)}) collective-permute-start(f32[2,2,8,32,128]{4,3,2,1,0:T(8,128)S(1)} %pad_maximum_fusion.3.own), channel_id=1, source_target_pairs={{0,4},{4,0},{8,12},{12,8},{16,20},{20,16},{24,28},{28,24},{1,5},{5... | collective-permute-start | bytes 1572872 | tf_op jit(solution)/shard_map/ppermute | solution.py:28
  299.9 21.6 %collective-permute-start.54 = (f32[2,2,8,32,128]{4,3,2,1,0:T(8,128)S(1)}, f32[2,2,8,32,128]{4,3,2,1,0:T(8,128)S(1)}, u32[]{:S(2)}, u32[]{:S(2)}) collective-permute-start(f32[2,2,8,32,128]{4,3,2,1,0:T(8,128)S(1)} %pad_maximum_fusion.2.own), channel_id=1, source_target_pairs={{0,12},{4,8},{8,4},{12,0},{16,28},{20,24},{24,20},{28,16},{1,13},{... | collective-permute-start | bytes 1572872 | tf_op jit(solution)/shard_map/ppermute | solution.py:28
  300.1 27.1 %collective-permute-start.49 = (f32[2,2,8,32,128]{4,3,2,1,0:T(8,128)S(1)}, f32[2,2,8,32,128]{4,3,2,1,0:T(8,128)}, u32[]{:S(2)}, u32[]{:S(2)}) collective-permute-start(f32[2,2,8,32,128]{4,3,2,1,0:T(8,128)S(1)} %pad_maximum_fusion.1.own), channel_id=1, source_target_pairs={{0,4},{4,0},{8,12},{12,8},{16,20},{20,16},{24,28},{28,24},{1,5},{5... | collective-permute-start | bytes 1572872 | tf_op jit(solution)/shard_map/ppermute | solution.py:28
  304.6 27.4 %collective-permute-start.44 = (f32[2,2,8,32,128]{4,3,2,1,0:T(8,128)S(1)}, f32[2,2,8,32,128]{4,3,2,1,0:T(8,128)}, u32[]{:S(2)}, u32[]{:S(2)}) collective-permute-start(f32[2,2,8,32,128]{4,3,2,1,0:T(8,128)S(1)} %pad_maximum_fusion.own), channel_id=1, source_target_pairs={{0,12},{4,8},{8,4},{12,0},{16,28},{20,24},{24,20},{28,16},{1,13},{... | collective-permute-start | bytes 1572872 | tf_op jit(solution)/shard_map/ppermute | solution.py:28
  (55 other events, 441.7 us)

commit v2 on v1

v2 whole, which is shorter than its diff:
```python
import functools

import jax
import jax.numpy as jnp
from jax import lax
from jax.experimental import pallas as pl
from jax.experimental.pallas import tpu as pltpu
from jax.sharding import PartitionSpec as P


STEPS = 4
GRANT = 4 * 2**20
ROUTES = ("over_near", "near", "far", "over_near")
SCALES = ((0, "both"), (2, "both"), (1, "both"), (3, "own"), (3, "other"))


def ring(value, axis, shift):
    devices = lax.axis_size(axis)
    return lax.ppermute(value, axis, [(i, (i + shift) % devices) for i in range(devices)])


def send_up(value, axis):
    return ring(value, axis, 1)


def send_down(value, axis):
    return ring(value, axis, -1)


def swap(value, mask):
    return lax.ppermute(value, "px", [(i, i ^ mask) for i in range(lax.axis_size("px"))])


def pair_swap(value, axis, odd):
    devices = lax.axis_size(axis)
    return lax.ppermute(value, axis, [(i, ((i - odd) ^ 1) + odd) for i in range(odd, devices - odd)])


def exchange(faces, axis):
    even = pair_swap(faces[0], axis, 0)
    odd = pair_swap(faces[1], axis, 1)
    return even, odd


def z_exchange(faces):
    last_x, last_z = lax.axis_size("px") - 1, lax.axis_size("pz") - 1
    flat = lambda x, z: x * (last_z + 1) + z
    direct = [(flat(x, a), flat(x, b)) for x in range(1, last_x) for a, b in ((1, 2), (2, 1))]
    out, back = [], []
    for x, over in ((0, last_x // 2 + 1), (last_x, last_x // 2)):
        out += [(flat(x, 1), flat(over, last_z)), (flat(x, 2), flat(over, 0))]
        back += [(flat(over, last_z), flat(x, 2)), (flat(over, 0), flat(x, 1))]
    even = pair_swap(faces[0], "pz", 0)
    odd = lax.ppermute(faces[1], ("px", "pz"), direct + out)
    over = lax.ppermute(odd, ("px", "pz"), back)
    return even, odd, over


def by_parity(axis, low, high):
    even = lax.axis_index(axis) % 2 == 0
    return jnp.where(even, high, low), jnp.where(even, low, high)


def inside(axis):
    at = lax.axis_index(axis)
    below = jnp.where(at > 0, 1.0, 0.0).astype(jnp.float32)
    above = jnp.where(at < lax.axis_size(axis) - 1, 1.0, 0.0).astype(jnp.float32)
    return below, above


def update_rows(refs, store, block, width, height, is_first, is_last, outer):
    u, before, after, low, high, xe, xo, ze, zo, zo_over, k, s = refs
    x_at, z_at = lax.axis_index("px"), lax.axis_index("pz")
    x_outer = (x_at == 0) | (x_at == lax.axis_size("px") - 1)
    z_inner = ((z_at > 0) & (z_at < lax.axis_size("pz") - 1)).astype(jnp.float32)
    x_even = lax.axis_index("px") % 2 == 0
    z_even = lax.axis_index("pz") % 2 == 0
    y_below, y_above = inside("py")
    sub = lax.broadcasted_iota(jnp.int32, (height, u.shape[-1]), 0)
    at_low = sub == 0
    at_high = sub == height - 1

    def one_row(r, below, above):
        for x in range(width):
            c = u[r, x]
            left = jnp.where(x_even, xo[r], xe[r]) if x == 0 else u[r, x - 1]
            right = jnp.where(x_even, xe[r], xo[r]) if x == width - 1 else u[r, x + 1]
            line = r * width + x
            z_first = ze[pl.ds(line, 1), :]
            z_second = jnp.where(x_outer, zo_over[pl.ds(line, 1), :], zo[pl.ds(line, 1), :]) * z_inner
            zd = jnp.where(at_low, jnp.where(z_even, z_second, z_first), pltpu.roll(c, 1, 0))
            zu = jnp.where(at_high, jnp.where(z_even, z_first, z_second), pltpu.roll(c, height - 1, 0))
            spread = below(x) + above(x) + left + right + zd + zu - 6.0 * c
            store(r, x, c + k[r, x] * spread + s[r, x])

    def lowest(x):
        return jnp.where(is_first, low[0, x] * y_below if outer[0] else low[0, x], before[0, x])

    def highest(x):
        return jnp.where(is_last, high[0, x] * y_above if outer[1] else high[0, x], after[0, x])

    one_row(0, lowest, lambda x: u[1, x])

    def middle(r, carry):
        one_row(r, lambda x: u[r - 1, x], lambda x: u[r + 1, x])
        return carry

    lax.fori_loop(1, block - 1, middle, 0)
    one_row(block - 1, lambda x: u[block - 2, x], highest)


def corner_body(right, middle, layer):
    at = lax.axis_index("px")
    column = at % 4
    right[0] = column // 2
    middle[0] = (column // 2 + column) % 2
    layer[0] = at // 4


def corner():
    bit = jax.ShapeDtypeStruct((1,), jnp.int32)
    return pl.pallas_call(
        corner_body,
        out_specs=[pl.BlockSpec(memory_space=pltpu.SMEM)] * 3,
        out_shape=[bit] * 3,
        compiler_params=pltpu.CompilerParams(vmem_limit_bytes=GRANT),
        name="corner",
    )()


def pick_body(low, high, even_face, odd_face):
    even_face[...], odd_face[...] = by_parity("px", low[:, 0], high[:, 0])


def pick(u, ranges, block):
    _, width, height, lanes = u.shape
    count = sum(length for _, length in ranges)
    position = positions(ranges, block)
    face = jax.ShapeDtypeStruct((count, height, lanes), jnp.float32)
    return pl.pallas_call(
        pick_body,
        grid=(count // block,),
        in_specs=[
            pl.BlockSpec((block, 1, height, lanes), lambda i: (position(i), 0, 0, 0)),
            pl.BlockSpec((block, 1, height, lanes), lambda i: (position(i), width - 1, 0, 0)),
        ],
        out_specs=[pl.BlockSpec((block, height, lanes), lambda i: (i, 0, 0))] * 2,
        out_shape=[face, face],
        compiler_params=pltpu.CompilerParams(dimension_semantics=("arbitrary",), vmem_limit_bytes=2 * GRANT),
        name="pick",
    )(u, u)


def step_body(*refs, block, position, last, extra, faces, outer):
    ins, outs = refs[:12], refs[12 + extra :]
    width, height = ins[0].shape[1:3]
    at = position(pl.program_id(0))
    kept = {}

    def store(r, x, value):
        outs[0][r, x] = value
        if x == 0:
            kept["low"] = value
        if x == width - 1:
            outs[3][r], outs[4][r] = by_parity("px", kept["low"], value)
        line = pl.ds(r * width + x, 1)
        outs[1][line, :], outs[2][line, :] = by_parity("pz", value[0:1], value[height - 1 : height])

    update_rows(ins, store, block, width, height, at == 0, at == last, outer)
    for face, (edge, row) in zip(outs[5:], faces):

        @pl.when(at == edge)
        def _(face=face, row=row):
            face[0] = outs[0][row]


def positions(ranges, block):
    def position(i):
        at, done = ranges[0][0] // block + i, ranges[0][1] // block
        for start, count in ranges[1:]:
            at = jnp.where(i < done, at, start // block + i - done)
            done += count // block
        return at

    return position


def field_specs(position, offset, rows, block, width, height, lanes, place):
    full = (block, width, height, lanes)
    one = (1, width, height, lanes)
    extra = offset // block
    at = lambda *g: position(place(*g))
    face = pl.BlockSpec((block, height, lanes), lambda *g: (extra + place(*g), 0, 0))
    edge = pl.BlockSpec((block * width, lanes), lambda *g: (at(*g), 0))
    return [
        pl.BlockSpec(full, lambda *g: (at(*g), 0, 0, 0)),
        pl.BlockSpec(one, lambda *g: (jnp.maximum(at(*g) * block - 1, 0), 0, 0, 0)),
        pl.BlockSpec(one, lambda *g: (jnp.minimum((at(*g) + 1) * block, rows - 1), 0, 0, 0)),
        pl.BlockSpec(one, lambda *g: (0, 0, 0, 0)),
        pl.BlockSpec(one, lambda *g: (0, 0, 0, 0)),
        face,
        face,
        edge,
        edge,
        edge,
        pl.BlockSpec(full, lambda *g: (at(*g), 0, 0, 0)),
        pl.BlockSpec(full, lambda *g: (at(*g), 0, 0, 0)),
    ]


def advance(u, halos, low, high, k, s, ranges, offset, targets, block):
    rows, width, height, lanes = u.shape
    count = sum(length for _, length in ranges)
    block = min(block, count)
    position = positions(ranges, block)
    last = rows // block - 1
    specs = field_specs(position, offset, rows, block, width, height, lanes, lambda i: i)
    operands = [u, u, u, low, high, *halos, k, s]
    aliases = {}
    for number, target in enumerate(targets):
        aliases[len(operands)] = number
        operands.append(target)
        specs.append(pl.BlockSpec(memory_space=pl.ANY))
    face = pl.BlockSpec((block, height, lanes), lambda i: (i, 0, 0))
    edge = pl.BlockSpec((block * width, lanes), lambda i: (position(i), 0))
    out_specs = [pl.BlockSpec((block, width, height, lanes), lambda i: (position(i), 0, 0, 0)), edge, edge, face, face]
    shapes = [u.shape] + [(rows * width, lanes)] * 2 + [(count, height, lanes)] * 2
    outer = (ranges[0][0] == 0, sum(ranges[-1]) == rows)
    faces = [(0, 0)] * outer[0] + [(last, block - 1)] * outer[1]
    out_specs += [pl.BlockSpec((1, width, height, lanes), lambda i: (0, 0, 0, 0))] * len(faces)
    shapes += [(1, width, height, lanes)] * len(faces)
    return pl.pallas_call(
        functools.partial(
            step_body, block=block, position=position, last=last, extra=len(targets), faces=faces, outer=outer
        ),
        grid=(count // block,),
        in_specs=specs,
        out_specs=out_specs,
        out_shape=[jax.ShapeDtypeStruct(shape, jnp.float32) for shape in shapes],
        input_output_aliases=aliases,
        compiler_params=pltpu.CompilerParams(dimension_semantics=("arbitrary",), vmem_limit_bytes=GRANT),
        name="advance",
    )(*operands)


def final_body(bit, *refs, block, per_part, position, last, extra, outer):
    ins, outs = refs[:12], refs[12 + extra :]
    width, height = ins[0].shape[1:3]
    p, i = pl.program_id(0), pl.program_id(1)
    at = position(jnp.where(p == 0, 1 - bit[0], bit[0]) * per_part + i)
    result, send, keep = outs
    totals = {}

    def stats_to(target):
        def store(r, x, value):
            result[r, x] = value
            moved = value - 1.0
            totals["sum"] = moved if x == 0 else totals["sum"] + moved
            totals["square"] = moved * moved if x == 0 else totals["square"] + moved * moved
            if x == width - 1:
                target[0, r] = totals["sum"]
                target[1, r] = totals["square"]

        update_rows(ins, store, block, width, height, at == 0, at == last, outer)

    @pl.when(p == 0)
    def _():
        stats_to(send)

    @pl.when(p == 1)
    def _():
        stats_to(keep)


def finish(u, halos, low, high, k, s, row0, count, target, bit, block):
    rows, width, height, lanes = u.shape
    block = min(block, count // 2)
    per_part = count // 2 // block
    position = positions([(row0, count)], block)

    def place(p, i, bit):
        return jnp.where(p == 0, 1 - bit[0], bit[0]) * per_part + i

    specs = field_specs(position, 0, rows, block, width, height, lanes, place)
    operands = [bit, u, u, u, low, high, *halos, k, s]
    aliases = {}
    if target is not None:
        aliases = {len(operands): 0}
        operands.append(target)
        specs.append(pl.BlockSpec(memory_space=pl.ANY))
    part = (2, block, height, lanes)
    out_specs = [
        pl.BlockSpec((block, width, height, lanes), lambda *g: (position(place(*g)), 0, 0, 0)),
        pl.BlockSpec(part, lambda p, i, m: (0, jnp.where(p == 0, i, per_part - 1), 0, 0)),
        pl.BlockSpec(part, lambda p, i, m: (0, jnp.where(p == 0, 0, i), 0, 0)),
    ]
    sums = (2, count // 2, height, lanes)
    return pl.pallas_call(
        functools.partial(
            final_body,
            block=block,
            per_part=per_part,
            position=position,
            last=rows // block - 1,
            extra=len(aliases),
            outer=(row0 == 0, row0 + count == rows),
        ),
        grid_spec=pltpu.PrefetchScalarGridSpec(
            num_scalar_prefetch=1, grid=(2, per_part), in_specs=specs, out_specs=out_specs
        ),
        out_shape=[jax.ShapeDtypeStruct(shape, jnp.float32) for shape in (u.shape, sums, sums)],
        input_output_aliases=aliases,
        compiler_params=pltpu.CompilerParams(
            dimension_semantics=("arbitrary", "arbitrary"), vmem_limit_bytes=GRANT
        ),
        name="finish",
    )(*operands)


def fold_body(bit, keep, came, mine, theirs):
    for half in range(2):
        total = keep[:, half] + came[:, half]

        @pl.when(half == bit[0])
        def _(total=total):
            mine[...] = total

        @pl.when(half != bit[0])
        def _(total=total):
            theirs[...] = total


def fold(keep, came, bit):
    _, rows, height, lanes = keep.shape
    cut = (2, 2, rows // 2, height, lanes)
    half = (2, rows // 2, height, lanes)
    return pl.pallas_call(
        fold_body,
        in_specs=[pl.BlockSpec(memory_space=pltpu.SMEM)] + [pl.BlockSpec(cut, lambda: (0,) * 5)] * 2,
        out_specs=[pl.BlockSpec(half, lambda: (0,) * 4)] * 2,
        out_shape=[jax.ShapeDtypeStruct(half, jnp.float32)] * 2,
        compiler_params=pltpu.CompilerParams(vmem_limit_bytes=GRANT),
        name="fold",
    )(bit, keep.reshape(cut), came.reshape(cut))


def scale_body(bit, piece_bit, u, *refs, parts, inverse):
    result = refs[-1]
    width = u.shape[1]

    def scaled(sums):
        def one_row(r, carry):
            mean = sums[0, 0, r] * inverse
            factor = lax.rsqrt(sums[0, 1, r] * inverse - mean * mean + 0.0001)
            mean = mean + 1.0
            for x in range(width):
                result[r, x] = (u[r, x] - mean) * factor
            return carry

        lax.fori_loop(0, u.shape[0], one_row, 0)

    for number, sums in enumerate(refs[:parts]):

        @pl.when(pl.program_id(0) == number)
        def _(sums=sums):
            scaled(sums)


def scale(u, halves, flips, bits, row0, target, line_length):
    _, width, height, lanes = u.shape
    pieces, _, block = halves[0].shape[:3]
    first = row0 // block

    def at(p, i, bit, piece_bit):
        flip = jnp.where(p == 0, flips[0], flips[-1])
        return first + (bit[0] ^ flip) * pieces + (piece_bit[0] ^ i)

    full = pl.BlockSpec((block, width, height, lanes), lambda *g: (at(*g), 0, 0, 0))
    part = (1, 2, block, height, lanes)
    specs = [full]
    for number in range(len(halves)):
        specs.append(
            pl.BlockSpec(
                part,
                lambda p, i, *m, number=number: (
                    jnp.where(p == number, i, jnp.where(p < number, 0, pieces - 1)), 0, 0, 0, 0
                ),
            )
        )
    operands = [*bits, u, *halves]
    aliases = {}
    if target is not None:
        aliases = {len(operands): 0}
        operands.append(target)
        specs.append(pl.BlockSpec(memory_space=pl.ANY))
    return pl.pallas_call(
        functools.partial(scale_body, parts=len(halves), inverse=1.0 / line_length),
        grid_spec=pltpu.PrefetchScalarGridSpec(
            num_scalar_prefetch=2, grid=(len(halves), pieces), in_specs=specs, out_specs=full
        ),
        out_shape=jax.ShapeDtypeStruct(u.shape, jnp.float32),
        input_output_aliases=aliases,
        compiler_params=pltpu.CompilerParams(
            dimension_semantics=("arbitrary", "arbitrary"), vmem_limit_bytes=GRANT
        ),
        name="scale",
    )(*operands)


def body(u, k, s):
    rows, width, height, lanes = u.shape
    half, quarter = rows // 2, rows // 4
    right, middle, layer = corner()
    routes = {
        "near": (1, 3, 4, (middle, right)),
        "far": (3, 1, 4, (right, middle)),
        "over_near": (4, 1, 3, (layer, middle)),
        "over_far": (4, 3, 1, (layer, right)),
    }

    inner = [(quarter, half)]
    outer = [(0, quarter), (rows - quarter, quarter)]
    quarters = [(quarter, quarter), (half, quarter), (0, quarter), (rows - quarter, quarter)]

    start = pltpu.with_memory_space_constraint(u, pltpu.HBM)
    x_halos = [exchange(pick(start, inner, quarter), "px"), exchange(pick(start, outer, quarter), "px")]
    z_halos = z_exchange(by_parity("pz", u[:, :, 0].reshape(-1, lanes), u[:, :, height - 1].reshape(-1, lanes)))
    y_low = send_up(u[rows - 1 :], "py")
    y_high = send_down(u[:1], "py")
    for step in range(1, STEPS):
        targets = ()
        arrived, borders = [], []
        chunks = [inner, outer] if step < STEPS - 1 else [[part] for part in quarters]
        for number, ranges in enumerate(chunks):
            received = x_halos[number * 2 // len(chunks)]
            offset = number % 2 * quarter if len(chunks) == 4 else 0
            low, high = (y_low, y_high) if number >= len(chunks) // 2 else (u, u)
            number = number * 4 // len(chunks)
            out = advance(u, (*received, *z_halos), low, high, k, s, ranges, offset, targets, 16)
            targets = out[:3]
            arrived.append(exchange(out[3:5], "px"))
            borders += out[5:]
        u = targets[0]
        z_halos = z_exchange(targets[1:])
        y_high = send_down(borders[0], "py")
        y_low = send_up(borders[1], "py")
        x_halos = arrived

    def line_sums(send, keep, route):
        outer_mask, inner_mask, last_mask, bits = route
        mine, theirs = fold(keep, swap(send, outer_mask), bits[1])
        total = mine + swap(theirs, inner_mask)
        total = total + swap(total, last_mask)
        total = jnp.stack([total, swap(total, inner_mask)])
        return total, swap(total, outer_mask), bits

    end = None
    sums = []
    for number, (row0, count) in enumerate(quarters):
        route = routes[ROUTES[number]]
        low, high = (y_low, y_high) if number >= 2 else (u, u)
        end, send, keep = finish(u, (*x_halos[number], *z_halos), low, high, k, s, row0, count, end, route[3][0], 8)
        sums.append(line_sums(send, keep, route))
    result = None
    for number, wanted in SCALES:
        own, other, bits = sums[number]
        halves = {"both": ((own, other), (0, 1)), "own": ((own,), (0,)), "other": ((other,), (1,))}[wanted]
        result = scale(end, *halves, bits, quarters[number][0], result, width * lax.axis_size("px"))
    return result, end


def solution(mesh):
    placed = P("py", "px", "pz", None)
    return jax.shard_map(
        body, mesh=mesh, in_specs=(placed, placed, placed), out_specs=(placed, placed), check_vma=False
    )
```

time: 341 us -> 279 us (0.82)
  Pallas kernels: 118 us -> 59.1 us
  starting transfers between devices: 80.8 us -> 102 us
  waiting for transfers between devices: 119 us -> 99.9 us
  other arithmetic: 6.92 us -> 3.2 us
    pallas_call x12 -> x18, Pallas kernels: 82.3 us -> 39.3 us  [the longest x8 21.3 us: advance(): pl.pallas_call(functools.partial(step_body, block=block, position=positio...]
    ppermute x20, starting transfers between devices: 11.3 us -> 32 us  [swap(): lax.ppermute(value, 'px', [(i, i ^ mask) for i in range(lax.axis_size('px...]
    ppermute x20, waiting for transfers between devices: 50.9 us -> 34.1 us  [swap(): lax.ppermute(value, 'px', [(i, i ^ mask) for i in range(lax.axis_size('px...]
    pallas_call x4, Pallas kernels: 28.4 us -> 14.5 us  [finish(): pl.pallas_call(functools.partial(final_body, block=block, per_part=per_pa...]
    ppermute x8, waiting for transfers between devices: 14.1 us -> 9.31 us  [ring(): lax.ppermute(value, axis, [(i, (i + shift) % devices) for i in range(devi...]
    ppermute x24, starting transfers between devices: 28.4 us -> 32.1 us  [pair_swap(): lax.ppermute(value, axis, [(i, (i - odd ^ 1) + odd) for i in range(odd, d...]
    unnamed x86 -> x14, local copies, waits for them, and re-layouts: 9.15 us -> 10.2 us
  transfers between devices with their start and end apart: 60 -> 60, of which waited for: 26 -> 25; matrix products, arithmetic and copies ran while one was open for 2% -> 1% of each run, Pallas kernels for 33% -> 20%
where the time goes in v2:
time: 279 us; the launch traced here: 277 us
  starting transfers between devices  102 us (37%)
  waiting for transfers between devices  99.9 us (36%)
  Pallas kernels  59.1 us (21%)
  local copies, waits for them, and re-layouts  11 us (4%)
  other arithmetic  3.2 us (1%)
    ppermute x20, waiting for transfers between devices, swap(): lax.ppermute(value, 'px', [(i, i ^ mask) for i in range(lax.axis_size('px...  34.1 us
    ppermute x4, waiting for transfers between devices, z_exchange(): over = lax.ppermute(odd, ('px', 'pz'), back)  32.3 us
    ppermute x24, starting transfers between devices, pair_swap(): lax.ppermute(value, axis, [(i, (i - odd ^ 1) + odd) for i in range(odd, d...  32.1 us
    ppermute x20, starting transfers between devices, swap(): lax.ppermute(value, 'px', [(i, i ^ mask) for i in range(lax.axis_size('px...  32 us
    ppermute x4, starting transfers between devices, z_exchange(): odd = lax.ppermute(faces[1], ('px', 'pz'), direct + out)  23.9 us
    pallas_call x8, Pallas kernels, advance(): pl.pallas_call(functools.partial(step_body, block=block, position=positio...  21.3 us
    ppermute x4, waiting for transfers between devices, z_exchange(): odd = lax.ppermute(faces[1], ('px', 'pz'), direct + out)  15.8 us
    pallas_call x5, Pallas kernels, scale(): pl.pallas_call(functools.partial(scale_body, parts=len(halves), inverse=1...  14.7 us
  transfers between devices with their start and end apart: 60, of which 25 were waited for; matrix products, arithmetic and copies ran while one was open for 1% of the time, Pallas kernels for 20%

profile of v2, /device:TPU:1, one launch (start us, length us, event | category | flops | bytes accessed | tf_op | source)
XLA Modules:
  0.0 276.6 jit_solution(9458916306154673440)
XLA Ops:
  0.6 2.6 pick.3
  6.0 2.7 pick.2
  8.7 3.3 %collective-permute-start.2 = (f32[64,32,128]{2,1,0:T(8,128)}, f32[64,32,128]{2,1,0:T(8,128)S(1)}, u32[]{:S(2)}, u32[]{:S(2)}) collective-permute-start(f32[64,32,128]{2,1,0:T(8,128)} %get-tuple-element.77), channel_id=1, source_target_pairs={{0,4},{4,0},{8,12},{12,8},{16,20},{20,16},{24,28},{28,24},{1,5},{5... | collective-permute-start | bytes 3145736 | tf_op jit(solution)/shard_map/ppermute | solution.py:36
  13.6 2.8 broadcast_select_fusion
  16.4 7.4 %collective-permute-start.5 = (f32[512,128]{1,0:T(8,128)S(1)}, f32[512,128]{1,0:T(8,128)S(1)}, u32[]{:S(2)}, u32[]{:S(2)}) collective-permute-start(f32[512,128]{1,0:T(8,128)S(1)} %bitcast.37), channel_id=1, source_target_pairs={{5,6},{6,5},{9,10},{10,9},{13,14},{14,13},{17,18},{18,17},{21,22},... | collective-permute-start | bytes 786440 | tf_op jit(solution)/shard_map/ppermute | solution.py:54
  23.8 6.1 %collective-permute-done.5.refs_8_ = f32[512,128]{1,0:T(8,128)S(1)} collective-permute-done((f32[512,128]{1,0:T(8,128)S(1)}, f32[512,128]{1,0:T(8,128)S(1)}, u32[]{:S(2)}, u32[]{:S(2)}) %collective-permute-start.5) | collective-permute-done | bytes 262176 | tf_op jit(solution)/shard_map/ppermute | solution.py:54
  33.6 5.8 %collective-permute-done.6.refs_9_ = f32[512,128]{1,0:T(8,128)S(1)} collective-permute-done((f32[512,128]{1,0:T(8,128)S(1)}, f32[512,128]{1,0:T(8,128)S(1)}, u32[]{:S(2)}, u32[]{:S(2)}) %collective-permute-start.6) | collective-permute-done | bytes 262176 | tf_op jit(solution)/shard_map/ppermute | solution.py:55
  40.7 3.4 %copy-done = f32[128,4,32,128]{3,2,1,0:T(8,128)S(1)} copy-done((f32[128,4,32,128]{3,2,1,0:T(8,128)S(1)}, f32[128,4,32,128]{3,2,1,0:T(8,128)}, u32[]{:S(2)}) %copy-start) | copy-done | bytes 8388632
  44.1 3.4 %copy-done.1 = f32[128,4,32,128]{3,2,1,0:T(8,128)S(1)} copy-done((f32[128,4,32,128]{3,2,1,0:T(8,128)S(1)}, f32[128,4,32,128]{3,2,1,0:T(8,128)}, u32[]{:S(2)}) %copy-start.1) | copy-done | bytes 8388632
  47.5 3.4 %copy-done.2 = f32[128,4,32,128]{3,2,1,0:T(8,128)S(1)} copy-done((f32[128,4,32,128]{3,2,1,0:T(8,128)S(1)}, f32[128,4,32,128]{3,2,1,0:T(8,128)}, u32[]{:S(2)}) %copy-start.2) | copy-done | bytes 8388632
  50.9 3.0 %advance.8 = (f32[128,4,32,128]{3,2,1,0:T(8,128)S(1)}, f32[512,128]{1,0:T(8,128)S(1)}, f32[512,128]{1,0:T(8,128)S(1)}, f32[64,32,128]{2,1,0:T(8,128)S(1)}, f32[64,32,128]{2,1,0:T(8,128)S(1)}) custom-call(f32[128,4,32,128]{3,2,1,0:T(8,128)S(1)} %copy-done, f32[128,4,32,128]{3,2,1,0:T(8,128)S(1)} %copy-done, f32[128,4,32,128]{3,2,1,0:T(8,128)S(1)} %copy-done, ...), custom_call_target="tpu_custom_call" | custom-call | tf_op jit(solution)/shard_map/advance/pallas_call | solution.py:232
  58.2 5.9 %advance.9 = (f32[128,4,32,128]{3,2,1,0:T(8,128)S(1)}, f32[512,128]{1,0:T(8,128)S(1)}, f32[512,128]{1,0:T(8,128)S(1)}, f32[64,32,128]{2,1,0:T(8,128)S(1)}, f32[6...) custom-call(f32[128,4,32,128]{3,2,1,0:T(8,128)S(1)} %copy-done, ...), custom_call_target="tpu_custom_call", output_to_operand_aliasing={{0}: (12, {}), {1}: (13, {}), {2}: (14, {})} | custom-call | tf_op jit(solution)/shard_map/advance/pallas_call | solution.py:232
  64.2 2.7 collective-permute-start.11
  67.6 5.7 %collective-permute-start.14 = (f32[512,128]{1,0:T(8,128)S(1)}, f32[512,128]{1,0:T(8,128)S(1)}, u32[]{:S(2)}, u32[]{:S(2)}) collective-permute-start(f32[512,128]{1,0:T(8,128)S(1)} %get-tuple-element.90), channel_id=1, source_target_pairs={{5,6},{6,5},{9,10},{10,9},{13,14},{14,13},{17,18},{18,17},{21,22},... | collective-permute-start | bytes 786440 | tf_op jit(solution)/shard_map/ppermute | solution.py:54
  73.3 3.3 %collective-permute-done.14.refs_8_ = f32[512,128]{1,0:T(8,128)S(1)} collective-permute-done((f32[512,128]{1,0:T(8,128)S(1)}, f32[512,128]{1,0:T(8,128)S(1)}, u32[]{:S(2)}, u32[]{:S(2)}) %collective-permute-start.14) | collective-permute-done | bytes 262176 | tf_op jit(solution)/shard_map/ppermute | solution.py:54
  79.4 12.7 %collective-permute-done.15.refs_9_ = f32[512,128]{1,0:T(8,128)S(1)} collective-permute-done((f32[512,128]{1,0:T(8,128)S(1)}, f32[512,128]{1,0:T(8,128)S(1)}, u32[]{:S(2)}, u32[]{:S(2)}) %collective-permute-start.15) | collective-permute-done | bytes 262176 | tf_op jit(solution)/shard_map/ppermute | solution.py:55
  94.7 3.1 %advance.10 = (f32[128,4,32,128]{3,2,1,0:T(8,128)S(1)}, f32[512,128]{1,0:T(8,128)S(1)}, f32[512,128]{1,0:T(8,128)S(1)}, f32[64,32,128]{2,1,0:T(8,128)S(1)}, f32[64,32,128]{2,1,0:T(8,128)S(1)}) custom-call(f32[128,4,32,128]{3,2,1,0:T(8,128)S(1)} %get-tuple-element.84.refs_0_.refs_1_.refs_2_.refs_3_.refs_4_, ...), custom_call_target="tpu_custom_call" | custom-call | tf_op jit(solution)/shard_map/advance/pallas_call | solution.py:232
  98.7 4.3 %collective-permute-done.9.refs_3_ = f32[1,4,32,128]{3,2,1,0:T(8,128)S(1)} collective-permute-done((f32[1,4,32,128]{3,2,1,0:T(8,128)S(1)}, f32[1,4,32,128]{3,2,1,0:T(8,128)S(1)}, u32[]{:S(2)}, u32[]{:S(2)}) %collective-permute-start.9) | collective-permute-done | bytes 65568 | tf_op jit(solution)/shard_map/ppermute | solution.py:19
  103.0 3.1 %advance.11 = (f32[128,4,32,128]{3,2,1,0:T(8,128)S(1)}, f32[512,128]{1,0:T(8,128)S(1)}, f32[512,128]{1,0:T(8,128)S(1)}, f32[64,32,128]{2,1,0:T(8,128)S(1)}, f32[...) custom-call(f32[128,4,32,128]{3,2,1,0:T(8,128)S(1)} %get-tuple-eleme, ...), custom_call_target="tpu_custom_call", output_to_operand_aliasing={{0}: (12, {}), {1}: (13, {}), {2}: (14, {})} | custom-call | tf_op jit(solution)/shard_map/advance/pallas_call | solution.py:232
  106.2 2.7 collective-permute-start.20
  109.6 5.5 %collective-permute-start.23 = (f32[512,128]{1,0:T(8,128)S(1)}, f32[512,128]{1,0:T(8,128)S(1)}, u32[]{:S(2)}, u32[]{:S(2)}) collective-permute-start(f32[512,128]{1,0:T(8,128)S(1)} %get-tuple-element.102), channel_id=1, source_target_pairs={{5,6},{6,5},{9,10},{10,9},{13,14},{14,13},{17,18},{18,17},{21,22},... | collective-permute-start | bytes 786440 | tf_op jit(solution)/shard_map/ppermute | solution.py:54
  115.1 3.3 %collective-permute-done.23.refs_8_ = f32[512,128]{1,0:T(8,128)S(1)} collective-permute-done((f32[512,128]{1,0:T(8,128)S(1)}, f32[512,128]{1,0:T(8,128)S(1)}, u32[]{:S(2)}, u32[]{:S(2)}) %collective-permute-start.23) | collective-permute-done | bytes 262176 | tf_op jit(solution)/shard_map/ppermute | solution.py:54
  121.2 12.9 %collective-permute-done.24.refs_9_ = f32[512,128]{1,0:T(8,128)S(1)} collective-permute-done((f32[512,128]{1,0:T(8,128)S(1)}, f32[512,128]{1,0:T(8,128)S(1)}, u32[]{:S(2)}, u32[]{:S(2)}) %collective-permute-start.24) | collective-permute-done | bytes 262176 | tf_op jit(solution)/shard_map/ppermute | solution.py:55
  141.8 3.7 %collective-permute-done.20.refs_5_ = f32[64,32,128]{2,1,0:T(8,128)S(1)} collective-permute-done((f32[64,32,128]{2,1,0:T(8,128)S(1)}, f32[64,32,128]{2,1,0:T(8,128)S(1)}, u32[]{:S(2)}, u32[]{:S(2)}) %collective-permute-start.20) | collective-permute-done | bytes 1048608 | tf_op jit(solution)/shard_map/ppermute | solution.py:36
  151.4 3.6 %collective-permute-start.36 = (f32[32,32,128]{2,1,0:T(8,128)S(1)}, f32[32,32,128]{2,1,0:T(8,128)S(1)}, u32[]{:S(2)}, u32[]{:S(2)}) collective-permute-start(f32[32,32,128]{2,1,0:T(8,128)S(1)} %get-tuple-element.124), channel_id=1, source_target_pairs={{0,4},{4,0},{8,12},{12,8},{16,20},{20,16},{24,28},{28,24},{1,5},{5... | collective-permute-start | bytes 1572872 | tf_op jit(solution)/shard_map/ppermute | solution.py:36
  155.0 5.3 %collective-permute-start.32 = (f32[512,128]{1,0:T(8,128)S(1)}, f32[512,128]{1,0:T(8,128)S(1)}, u32[]{:S(2)}, u32[]{:S(2)}) collective-permute-start(f32[512,128]{1,0:T(8,128)S(1)} %get-tuple-element.120), channel_id=1, source_target_pairs={{5,6},{6,5},{9,10},{10,9},{13,14},{14,13},{17,18},{18,17},{21,22},... | collective-permute-start | bytes 786440 | tf_op jit(solution)/shard_map/ppermute | solution.py:54
  160.4 3.2 %collective-permute-done.32.refs_8_ = f32[512,128]{1,0:T(8,128)S(1)} collective-permute-done((f32[512,128]{1,0:T(8,128)S(1)}, f32[512,128]{1,0:T(8,128)S(1)}, u32[]{:S(2)}, u32[]{:S(2)}) %collective-permute-start.32) | collective-permute-done | bytes 262176 | tf_op jit(solution)/shard_map/ppermute | solution.py:54
  165.6 5.0 %collective-permute-start.34 = (f32[32,32,128]{2,1,0:T(8,128)S(1)}, f32[32,32,128]{2,1,0:T(8,128)S(1)}, u32[]{:S(2)}, u32[]{:S(2)}) collective-permute-start(f32[32,32,128]{2,1,0:T(8,128)S(1)} %get-tuple-element.122), channel_id=1, source_target_pairs={{0,4},{4,0},{8,12},{12,8},{16,20},{20,16},{24,28},{28,24},{1,5},{5... | collective-permute-start | bytes 1572872 | tf_op jit(solution)/shard_map/ppermute | solution.py:36
  171.3 4.2 %collective-permute-start.29 = (f32[32,32,128]{2,1,0:T(8,128)S(1)}, f32[32,32,128]{2,1,0:T(8,128)S(1)}, u32[]{:S(2)}, u32[]{:S(2)}) collective-permute-start(f32[32,32,128]{2,1,0:T(8,128)S(1)} %get-tuple-element.117), channel_id=1, source_target_pairs={{0,4},{4,0},{8,12},{12,8},{16,20},{20,16},{24,28},{28,24},{1,5},{5... | collective-permute-start | bytes 1572872 | tf_op jit(solution)/shard_map/ppermute | solution.py:36
  177.9 3.6 %finish.4 = (f32[128,4,32,128]{3,2,1,0:T(8,128)}, f32[2,16,32,128]{3,2,1,0:T(8,128)S(1)}, f32[2,16,32,128]{3,2,1,0:T(8,128)S(1)}) custom-call(s32[1]{0:T(128)} %get-tuple-element.75.bit, f32[128,4,32,128]{3,2,1,0:T(8,128)S(1)} %get-tuple-element.114.refs_0_.refs_1_.refs_2_.refs_3_.refs_4_, ...), custom_call_target="tpu_custom_call" | custom-call | tf_op jit(solution)/shard_map/finish/pallas_call | solution.py:298
  183.7 3.6 %finish.5 = (f32[128,4,32,128]{3,2,1,0:T(8,128)}, f32[2,16,32,128]{3,2,1,0:T(8,128)S(1)}, f32[2,16,32,128]{3,2,1,0:T(8,128)S(1)}) custom-call(s32[1]{0:T(128)} %get-tuple-element.76.bit.piece_bit, f32[128,4,32,128]{3,2,1,0:T(8,128)S(1)} %get-tuple-element.114.refs_0_.refs_1_.refs_2_.refs_3_.refs_4_, ...), custom_call_target="tpu_custom_call", output_to_operand_aliasing={{0}: (13, {})} | custom-call | tf_op jit(solution)/shard_map/finish/pallas_call | solution.py:298
  187.3 3.6 %finish.6 = (f32[128,4,32,128]{3,2,1,0:T(8,128)}, f32[2,16,32,128]{3,2,1,0:T(8,128)S(1)}, f32[2,16,32,128]{3,2,1,0:T(8,128)S(1)}) custom-call(s32[1]{0:T(128)} %get-tuple-element.121.bit.piece_bit, f32[128,4,32,128]{3,2,1,0:T(8,128)S(1)} %get-tuple-element.114.refs_0_.refs_1_.refs_2_.refs_3_.refs_4_, ...), custom_call_target="tpu_custom_call", output_to_operand_aliasing={{0}: (13, {})} | custom-call | tf_op jit(solution)/shard_map/finish/pallas_call | solution.py:298
  191.0 6.0 %collective-permute-start.50 = (f32[2,16,32,128]{3,2,1,0:T(8,128)S(1)}, f32[2,16,32,128]{3,2,1,0:T(8,128)S(1)}, u32[]{:S(2)}, u32[]{:S(2)}) collective-permute-start(f32[2,16,32,128]{3,2,1,0:T(8,128)S(1)} %get-tuple-element.141), channel_id=1, source_target_pairs={{0,12},{4,8},{8,4},{12,0},{16,28},{20,24},{24,20},{28,16},{1,13},{... | collective-permute-start | bytes 1572872 | tf_op jit(solution)/shard_map/ppermute | solution.py:31
  197.0 3.6 %finish.7 = (f32[128,4,32,128]{3,2,1,0:T(8,128)}, f32[2,16,32,128]{3,2,1,0:T(8,128)S(1)}, f32[2,16,32,128]{3,2,1,0:T(8,128)S(1)}) custom-call(s32[1]{0:T(128)} %get-tuple-element.75.bit, f32[128,4,32,128]{3,2,1,0:T(8,128)S(1)} %get-tuple-element.114.refs_0_.refs_1_.refs_2_.refs_3_.refs_4_, ...), custom_call_target="tpu_custom_call", output_to_operand_aliasing={{0}: (13, {})} | custom-call | tf_op jit(solution)/shard_map/finish/pallas_call | solution.py:298
  200.7 7.2 %collective-permute-start.40 = (f32[2,16,32,128]{3,2,1,0:T(8,128)S(1)}, f32[2,16,32,128]{3,2,1,0:T(8,128)S(1)}, u32[]{:S(2)}, u32[]{:S(2)}) collective-permute-start(f32[2,16,32,128]{3,2,1,0:T(8,128)S(1)} %get-tuple-element.133), channel_id=1, source_target_pairs={{0,16},{4,20},{8,24},{12,28},{16,0},{20,4},{24,8},{28,12},{1,17},{... | collective-permute-start | bytes 1572872 | tf_op jit(solution)/shard_map/ppermute | solution.py:31
  207.8 9.7 %collective-permute-done.55 = f32[2,16,32,128]{3,2,1,0:T(8,128)S(1)} collective-permute-done((f32[2,16,32,128]{3,2,1,0:T(8,128)S(1)}, f32[2,16,32,128]{3,2,1,0:T(8,128)S(1)}, u32[]{:S(2)}, u32[]{:S(2)}) %collective-permute-start.55) | collective-permute-done | bytes 524320 | tf_op jit(solution)/shard_map/ppermute | solution.py:31
  221.4 2.7 collective-permute-start.46
  224.1 4.4 %collective-permute-done.40 = f32[2,16,32,128]{3,2,1,0:T(8,128)S(1)} collective-permute-done((f32[2,16,32,128]{3,2,1,0:T(8,128)S(1)}, f32[2,16,32,128]{3,2,1,0:T(8,128)S(1)}, u32[]{:S(2)}, u32[]{:S(2)}) %collective-permute-start.40) | collective-permute-done | bytes 524320 | tf_op jit(solution)/shard_map/ppermute | solution.py:31
  229.3 2.7 collective-permute-start.57
  233.7 3.2 %collective-permute-done.41 = f32[2,8,32,128]{3,2,1,0:T(8,128)S(1)} collective-permute-done((f32[2,8,32,128]{3,2,1,0:T(8,128)S(1)}, f32[2,8,32,128]{3,2,1,0:T(8,128)S(1)}, u32[]{:S(2)}, u32[]{:S(2)}) %collective-permute-start.41) | collective-permute-done | bytes 262176 | tf_op jit(solution)/shard_map/ppermute | solution.py:31
  237.0 2.7 collective-permute-start.42
  241.4 2.6 collective-permute-done.47
  247.3 4.4 %collective-permute-done.53 = f32[2,8,32,128]{3,2,1,0:T(8,128)S(1)} collective-permute-done((f32[2,8,32,128]{3,2,1,0:T(8,128)S(1)}, f32[2,8,32,128]{3,2,1,0:T(8,128)S(1)}, u32[]{:S(2)}, u32[]{:S(2)}) %collective-permute-start.53) | collective-permute-done | bytes 262176 | tf_op jit(solution)/shard_map/ppermute | solution.py:31
  252.2 5.1 %collective-permute-done.43 = f32[2,8,32,128]{3,2,1,0:T(8,128)S(1)} collective-permute-done((f32[2,8,32,128]{3,2,1,0:T(8,128)S(1)}, f32[2,8,32,128]{3,2,1,0:T(8,128)S(1)}, u32[]{:S(2)}, u32[]{:S(2)}) %collective-permute-start.43) | collective-permute-done | bytes 262176 | tf_op jit(solution)/shard_map/ppermute | solution.py:31
  257.5 3.3 %scale.5.refs_2_ = f32[128,4,32,128]{3,2,1,0:T(8,128)} custom-call(s32[1]{0:T(128)} %get-tuple-element.75.bit, s32[1]{0:T(128)} %get-tuple-element.76.bit.piece_bit, f32[128,4,32,128]{3,2,1,0:T(8,128)S(1)} %copy-done.4, f32[2,2,8,32,128]{4,3,2,1,0:T(8,128)S(1)} %pad_maximum_fusion.3.refs_0_, f32[2,2,8,32,128]{4,3,2,1,0:T(8,128)S(1)} %collective-permute-done.59.refs_1_), custom_call_target="tpu_custom_call" | custom-call | tf_op jit(solution)/shard_map/scale/pallas_call | solution.py:396
  261.9 3.3 %scale.6.refs_2_ = f32[128,4,32,128]{3,2,1,0:T(8,128)} custom-call(s32[1]{0:T(128)} %get-tuple-element.121.bit.piece_bit, s32[1]{0:T(128)} %get-tuple-element.76.bit.piece_bit, f32[128,4,32,128]{3,2,1,0:T(8,128)S(1)} %copy-done.4, f32[2,2,8,32,128]{4,3,2,1,0:T(8,128)S(1)} %pad_maximum_fusion.2.refs_0_, ...), custom_call_target="tpu_custom_call", output_to_operand_aliasing={{}: (5, {})} | custom-call | tf_op jit(solution)/shard_map/scale/pallas_call | solution.py:396
  265.2 3.3 %collective-permute-done.49.refs_1_ = f32[2,2,8,32,128]{4,3,2,1,0:T(8,128)S(1)} collective-permute-done((f32[2,2,8,32,128]{4,3,2,1,0:T(8,128)S(1)}, f32[2,2,8,32,128]{4,3,2,1,0:T(8,128)S(1)}, u32[]{:S(2)}, u32[]{:S(2)}) %collective-permute-start.49) | collective-permute-done | bytes 524320 | tf_op jit(solution)/shard_map/ppermute | solution.py:31
  268.5 3.3 %scale.7.refs_1_ = f32[128,4,32,128]{3,2,1,0:T(8,128)} custom-call(s32[1]{0:T(128)} %get-tuple-element.76.bit.piece_bit, s32[1]{0:T(128)} %get-tuple-element.121.bit.piece_bit, f32[128,4,32,128]{3,2,1,0:T(8,128)S(1)} %copy-done.4, f32[2,2,8,32,128]{4,3,2,1,0:T(8,128)S(1)} %pad_maximum_fusion.1.refs_0_, ...), custom_call_target="tpu_custom_call", output_to_operand_aliasing={{}: (5, {})} | custom-call | tf_op jit(solution)/shard_map/scale/pallas_call | solution.py:396
  (125 shorter events, 63.1 us)
Async XLA Ops:
  3.3 37.4 %collective-permute-start.7 = (f32[64,32,128]{2,1,0:T(8,128)}, f32[64,32,128]{2,1,0:T(8,128)S(1)}, u32[]{:S(2)}, u32[]{:S(2)}) collective-permute-start(f32[64,32,128]{2,1,0:T(8,128)} %get-tuple-element.79), channel_id=1, source_target_pairs={{0,4},{4,0},{8,12},{12,8},{16,20},{20,16},{24,28},{28,24},{1,5},{5... | collective-permute-start | bytes 3145736 | tf_op jit(solution)/shard_map/ppermute | solution.py:36
  5.3 35.4 %collective-permute-start.8 = (f32[64,32,128]{2,1,0:T(8,128)}, f32[64,32,128]{2,1,0:T(8,128)S(1)}, u32[]{:S(2)}, u32[]{:S(2)}) collective-permute-start(f32[64,32,128]{2,1,0:T(8,128)} %get-tuple-element.80), channel_id=1, source_target_pairs={{4,8},{8,4},{12,16},{16,12},{20,24},{24,20},{5,9},{9,5},{13,17},{1... | collective-permute-start | bytes 3145736 | tf_op jit(solution)/shard_map/ppermute | solution.py:36
  8.7 49.5 %collective-permute-start.2 = (f32[64,32,128]{2,1,0:T(8,128)}, f32[64,32,128]{2,1,0:T(8,128)S(1)}, u32[]{:S(2)}, u32[]{:S(2)}) collective-permute-start(f32[64,32,128]{2,1,0:T(8,128)} %get-tuple-element.77), channel_id=1, source_target_pairs={{0,4},{4,0},{8,12},{12,8},{16,20},{20,16},{24,28},{28,24},{1,5},{5... | collective-permute-start | bytes 3145736 | tf_op jit(solution)/shard_map/ppermute | solution.py:36
  12.0 46.2 %collective-permute-start.3 = (f32[64,32,128]{2,1,0:T(8,128)}, f32[64,32,128]{2,1,0:T(8,128)}, u32[]{:S(2)}, u32[]{:S(2)}) collective-permute-start(f32[64,32,128]{2,1,0:T(8,128)} %get-tuple-element.78), channel_id=1, source_target_pairs={{4,8},{8,4},{12,16},{16,12},{20,24},{24,20},{5,9},{9,5},{13,17},{1... | collective-permute-start | bytes 3145736 | tf_op jit(solution)/shard_map/ppermute | solution.py:36
  16.4 13.5 %collective-permute-start.5 = (f32[512,128]{1,0:T(8,128)S(1)}, f32[512,128]{1,0:T(8,128)S(1)}, u32[]{:S(2)}, u32[]{:S(2)}) collective-permute-start(f32[512,128]{1,0:T(8,128)S(1)} %bitcast.37), channel_id=1, source_target_pairs={{5,6},{6,5},{9,10},{10,9},{13,14},{14,13},{17,18},{18,17},{21,22},... | collective-permute-start | bytes 786440 | tf_op jit(solution)/shard_map/ppermute | solution.py:54
  31.4 8.0 %collective-permute-start.6 = (f32[512,128]{1,0:T(8,128)S(1)}, f32[512,128]{1,0:T(8,128)S(1)}, u32[]{:S(2)}, u32[]{:S(2)}) collective-permute-start(f32[512,128]{1,0:T(8,128)S(1)} %collective-permute-done.5.refs_8_), channel_id=1, source_target_pairs={{19,2},{16,1},{15,30},{12,29},{51,34},{48,33},{47,62},{44,61},{83,... | collective-permute-start | bytes 786440 | tf_op jit(solution)/shard_map/ppermute | solution.py:55
  39.4 15.3 %collective-permute-start = (f32[1,4,32,128]{3,2,1,0:T(8,128)S(1)}, f32[1,4,32,128]{3,2,1,0:T(8,128)S(1)}, u32[]{:S(2)}, u32[]{:S(2)}) collective-permute-start(f32[1,4,32,128]{3,2,1,0:T(8,128)S(1)} %get-tuple-element.151), channel_id=1, source_target_pairs={{0,32},{32,64},{64,96},{96,0},{1,33},{33,65},{65,97},{97,1},{2,34}... | collective-permute-start | bytes 196616 | tf_op jit(solution)/shard_map/ppermute | solution.py:19
  53.9 40.8 %collective-permute-start.16 = (f32[64,32,128]{2,1,0:T(8,128)S(1)}, f32[64,32,128]{2,1,0:T(8,128)S(1)}, u32[]{:S(2)}, u32[]{:S(2)}) collective-permute-start(f32[64,32,128]{2,1,0:T(8,128)S(1)} %get-tuple-element.91), channel_id=1, source_target_pairs={{0,4},{4,0},{8,12},{12,8},{16,20},{20,16},{24,28},{28,24},{1,5},{5... | collective-permute-start | bytes 3145736 | tf_op jit(solution)/shard_map/ppermute | solution.py:36
  54.0 40.7 %collective-permute-start.17 = (f32[64,32,128]{2,1,0:T(8,128)S(1)}, f32[64,32,128]{2,1,0:T(8,128)S(1)}, u32[]{:S(2)}, u32[]{:S(2)}) collective-permute-start(f32[64,32,128]{2,1,0:T(8,128)S(1)} %get-tuple-element.92), channel_id=1, source_target_pairs={{4,8},{8,4},{12,16},{16,12},{20,24},{24,20},{5,9},{9,5},{13,17},{1... | collective-permute-start | bytes 3145736 | tf_op jit(solution)/shard_map/ppermute | solution.py:36
  64.2 38.9 %collective-permute-start.11 = (f32[64,32,128]{2,1,0:T(8,128)S(1)}, f32[64,32,128]{2,1,0:T(8,128)S(1)}, u32[]{:S(2)}, u32[]{:S(2)}) collective-permute-start(f32[64,32,128]{2,1,0:T(8,128)S(1)} %get-tuple-element.87), channel_id=1, source_target_pairs={{0,4},{4,0},{8,12},{12,8},{16,20},{20,16},{24,28},{28,24},{1,5},{5... | collective-permute-start | bytes 3145736 | tf_op jit(solution)/shard_map/ppermute | solution.py:36
  66.9 36.2 %collective-permute-start.12 = (f32[64,32,128]{2,1,0:T(8,128)S(1)}, f32[64,32,128]{2,1,0:T(8,128)S(1)}, u32[]{:S(2)}, u32[]{:S(2)}) collective-permute-start(f32[64,32,128]{2,1,0:T(8,128)S(1)} %get-tuple-element.88), channel_id=1, source_target_pairs={{4,8},{8,4},{12,16},{16,12},{20,24},{24,20},{5,9},{9,5},{13,17},{1... | collective-permute-start | bytes 3145736 | tf_op jit(solution)/shard_map/ppermute | solution.py:36
  67.6 9.0 %collective-permute-start.14 = (f32[512,128]{1,0:T(8,128)S(1)}, f32[512,128]{1,0:T(8,128)S(1)}, u32[]{:S(2)}, u32[]{:S(2)}) collective-permute-start(f32[512,128]{1,0:T(8,128)S(1)} %get-tuple-element.90), channel_id=1, source_target_pairs={{5,6},{6,5},{9,10},{10,9},{13,14},{14,13},{17,18},{18,17},{21,22},... | collective-permute-start | bytes 786440 | tf_op jit(solution)/shard_map/ppermute | solution.py:54
  78.2 14.0 %collective-permute-start.15 = (f32[512,128]{1,0:T(8,128)S(1)}, f32[512,128]{1,0:T(8,128)S(1)}, u32[]{:S(2)}, u32[]{:S(2)}) collective-permute-start(f32[512,128]{1,0:T(8,128)S(1)} %collective-permute-done.14.refs_8_), channel_id=1, source_target_pairs={{19,2},{16,1},{15,30},{12,29},{51,34},{48,33},{47,62},{44,61},{83,... | collective-permute-start | bytes 786440 | tf_op jit(solution)/shard_map/ppermute | solution.py:55
  97.8 36.3 %collective-permute-start.25 = (f32[64,32,128]{2,1,0:T(8,128)S(1)}, f32[64,32,128]{2,1,0:T(8,128)S(1)}, u32[]{:S(2)}, u32[]{:S(2)}) collective-permute-start(f32[64,32,128]{2,1,0:T(8,128)S(1)} %get-tuple-element.103), channel_id=1, source_target_pairs={{0,4},{4,0},{8,12},{12,8},{16,20},{20,16},{24,28},{28,24},{1,5},{5... | collective-permute-start | bytes 3145736 | tf_op jit(solution)/shard_map/ppermute | solution.py:36
  97.9 36.2 %collective-permute-start.26 = (f32[64,32,128]{2,1,0:T(8,128)S(1)}, f32[64,32,128]{2,1,0:T(8,128)S(1)}, u32[]{:S(2)}, u32[]{:S(2)}) collective-permute-start(f32[64,32,128]{2,1,0:T(8,128)S(1)} %get-tuple-element.104), channel_id=1, source_target_pairs={{4,8},{8,4},{12,16},{16,12},{20,24},{24,20},{5,9},{9,5},{13,17},{1... | collective-permute-start | bytes 3145736 | tf_op jit(solution)/shard_map/ppermute | solution.py:36
  106.2 39.4 %collective-permute-start.20 = (f32[64,32,128]{2,1,0:T(8,128)S(1)}, f32[64,32,128]{2,1,0:T(8,128)S(1)}, u32[]{:S(2)}, u32[]{:S(2)}) collective-permute-start(f32[64,32,128]{2,1,0:T(8,128)S(1)} %get-tuple-element.99), channel_id=1, source_target_pairs={{0,4},{4,0},{8,12},{12,8},{16,20},{20,16},{24,28},{28,24},{1,5},{5... | collective-permute-start | bytes 3145736 | tf_op jit(solution)/shard_map/ppermute | solution.py:36
  108.9 36.6 %collective-permute-start.21 = (f32[64,32,128]{2,1,0:T(8,128)S(1)}, f32[64,32,128]{2,1,0:T(8,128)S(1)}, u32[]{:S(2)}, u32[]{:S(2)}) collective-permute-start(f32[64,32,128]{2,1,0:T(8,128)S(1)} %get-tuple-element.100), channel_id=1, source_target_pairs={{4,8},{8,4},{12,16},{16,12},{20,24},{24,20},{5,9},{9,5},{13,17},{1... | collective-permute-start | bytes 3145736 | tf_op jit(solution)/shard_map/ppermute | solution.py:36
  109.6 8.8 %collective-permute-start.23 = (f32[512,128]{1,0:T(8,128)S(1)}, f32[512,128]{1,0:T(8,128)S(1)}, u32[]{:S(2)}, u32[]{:S(2)}) collective-permute-start(f32[512,128]{1,0:T(8,128)S(1)} %get-tuple-element.102), channel_id=1, source_target_pairs={{5,6},{6,5},{9,10},{10,9},{13,14},{14,13},{17,18},{18,17},{21,22},... | collective-permute-start | bytes 786440 | tf_op jit(solution)/shard_map/ppermute | solution.py:54
  120.0 14.2 %collective-permute-start.24 = (f32[512,128]{1,0:T(8,128)S(1)}, f32[512,128]{1,0:T(8,128)S(1)}, u32[]{:S(2)}, u32[]{:S(2)}) collective-permute-start(f32[512,128]{1,0:T(8,128)S(1)} %collective-permute-done.23.refs_8_), channel_id=1, source_target_pairs={{19,2},{16,1},{15,30},{12,29},{51,34},{48,33},{47,62},{44,61},{83,... | collective-permute-start | bytes 786440 | tf_op jit(solution)/shard_map/ppermute | solution.py:55
  135.7 29.9 %collective-permute-start.38 = (f32[32,32,128]{2,1,0:T(8,128)S(1)}, f32[32,32,128]{2,1,0:T(8,128)S(1)}, u32[]{:S(2)}, u32[]{:S(2)}) collective-permute-start(f32[32,32,128]{2,1,0:T(8,128)S(1)} %get-tuple-element.126), channel_id=1, source_target_pairs={{0,4},{4,0},{8,12},{12,8},{16,20},{20,16},{24,28},{28,24},{1,5},{5... | collective-permute-start | bytes 1572872 | tf_op jit(solution)/shard_map/ppermute | solution.py:36
  135.8 34.8 %collective-permute-start.39 = (f32[32,32,128]{2,1,0:T(8,128)S(1)}, f32[32,32,128]{2,1,0:T(8,128)S(1)}, u32[]{:S(2)}, u32[]{:S(2)}) collective-permute-start(f32[32,32,128]{2,1,0:T(8,128)S(1)} %get-tuple-element.127), channel_id=1, source_target_pairs={{4,8},{8,4},{12,16},{16,12},{20,24},{24,20},{5,9},{9,5},{13,17},{1... | collective-permute-start | bytes 1572872 | tf_op jit(solution)/shard_map/ppermute | solution.py:36
  149.3 11.0 %collective-permute-start.28 = (f32[1,4,32,128]{3,2,1,0:T(8,128)S(1)}, f32[1,4,32,128]{3,2,1,0:T(8,128)S(1)}, u32[]{:S(2)}, u32[]{:S(2)}) collective-permute-start(f32[1,4,32,128]{3,2,1,0:T(8,128)S(1)} %get-tuple-element.116), channel_id=1, source_target_pairs={{0,96},{32,0},{64,32},{96,64},{1,97},{33,1},{65,33},{97,65},{2,98}... | collective-permute-start | bytes 196616 | tf_op jit(solution)/shard_map/ppermute | solution.py:19
  151.4 19.9 %collective-permute-start.36 = (f32[32,32,128]{2,1,0:T(8,128)S(1)}, f32[32,32,128]{2,1,0:T(8,128)S(1)}, u32[]{:S(2)}, u32[]{:S(2)}) collective-permute-start(f32[32,32,128]{2,1,0:T(8,128)S(1)} %get-tuple-element.124), channel_id=1, source_target_pairs={{0,4},{4,0},{8,12},{12,8},{16,20},{20,16},{24,28},{28,24},{1,5},{5... | collective-permute-start | bytes 1572872 | tf_op jit(solution)/shard_map/ppermute | solution.py:36
  155.0 8.6 %collective-permute-start.32 = (f32[512,128]{1,0:T(8,128)S(1)}, f32[512,128]{1,0:T(8,128)S(1)}, u32[]{:S(2)}, u32[]{:S(2)}) collective-permute-start(f32[512,128]{1,0:T(8,128)S(1)} %get-tuple-element.120), channel_id=1, source_target_pairs={{5,6},{6,5},{9,10},{10,9},{13,14},{14,13},{17,18},{18,17},{21,22},... | collective-permute-start | bytes 786440 | tf_op jit(solution)/shard_map/ppermute | solution.py:54
  163.6 12.9 %collective-permute-start.33 = (f32[512,128]{1,0:T(8,128)S(1)}, f32[512,128]{1,0:T(8,128)S(1)}, u32[]{:S(2)}, u32[]{:S(2)}) collective-permute-start(f32[512,128]{1,0:T(8,128)S(1)} %collective-permute-done.32.refs_8_), channel_id=1, source_target_pairs={{19,2},{16,1},{15,30},{12,29},{51,34},{48,33},{47,62},{44,61},{83,... | collective-permute-start | bytes 786440 | tf_op jit(solution)/shard_map/ppermute | solution.py:55
  164.9 16.6 %collective-permute-start.37 = (f32[32,32,128]{2,1,0:T(8,128)S(1)}, f32[32,32,128]{2,1,0:T(8,128)S(1)}, u32[]{:S(2)}, u32[]{:S(2)}) collective-permute-start(f32[32,32,128]{2,1,0:T(8,128)S(1)} %get-tuple-element.125), channel_id=1, source_target_pairs={{4,8},{8,4},{12,16},{16,12},{20,24},{24,20},{5,9},{9,5},{13,17},{1... | collective-permute-start | bytes 1572872 | tf_op jit(solution)/shard_map/ppermute | solution.py:36
  165.6 21.7 %collective-permute-start.34 = (f32[32,32,128]{2,1,0:T(8,128)S(1)}, f32[32,32,128]{2,1,0:T(8,128)S(1)}, u32[]{:S(2)}, u32[]{:S(2)}) collective-permute-start(f32[32,32,128]{2,1,0:T(8,128)S(1)} %get-tuple-element.122), channel_id=1, source_target_pairs={{0,4},{4,0},{8,12},{12,8},{16,20},{20,16},{24,28},{28,24},{1,5},{5... | collective-permute-start | bytes 1572872 | tf_op jit(solution)/shard_map/ppermute | solution.py:36
  170.6 16.8 %collective-permute-start.35 = (f32[32,32,128]{2,1,0:T(8,128)S(1)}, f32[32,32,128]{2,1,0:T(8,128)S(1)}, u32[]{:S(2)}, u32[]{:S(2)}) collective-permute-start(f32[32,32,128]{2,1,0:T(8,128)S(1)} %get-tuple-element.123), channel_id=1, source_target_pairs={{4,8},{8,4},{12,16},{16,12},{20,24},{24,20},{5,9},{9,5},{13,17},{1... | collective-permute-start | bytes 1572872 | tf_op jit(solution)/shard_map/ppermute | solution.py:36
  171.3 25.7 %collective-permute-start.29 = (f32[32,32,128]{2,1,0:T(8,128)S(1)}, f32[32,32,128]{2,1,0:T(8,128)S(1)}, u32[]{:S(2)}, u32[]{:S(2)}) collective-permute-start(f32[32,32,128]{2,1,0:T(8,128)S(1)} %get-tuple-element.117), channel_id=1, source_target_pairs={{0,4},{4,0},{8,12},{12,8},{16,20},{20,16},{24,28},{28,24},{1,5},{5... | collective-permute-start | bytes 1572872 | tf_op jit(solution)/shard_map/ppermute | solution.py:36
  176.4 20.6 %collective-permute-start.30 = (f32[32,32,128]{2,1,0:T(8,128)S(1)}, f32[32,32,128]{2,1,0:T(8,128)S(1)}, u32[]{:S(2)}, u32[]{:S(2)}) collective-permute-start(f32[32,32,128]{2,1,0:T(8,128)S(1)} %get-tuple-element.118), channel_id=1, source_target_pairs={{4,8},{8,4},{12,16},{16,12},{20,24},{24,20},{5,9},{9,5},{13,17},{1... | collective-permute-start | bytes 1572872 | tf_op jit(solution)/shard_map/ppermute | solution.py:36
  181.5 36.1 %collective-permute-start.55 = (f32[2,16,32,128]{3,2,1,0:T(8,128)S(1)}, f32[2,16,32,128]{3,2,1,0:T(8,128)S(1)}, u32[]{:S(2)}, u32[]{:S(2)}) collective-permute-start(f32[2,16,32,128]{3,2,1,0:T(8,128)S(1)} %get-tuple-element.145), channel_id=1, source_target_pairs={{0,16},{4,20},{8,24},{12,28},{16,0},{20,4},{24,8},{28,12},{1,17},{... | collective-permute-start | bytes 1572872 | tf_op jit(solution)/shard_map/ppermute | solution.py:31
  191.0 27.4 %collective-permute-start.50 = (f32[2,16,32,128]{3,2,1,0:T(8,128)S(1)}, f32[2,16,32,128]{3,2,1,0:T(8,128)S(1)}, u32[]{:S(2)}, u32[]{:S(2)}) collective-permute-start(f32[2,16,32,128]{3,2,1,0:T(8,128)S(1)} %get-tuple-element.141), channel_id=1, source_target_pairs={{0,12},{4,8},{8,4},{12,0},{16,28},{20,24},{24,20},{28,16},{1,13},{... | collective-permute-start | bytes 1572872 | tf_op jit(solution)/shard_map/ppermute | solution.py:31
  197.0 23.6 %collective-permute-start.45 = (f32[2,16,32,128]{3,2,1,0:T(8,128)S(1)}, f32[2,16,32,128]{3,2,1,0:T(8,128)S(1)}, u32[]{:S(2)}, u32[]{:S(2)}) collective-permute-start(f32[2,16,32,128]{3,2,1,0:T(8,128)S(1)} %get-tuple-element.137), channel_id=1, source_target_pairs={{0,4},{4,0},{8,12},{12,8},{16,20},{20,16},{24,28},{28,24},{1,5},{5... | collective-permute-start | bytes 1572872 | tf_op jit(solution)/shard_map/ppermute | solution.py:31
  200.7 27.8 %collective-permute-start.40 = (f32[2,16,32,128]{3,2,1,0:T(8,128)S(1)}, f32[2,16,32,128]{3,2,1,0:T(8,128)S(1)}, u32[]{:S(2)}, u32[]{:S(2)}) collective-permute-start(f32[2,16,32,128]{3,2,1,0:T(8,128)S(1)} %get-tuple-element.133), channel_id=1, source_target_pairs={{0,16},{4,20},{8,24},{12,28},{16,0},{20,4},{24,8},{28,12},{1,17},{... | collective-permute-start | bytes 1572872 | tf_op jit(solution)/shard_map/ppermute | solution.py:31
  218.3 10.9 %collective-permute-start.56 = (f32[2,8,32,128]{3,2,1,0:T(8,128)S(1)}, f32[2,8,32,128]{3,2,1,0:T(8,128)S(1)}, u32[]{:S(2)}, u32[]{:S(2)}) collective-permute-start(f32[2,8,32,128]{3,2,1,0:T(8,128)S(1)} %get-tuple-element.147), channel_id=1, source_target_pairs={{0,4},{4,0},{8,12},{12,8},{16,20},{20,16},{24,28},{28,24},{1,5},{5... | collective-permute-start | bytes 786440 | tf_op jit(solution)/shard_map/ppermute | solution.py:31
  219.1 12.8 %collective-permute-start.51 = (f32[2,8,32,128]{3,2,1,0:T(8,128)S(1)}, f32[2,8,32,128]{3,2,1,0:T(8,128)S(1)}, u32[]{:S(2)}, u32[]{:S(2)}) collective-permute-start(f32[2,8,32,128]{3,2,1,0:T(8,128)S(1)} %get-tuple-element.143), channel_id=1, source_target_pairs={{0,4},{4,0},{8,12},{12,8},{16,20},{20,16},{24,28},{28,24},{1,5},{5... | collective-permute-start | bytes 786440 | tf_op jit(solution)/shard_map/ppermute | solution.py:31
  221.4 12.2 %collective-permute-start.46 = (f32[2,8,32,128]{3,2,1,0:T(8,128)S(1)}, f32[2,8,32,128]{3,2,1,0:T(8,128)S(1)}, u32[]{:S(2)}, u32[]{:S(2)}) collective-permute-start(f32[2,8,32,128]{3,2,1,0:T(8,128)S(1)} %get-tuple-element.139), channel_id=1, source_target_pairs={{0,12},{4,8},{8,4},{12,0},{16,28},{20,24},{24,20},{28,16},{1,13},{... | collective-permute-start | bytes 786440 | tf_op jit(solution)/shard_map/ppermute | solution.py:31
  229.1 7.9 %collective-permute-start.41 = (f32[2,8,32,128]{3,2,1,0:T(8,128)S(1)}, f32[2,8,32,128]{3,2,1,0:T(8,128)S(1)}, u32[]{:S(2)}, u32[]{:S(2)}) collective-permute-start(f32[2,8,32,128]{3,2,1,0:T(8,128)S(1)} %get-tuple-element.135), channel_id=1, source_target_pairs={{0,4},{4,0},{8,12},{12,8},{16,20},{20,16},{24,28},{28,24},{1,5},{5... | collective-permute-start | bytes 786440 | tf_op jit(solution)/shard_map/ppermute | solution.py:31
  229.3 10.4 %collective-permute-start.57 = (f32[2,8,32,128]{3,2,1,0:T(8,128)S(1)}, f32[2,8,32,128]{3,2,1,0:T(8,128)S(1)}, u32[]{:S(2)}, u32[]{:S(2)}) collective-permute-start(f32[2,8,32,128]{3,2,1,0:T(8,128)S(1)} %add.35), channel_id=1, source_target_pairs={{0,12},{4,8},{8,4},{12,0},{16,28},{20,24},{24,20},{28,16},{1,13},{... | collective-permute-start | bytes 786440 | tf_op jit(solution)/shard_map/ppermute | solution.py:31
  233.6 10.4 %collective-permute-start.47 = (f32[2,8,32,128]{3,2,1,0:T(8,128)S(1)}, f32[2,8,32,128]{3,2,1,0:T(8,128)S(1)}, u32[]{:S(2)}, u32[]{:S(2)}) collective-permute-start(f32[2,8,32,128]{3,2,1,0:T(8,128)S(1)} %add.31), channel_id=1, source_target_pairs={{0,16},{4,20},{8,24},{12,28},{16,0},{20,4},{24,8},{28,12},{1,17},{... | collective-permute-start | bytes 786440 | tf_op jit(solution)/shard_map/ppermute | solution.py:31
  237.0 8.7 %collective-permute-start.42 = (f32[2,8,32,128]{3,2,1,0:T(8,128)S(1)}, f32[2,8,32,128]{3,2,1,0:T(8,128)S(1)}, u32[]{:S(2)}, u32[]{:S(2)}) collective-permute-start(f32[2,8,32,128]{3,2,1,0:T(8,128)S(1)} %add.29), channel_id=1, source_target_pairs={{0,12},{4,8},{8,4},{12,0},{16,28},{20,24},{24,20},{28,16},{1,13},{... | collective-permute-start | bytes 786440 | tf_op jit(solution)/shard_map/ppermute | solution.py:31
  239.9 11.8 %collective-permute-start.53 = (f32[2,8,32,128]{3,2,1,0:T(8,128)S(1)}, f32[2,8,32,128]{3,2,1,0:T(8,128)S(1)}, u32[]{:S(2)}, u32[]{:S(2)}) collective-permute-start(f32[2,8,32,128]{3,2,1,0:T(8,128)S(1)} %add.34), channel_id=1, source_target_pairs={{0,4},{4,0},{8,12},{12,8},{16,20},{20,16},{24,28},{28,24},{1,5},{5... | collective-permute-start | bytes 786440 | tf_op jit(solution)/shard_map/ppermute | solution.py:31
  244.1 8.0 %collective-permute-start.48 = (f32[2,8,32,128]{3,2,1,0:T(8,128)S(1)}, f32[2,8,32,128]{3,2,1,0:T(8,128)S(1)}, u32[]{:S(2)}, u32[]{:S(2)}) collective-permute-start(f32[2,8,32,128]{3,2,1,0:T(8,128)S(1)} %add.32), channel_id=1, source_target_pairs={{0,12},{4,8},{8,4},{12,0},{16,28},{20,24},{24,20},{28,16},{1,13},{... | collective-permute-start | bytes 786440 | tf_op jit(solution)/shard_map/ppermute | solution.py:31
  245.8 11.5 %collective-permute-start.43 = (f32[2,8,32,128]{3,2,1,0:T(8,128)S(1)}, f32[2,8,32,128]{3,2,1,0:T(8,128)S(1)}, u32[]{:S(2)}, u32[]{:S(2)}) collective-permute-start(f32[2,8,32,128]{3,2,1,0:T(8,128)S(1)} %add.30), channel_id=1, source_target_pairs={{0,4},{4,0},{8,12},{12,8},{16,20},{20,16},{24,28},{28,24},{1,5},{5... | collective-permute-start | bytes 786440 | tf_op jit(solution)/shard_map/ppermute | solution.py:31
  246.1 11.3 %collective-permute-start.59 = (f32[2,2,8,32,128]{4,3,2,1,0:T(8,128)S(1)}, f32[2,2,8,32,128]{4,3,2,1,0:T(8,128)S(1)}, u32[]{:S(2)}, u32[]{:S(2)}) collective-permute-start(f32[2,2,8,32,128]{4,3,2,1,0:T(8,128)S(1)} %pad_maximum_fusion.3.refs_0_), channel_id=1, source_target_pairs={{0,16},{4,20},{8,24},{12,28},{16,0},{20,4},{24,8},{28,12},{1,17},{... | collective-permute-start | bytes 1572872 | tf_op jit(solution)/shard_map/ppermute | solution.py:31
  251.7 10.2 %collective-permute-start.54 = (f32[2,2,8,32,128]{4,3,2,1,0:T(8,128)S(1)}, f32[2,2,8,32,128]{4,3,2,1,0:T(8,128)S(1)}, u32[]{:S(2)}, u32[]{:S(2)}) collective-permute-start(f32[2,2,8,32,128]{4,3,2,1,0:T(8,128)S(1)} %pad_maximum_fusion.2.refs_0_), channel_id=1, source_target_pairs={{0,12},{4,8},{8,4},{12,0},{16,28},{20,24},{24,20},{28,16},{1,13},{... | collective-permute-start | bytes 1572872 | tf_op jit(solution)/shard_map/ppermute | solution.py:31
  252.1 16.4 %collective-permute-start.49 = (f32[2,2,8,32,128]{4,3,2,1,0:T(8,128)S(1)}, f32[2,2,8,32,128]{4,3,2,1,0:T(8,128)S(1)}, u32[]{:S(2)}, u32[]{:S(2)}) collective-permute-start(f32[2,2,8,32,128]{4,3,2,1,0:T(8,128)S(1)} %pad_maximum_fusion.1.refs_0_), channel_id=1, source_target_pairs={{0,4},{4,0},{8,12},{12,8},{16,20},{20,16},{24,28},{28,24},{1,5},{5... | collective-permute-start | bytes 1572872 | tf_op jit(solution)/shard_map/ppermute | solution.py:31
  257.3 16.9 %collective-permute-start.44 = (f32[2,2,8,32,128]{4,3,2,1,0:T(8,128)S(1)}, f32[2,2,8,32,128]{4,3,2,1,0:T(8,128)S(1)}, u32[]{:S(2)}, u32[]{:S(2)}) collective-permute-start(f32[2,2,8,32,128]{4,3,2,1,0:T(8,128)S(1)} %pad_maximum_fusion.refs_0_), channel_id=1, source_target_pairs={{0,16},{4,20},{8,24},{12,28},{16,0},{20,4},{24,8},{28,12},{1,17},{... | collective-permute-start | bytes 1572872 | tf_op jit(solution)/shard_map/ppermute | solution.py:31
  (19 other events, 270.6 us)

commit v3 on v2

--- a/solution.py
+++ b/solution.py
@@ -11,7 +11,7 @@
 STEPS = 4
 GRANT = 4 * 2**20
 ROUTES = ("over_near", "near", "far", "over_near")
-SCALES = ((0, "both"), (2, "both"), (1, "both"), (3, "own"), (3, "other"))
+SCALES = ((0, "own"), (2, "own"), (0, "other"), (3, "own"), (2, "other"), (1, "both"), (3, "other"))
 
 
 def ring(value, axis, shift):
@@ -436,7 +436,7 @@
             offset = number % 2 * quarter if len(chunks) == 4 else 0
             low, high = (y_low, y_high) if number >= len(chunks) // 2 else (u, u)
             number = number * 4 // len(chunks)
-            out = advance(u, (*received, *z_halos), low, high, k, s, ranges, offset, targets, 16)
+            out = advance(u, (*received, *z_halos), low, high, k, s, ranges, offset, targets, 32)
             targets = out[:3]
             arrived.append(exchange(out[3:5], "px"))
             borders += out[5:]
@@ -459,7 +459,7 @@
     for number, (row0, count) in enumerate(quarters):
         route = routes[ROUTES[number]]
         low, high = (y_low, y_high) if number >= 2 else (u, u)
-        end, send, keep = finish(u, (*x_halos[number], *z_halos), low, high, k, s, row0, count, end, route[3][0], 8)
+        end, send, keep = finish(u, (*x_halos[number], *z_halos), low, high, k, s, row0, count, end, route[3][0], 16)
         sums.append(line_sums(send, keep, route))
     result = None
     for number, wanted in SCALES:

time: 279 us -> 280 us (level)
  waiting for transfers between devices: 99.9 us -> 96.5 us
  starting transfers between devices: 102 us -> 105 us
    ppermute x4, waiting for transfers between devices: 32.3 us -> 27.9 us  [z_exchange(): over = lax.ppermute(odd, ('px', 'pz'), back)]
    ppermute x20, waiting for transfers between devices: 34.1 us -> 30.4 us  [swap(): lax.ppermute(value, 'px', [(i, i ^ mask) for i in range(lax.axis_size('px...]
    pallas_call x5 -> x7, Pallas kernels: 14.7 us -> 17.5 us  [scale(): pl.pallas_call(functools.partial(scale_body, parts=len(halves), inverse=1...]
    ppermute x4, waiting for transfers between devices: 15.8 us -> 18.6 us  [z_exchange(): odd = lax.ppermute(faces[1], ('px', 'pz'), direct + out)]
  transfers between devices with their start and end apart: 60 -> 60, of which waited for: 25 -> 23; matrix products, arithmetic and copies ran while one was open for 1% -> 1% of each run, Pallas kernels for 20% -> 19%
where the time goes in v3:
time: 280 us; the launch traced here: 276 us
  starting transfers between devices  105 us (38%)
  waiting for transfers between devices  96.5 us (34%)
  Pallas kernels  58.7 us (21%)
  local copies, waits for them, and re-layouts  11 us (4%)
  other arithmetic  3.19 us (1%)
    ppermute x20, starting transfers between devices, swap(): lax.ppermute(value, 'px', [(i, i ^ mask) for i in range(lax.axis_size('px...  33.2 us
    ppermute x24, starting transfers between devices, pair_swap(): lax.ppermute(value, axis, [(i, (i - odd ^ 1) + odd) for i in range(odd, d...  31.8 us
    ppermute x20, waiting for transfers between devices, swap(): lax.ppermute(value, 'px', [(i, i ^ mask) for i in range(lax.axis_size('px...  30.4 us
    ppermute x4, waiting for transfers between devices, z_exchange(): over = lax.ppermute(odd, ('px', 'pz'), back)  27.9 us
    ppermute x4, starting transfers between devices, z_exchange(): odd = lax.ppermute(faces[1], ('px', 'pz'), direct + out)  25.4 us
    pallas_call x8, Pallas kernels, advance(): pl.pallas_call(functools.partial(step_body, block=block, position=positio...  19.2 us
    ppermute x4, waiting for transfers between devices, z_exchange(): odd = lax.ppermute(faces[1], ('px', 'pz'), direct + out)  18.6 us
    pallas_call x7, Pallas kernels, scale(): pl.pallas_call(functools.partial(scale_body, parts=len(halves), inverse=1...  17.5 us
  transfers between devices with their start and end apart: 60, of which 23 were waited for; matrix products, arithmetic and copies ran while one was open for 1% of the time, Pallas kernels for 19%

profile of v3, /device:TPU:1, one launch (start us, length us, event | category | flops | bytes accessed | tf_op | source)
XLA Modules:
  0.0 275.6 jit_solution(4981565875919754037)
XLA Ops:
  0.6 2.6 pick.3
  6.0 2.7 pick.2
  8.7 3.3 %collective-permute-start.2 = (f32[64,32,128]{2,1,0:T(8,128)}, f32[64,32,128]{2,1,0:T(8,128)S(1)}, u32[]{:S(2)}, u32[]{:S(2)}) collective-permute-start(f32[64,32,128]{2,1,0:T(8,128)} %get-tuple-element.77), channel_id=1, source_target_pairs={{0,4},{4,0},{8,12},{12,8},{16,20},{20,16},{24,28},{28,24},{1,5},{5... | collective-permute-start | bytes 3145736 | tf_op jit(solution)/shard_map/ppermute | solution.py:36
  13.6 2.8 %broadcast_select_fusion = (f32[128,4,1,128]{3,2,1,0:T(1,128)S(1)}, f32[128,4,1,128]{3,2,1,0:T(1,128)S(1)}) fusion(pred[]{:T(512)S(6)} %eq.5, f32[128,4,32,128]{3,2,1,0:T(8,128)} %refs_2_.3), kind=kLoop, calls=%fused_computation.4 | loop fusion | flops 131072 | bytes 1048577 | tf_op jit(solution)/shard_map/jit(_where)/select_n | solution.py:61
  16.4 7.4 %collective-permute-start.5 = (f32[512,128]{1,0:T(8,128)S(1)}, f32[512,128]{1,0:T(8,128)S(1)}, u32[]{:S(2)}, u32[]{:S(2)}) collective-permute-start(f32[512,128]{1,0:T(8,128)S(1)} %bitcast.37), channel_id=1, source_target_pairs={{5,6},{6,5},{9,10},{10,9},{13,14},{14,13},{17,18},{18,17},{21,22},... | collective-permute-start | bytes 786440 | tf_op jit(solution)/shard_map/ppermute | solution.py:54
  23.8 6.1 %collective-permute-done.5.refs_8_ = f32[512,128]{1,0:T(8,128)S(1)} collective-permute-done((f32[512,128]{1,0:T(8,128)S(1)}, f32[512,128]{1,0:T(8,128)S(1)}, u32[]{:S(2)}, u32[]{:S(2)}) %collective-permute-start.5) | collective-permute-done | bytes 262176 | tf_op jit(solution)/shard_map/ppermute | solution.py:54
  33.6 5.8 %collective-permute-done.6.refs_9_ = f32[512,128]{1,0:T(8,128)S(1)} collective-permute-done((f32[512,128]{1,0:T(8,128)S(1)}, f32[512,128]{1,0:T(8,128)S(1)}, u32[]{:S(2)}, u32[]{:S(2)}) %collective-permute-start.6) | collective-permute-done | bytes 262176 | tf_op jit(solution)/shard_map/ppermute | solution.py:55
  40.7 3.4 %copy-done = f32[128,4,32,128]{3,2,1,0:T(8,128)S(1)} copy-done((f32[128,4,32,128]{3,2,1,0:T(8,128)S(1)}, f32[128,4,32,128]{3,2,1,0:T(8,128)}, u32[]{:S(2)}) %copy-start) | copy-done | bytes 8388632
  44.1 3.4 %copy-done.1 = f32[128,4,32,128]{3,2,1,0:T(8,128)S(1)} copy-done((f32[128,4,32,128]{3,2,1,0:T(8,128)S(1)}, f32[128,4,32,128]{3,2,1,0:T(8,128)}, u32[]{:S(2)}) %copy-start.1) | copy-done | bytes 8388632
  47.5 3.4 %copy-done.2 = f32[128,4,32,128]{3,2,1,0:T(8,128)S(1)} copy-done((f32[128,4,32,128]{3,2,1,0:T(8,128)S(1)}, f32[128,4,32,128]{3,2,1,0:T(8,128)}, u32[]{:S(2)}) %copy-start.2) | copy-done | bytes 8388632
  50.9 3.0 %advance.8 = (f32[128,4,32,128]{3,2,1,0:T(8,128)S(1)}, f32[512,128]{1,0:T(8,128)S(1)}, f32[512,128]{1,0:T(8,128)S(1)}, f32[64,32,128]{2,1,0:T(8,128)S(1)}, f32[64,32,128]{2,1,0:T(8,128)S(1)}) custom-call(f32[128,4,32,128]{3,2,1,0:T(8,128)S(1)} %copy-done, f32[128,4,32,128]{3,2,1,0:T(8,128)S(1)} %copy-done, f32[128,4,32,128]{3,2,1,0:T(8,128)S(1)} %copy-done, ...), custom_call_target="tpu_custom_call" | custom-call | tf_op jit(solution)/shard_map/advance/pallas_call | solution.py:232
  58.2 4.3 %advance.9 = (f32[128,4,32,128]{3,2,1,0:T(8,128)S(1)}, f32[512,128]{1,0:T(8,128)S(1)}, f32[512,128]{1,0:T(8,128)S(1)}, f32[64,32,128]{2,1,0:T(8,128)S(1)}, f32[6...) custom-call(f32[128,4,32,128]{3,2,1,0:T(8,128)S(1)} %copy-done, ...), custom_call_target="tpu_custom_call", output_to_operand_aliasing={{0}: (12, {}), {1}: (13, {}), {2}: (14, {})} | custom-call | tf_op jit(solution)/shard_map/advance/pallas_call | solution.py:232
  62.5 2.7 collective-permute-start.11
  65.9 5.7 %collective-permute-start.14 = (f32[512,128]{1,0:T(8,128)S(1)}, f32[512,128]{1,0:T(8,128)S(1)}, u32[]{:S(2)}, u32[]{:S(2)}) collective-permute-start(f32[512,128]{1,0:T(8,128)S(1)} %get-tuple-element.90), channel_id=1, source_target_pairs={{5,6},{6,5},{9,10},{10,9},{13,14},{14,13},{17,18},{18,17},{21,22},... | collective-permute-start | bytes 786440 | tf_op jit(solution)/shard_map/ppermute | solution.py:54
  71.6 3.3 %collective-permute-done.14.refs_8_ = f32[512,128]{1,0:T(8,128)S(1)} collective-permute-done((f32[512,128]{1,0:T(8,128)S(1)}, f32[512,128]{1,0:T(8,128)S(1)}, u32[]{:S(2)}, u32[]{:S(2)}) %collective-permute-start.14) | collective-permute-done | bytes 262176 | tf_op jit(solution)/shard_map/ppermute | solution.py:54
  77.7 12.7 %collective-permute-done.15.refs_9_ = f32[512,128]{1,0:T(8,128)S(1)} collective-permute-done((f32[512,128]{1,0:T(8,128)S(1)}, f32[512,128]{1,0:T(8,128)S(1)}, u32[]{:S(2)}, u32[]{:S(2)}) %collective-permute-start.15) | collective-permute-done | bytes 262176 | tf_op jit(solution)/shard_map/ppermute | solution.py:55
  90.4 2.6 collective-permute-start.10
  93.0 3.0 %advance.10 = (f32[128,4,32,128]{3,2,1,0:T(8,128)S(1)}, f32[512,128]{1,0:T(8,128)S(1)}, f32[512,128]{1,0:T(8,128)S(1)}, f32[64,32,128]{2,1,0:T(8,128)S(1)}, f32[64,32,128]{2,1,0:T(8,128)S(1)}) custom-call(f32[128,4,32,128]{3,2,1,0:T(8,128)S(1)} %get-tuple-element.84.refs_0_.refs_1_.refs_2_.refs_3_.refs_4_, ...), custom_call_target="tpu_custom_call" | custom-call | tf_op jit(solution)/shard_map/advance/pallas_call | solution.py:232
  97.0 4.3 %collective-permute-done.9.refs_3_ = f32[1,4,32,128]{3,2,1,0:T(8,128)S(1)} collective-permute-done((f32[1,4,32,128]{3,2,1,0:T(8,128)S(1)}, f32[1,4,32,128]{3,2,1,0:T(8,128)S(1)}, u32[]{:S(2)}, u32[]{:S(2)}) %collective-permute-start.9) | collective-permute-done | bytes 65568 | tf_op jit(solution)/shard_map/ppermute | solution.py:19
  101.3 3.0 %advance.11 = (f32[128,4,32,128]{3,2,1,0:T(8,128)S(1)}, f32[512,128]{1,0:T(8,128)S(1)}, f32[512,128]{1,0:T(8,128)S(1)}, f32[64,32,128]{2,1,0:T(8,128)S(1)}, f32[...) custom-call(f32[128,4,32,128]{3,2,1,0:T(8,128)S(1)} %get-tuple-eleme, ...), custom_call_target="tpu_custom_call", output_to_operand_aliasing={{0}: (12, {}), {1}: (13, {}), {2}: (14, {})} | custom-call | tf_op jit(solution)/shard_map/advance/pallas_call | solution.py:232
  104.3 2.9 %collective-permute-start.20 = (f32[64,32,128]{2,1,0:T(8,128)S(1)}, f32[64,32,128]{2,1,0:T(8,128)S(1)}, u32[]{:S(2)}, u32[]{:S(2)}) collective-permute-start(f32[64,32,128]{2,1,0:T(8,128)S(1)} %get-tuple-element.99), channel_id=1, source_target_pairs={{0,4},{4,0},{8,12},{12,8},{16,20},{20,16},{24,28},{28,24},{1,5},{5... | collective-permute-start | bytes 3145736 | tf_op jit(solution)/shard_map/ppermute | solution.py:36
  108.0 7.0 %collective-permute-start.23 = (f32[512,128]{1,0:T(8,128)S(1)}, f32[512,128]{1,0:T(8,128)S(1)}, u32[]{:S(2)}, u32[]{:S(2)}) collective-permute-start(f32[512,128]{1,0:T(8,128)S(1)} %get-tuple-element.102), channel_id=1, source_target_pairs={{5,6},{6,5},{9,10},{10,9},{13,14},{14,13},{17,18},{18,17},{21,22},... | collective-permute-start | bytes 786440 | tf_op jit(solution)/shard_map/ppermute | solution.py:54
  115.0 6.1 %collective-permute-done.23.refs_8_ = f32[512,128]{1,0:T(8,128)S(1)} collective-permute-done((f32[512,128]{1,0:T(8,128)S(1)}, f32[512,128]{1,0:T(8,128)S(1)}, u32[]{:S(2)}, u32[]{:S(2)}) %collective-permute-start.23) | collective-permute-done | bytes 262176 | tf_op jit(solution)/shard_map/ppermute | solution.py:54
  123.9 8.5 %collective-permute-done.24.refs_9_ = f32[512,128]{1,0:T(8,128)S(1)} collective-permute-done((f32[512,128]{1,0:T(8,128)S(1)}, f32[512,128]{1,0:T(8,128)S(1)}, u32[]{:S(2)}, u32[]{:S(2)}) %collective-permute-start.24) | collective-permute-done | bytes 262176 | tf_op jit(solution)/shard_map/ppermute | solution.py:55
  140.1 5.9 %collective-permute-done.20.refs_5_ = f32[64,32,128]{2,1,0:T(8,128)S(1)} collective-permute-done((f32[64,32,128]{2,1,0:T(8,128)S(1)}, f32[64,32,128]{2,1,0:T(8,128)S(1)}, u32[]{:S(2)}, u32[]{:S(2)}) %collective-permute-start.20) | collective-permute-done | bytes 1048608 | tf_op jit(solution)/shard_map/ppermute | solution.py:36
  151.7 3.1 %collective-permute-start.36 = (f32[32,32,128]{2,1,0:T(8,128)S(1)}, f32[32,32,128]{2,1,0:T(8,128)S(1)}, u32[]{:S(2)}, u32[]{:S(2)}) collective-permute-start(f32[32,32,128]{2,1,0:T(8,128)S(1)} %get-tuple-element.124), channel_id=1, source_target_pairs={{0,4},{4,0},{8,12},{12,8},{16,20},{20,16},{24,28},{28,24},{1,5},{5... | collective-permute-start | bytes 1572872 | tf_op jit(solution)/shard_map/ppermute | solution.py:36
  154.8 5.3 %collective-permute-start.32 = (f32[512,128]{1,0:T(8,128)S(1)}, f32[512,128]{1,0:T(8,128)S(1)}, u32[]{:S(2)}, u32[]{:S(2)}) collective-permute-start(f32[512,128]{1,0:T(8,128)S(1)} %get-tuple-element.120), channel_id=1, source_target_pairs={{5,6},{6,5},{9,10},{10,9},{13,14},{14,13},{17,18},{18,17},{21,22},... | collective-permute-start | bytes 786440 | tf_op jit(solution)/shard_map/ppermute | solution.py:54
  160.2 3.2 %collective-permute-done.32.refs_8_ = f32[512,128]{1,0:T(8,128)S(1)} collective-permute-done((f32[512,128]{1,0:T(8,128)S(1)}, f32[512,128]{1,0:T(8,128)S(1)}, u32[]{:S(2)}, u32[]{:S(2)}) %collective-permute-start.32) | collective-permute-done | bytes 262176 | tf_op jit(solution)/shard_map/ppermute | solution.py:54
  165.4 5.2 %collective-permute-start.34 = (f32[32,32,128]{2,1,0:T(8,128)S(1)}, f32[32,32,128]{2,1,0:T(8,128)S(1)}, u32[]{:S(2)}, u32[]{:S(2)}) collective-permute-start(f32[32,32,128]{2,1,0:T(8,128)S(1)} %get-tuple-element.122), channel_id=1, source_target_pairs={{0,4},{4,0},{8,12},{12,8},{16,20},{20,16},{24,28},{28,24},{1,5},{5... | collective-permute-start | bytes 1572872 | tf_op jit(solution)/shard_map/ppermute | solution.py:36
  171.4 4.0 %collective-permute-start.29 = (f32[32,32,128]{2,1,0:T(8,128)S(1)}, f32[32,32,128]{2,1,0:T(8,128)S(1)}, u32[]{:S(2)}, u32[]{:S(2)}) collective-permute-start(f32[32,32,128]{2,1,0:T(8,128)S(1)} %get-tuple-element.117), channel_id=1, source_target_pairs={{0,4},{4,0},{8,12},{12,8},{16,20},{20,16},{24,28},{28,24},{1,5},{5... | collective-permute-start | bytes 1572872 | tf_op jit(solution)/shard_map/ppermute | solution.py:36
  177.8 3.3 %finish.4 = (f32[128,4,32,128]{3,2,1,0:T(8,128)}, f32[2,16,32,128]{3,2,1,0:T(8,128)S(1)}, f32[2,16,32,128]{3,2,1,0:T(8,128)S(1)}) custom-call(s32[1]{0:T(128)} %get-tuple-element.75.bit, f32[128,4,32,128]{3,2,1,0:T(8,128)S(1)} %get-tuple-element.114.refs_0_.refs_1_.refs_2_.refs_3_.refs_4_, ...), custom_call_target="tpu_custom_call" | custom-call | tf_op jit(solution)/shard_map/finish/pallas_call | solution.py:298
  181.1 2.8 collective-permute-start.55
  183.8 3.3 %finish.5 = (f32[128,4,32,128]{3,2,1,0:T(8,128)}, f32[2,16,32,128]{3,2,1,0:T(8,128)S(1)}, f32[2,16,32,128]{3,2,1,0:T(8,128)S(1)}) custom-call(s32[1]{0:T(128)} %get-tuple-element.76.bit.piece_bit, f32[128,4,32,128]{3,2,1,0:T(8,128)S(1)} %get-tuple-element.114.refs_0_.refs_1_.refs_2_.refs_3_.refs_4_, ...), custom_call_target="tpu_custom_call", output_to_operand_aliasing={{0}: (13, {})} | custom-call | tf_op jit(solution)/shard_map/finish/pallas_call | solution.py:298
  187.1 3.3 %finish.6 = (f32[128,4,32,128]{3,2,1,0:T(8,128)}, f32[2,16,32,128]{3,2,1,0:T(8,128)S(1)}, f32[2,16,32,128]{3,2,1,0:T(8,128)S(1)}) custom-call(s32[1]{0:T(128)} %get-tuple-element.121.bit.piece_bit, f32[128,4,32,128]{3,2,1,0:T(8,128)S(1)} %get-tuple-element.114.refs_0_.refs_1_.refs_2_.refs_3_.refs_4_, ...), custom_call_target="tpu_custom_call", output_to_operand_aliasing={{0}: (13, {})} | custom-call | tf_op jit(solution)/shard_map/finish/pallas_call | solution.py:298
  190.5 5.7 %collective-permute-start.50 = (f32[2,16,32,128]{3,2,1,0:T(8,128)S(1)}, f32[2,16,32,128]{3,2,1,0:T(8,128)S(1)}, u32[]{:S(2)}, u32[]{:S(2)}) collective-permute-start(f32[2,16,32,128]{3,2,1,0:T(8,128)S(1)} %get-tuple-element.141), channel_id=1, source_target_pairs={{0,12},{4,8},{8,4},{12,0},{16,28},{20,24},{24,20},{28,16},{1,13},{... | collective-permute-start | bytes 1572872 | tf_op jit(solution)/shard_map/ppermute | solution.py:31
  197.3 3.4 %finish.7 = (f32[128,4,32,128]{3,2,1,0:T(8,128)}, f32[2,16,32,128]{3,2,1,0:T(8,128)S(1)}, f32[2,16,32,128]{3,2,1,0:T(8,128)S(1)}) custom-call(s32[1]{0:T(128)} %get-tuple-element.75.bit, f32[128,4,32,128]{3,2,1,0:T(8,128)S(1)} %get-tuple-element.114.refs_0_.refs_1_.refs_2_.refs_3_.refs_4_, ...), custom_call_target="tpu_custom_call", output_to_operand_aliasing={{0}: (13, {})} | custom-call | tf_op jit(solution)/shard_map/finish/pallas_call | solution.py:298
  200.6 6.8 %collective-permute-start.40 = (f32[2,16,32,128]{3,2,1,0:T(8,128)S(1)}, f32[2,16,32,128]{3,2,1,0:T(8,128)S(1)}, u32[]{:S(2)}, u32[]{:S(2)}) collective-permute-start(f32[2,16,32,128]{3,2,1,0:T(8,128)S(1)} %get-tuple-element.133), channel_id=1, source_target_pairs={{0,16},{4,20},{8,24},{12,28},{16,0},{20,4},{24,8},{28,12},{1,17},{... | collective-permute-start | bytes 1572872 | tf_op jit(solution)/shard_map/ppermute | solution.py:31
  207.4 10.0 %collective-permute-done.55 = f32[2,16,32,128]{3,2,1,0:T(8,128)S(1)} collective-permute-done((f32[2,16,32,128]{3,2,1,0:T(8,128)S(1)}, f32[2,16,32,128]{3,2,1,0:T(8,128)S(1)}, u32[]{:S(2)}, u32[]{:S(2)}) %collective-permute-start.55) | collective-permute-done | bytes 524320 | tf_op jit(solution)/shard_map/ppermute | solution.py:31
  221.2 2.6 collective-permute-start.46
  223.9 4.7 %collective-permute-done.40 = f32[2,16,32,128]{3,2,1,0:T(8,128)S(1)} collective-permute-done((f32[2,16,32,128]{3,2,1,0:T(8,128)S(1)}, f32[2,16,32,128]{3,2,1,0:T(8,128)S(1)}, u32[]{:S(2)}, u32[]{:S(2)}) %collective-permute-start.40) | collective-permute-done | bytes 524320 | tf_op jit(solution)/shard_map/ppermute | solution.py:31
  233.6 3.2 %collective-permute-done.41 = f32[2,8,32,128]{3,2,1,0:T(8,128)S(1)} collective-permute-done((f32[2,8,32,128]{3,2,1,0:T(8,128)S(1)}, f32[2,8,32,128]{3,2,1,0:T(8,128)S(1)}, u32[]{:S(2)}, u32[]{:S(2)}) %collective-permute-start.41) | collective-permute-done | bytes 262176 | tf_op jit(solution)/shard_map/ppermute | solution.py:31
  236.9 2.6 collective-permute-start.42
  241.2 3.0 %collective-permute-done.47 = f32[2,8,32,128]{3,2,1,0:T(8,128)S(1)} collective-permute-done((f32[2,8,32,128]{3,2,1,0:T(8,128)S(1)}, f32[2,8,32,128]{3,2,1,0:T(8,128)S(1)}, u32[]{:S(2)}, u32[]{:S(2)}) %collective-permute-start.47) | collective-permute-done | bytes 262176 | tf_op jit(solution)/shard_map/ppermute | solution.py:31
  247.4 4.1 %collective-permute-done.53 = f32[2,8,32,128]{3,2,1,0:T(8,128)S(1)} collective-permute-done((f32[2,8,32,128]{3,2,1,0:T(8,128)S(1)}, f32[2,8,32,128]{3,2,1,0:T(8,128)S(1)}, u32[]{:S(2)}, u32[]{:S(2)}) %collective-permute-start.53) | collective-permute-done | bytes 262176 | tf_op jit(solution)/shard_map/ppermute | solution.py:31
  252.0 5.1 %collective-permute-done.43 = f32[2,8,32,128]{3,2,1,0:T(8,128)S(1)} collective-permute-done((f32[2,8,32,128]{3,2,1,0:T(8,128)S(1)}, f32[2,8,32,128]{3,2,1,0:T(8,128)S(1)}, u32[]{:S(2)}, u32[]{:S(2)}) %collective-permute-start.43) | collective-permute-done | bytes 262176 | tf_op jit(solution)/shard_map/ppermute | solution.py:31
  262.8 2.4 scale.9.refs_1_
  269.9 3.3 %scale.12.refs_1_ = f32[128,4,32,128]{3,2,1,0:T(8,128)} custom-call(s32[1]{0:T(128)} %get-tuple-element.76.bit.piece_bit, s32[1]{0:T(128)} %get-tuple-element.121.bit.piece_bit, f32[128,4,32,128]{3,2,1,0:T(8,128)S(1)} %copy-done.4, f32[2,2,8,32,128]{4,3,2,1,0:T(8,128)S(1)} %pad_maximum_fusion.1.refs_0_, ...), custom_call_target="tpu_custom_call", output_to_operand_aliasing={{}: (5, {})} | custom-call | tf_op jit(solution)/shard_map/scale/pallas_call | solution.py:396
  273.2 2.4 scale.13
  (127 shorter events, 66.0 us)
Async XLA Ops:
  3.3 37.4 %collective-permute-start.7 = (f32[64,32,128]{2,1,0:T(8,128)}, f32[64,32,128]{2,1,0:T(8,128)S(1)}, u32[]{:S(2)}, u32[]{:S(2)}) collective-permute-start(f32[64,32,128]{2,1,0:T(8,128)} %get-tuple-element.79), channel_id=1, source_target_pairs={{0,4},{4,0},{8,12},{12,8},{16,20},{20,16},{24,28},{28,24},{1,5},{5... | collective-permute-start | bytes 3145736 | tf_op jit(solution)/shard_map/ppermute | solution.py:36
  5.3 35.4 %collective-permute-start.8 = (f32[64,32,128]{2,1,0:T(8,128)}, f32[64,32,128]{2,1,0:T(8,128)S(1)}, u32[]{:S(2)}, u32[]{:S(2)}) collective-permute-start(f32[64,32,128]{2,1,0:T(8,128)} %get-tuple-element.80), channel_id=1, source_target_pairs={{4,8},{8,4},{12,16},{16,12},{20,24},{24,20},{5,9},{9,5},{13,17},{1... | collective-permute-start | bytes 3145736 | tf_op jit(solution)/shard_map/ppermute | solution.py:36
  8.7 49.5 %collective-permute-start.2 = (f32[64,32,128]{2,1,0:T(8,128)}, f32[64,32,128]{2,1,0:T(8,128)S(1)}, u32[]{:S(2)}, u32[]{:S(2)}) collective-permute-start(f32[64,32,128]{2,1,0:T(8,128)} %get-tuple-element.77), channel_id=1, source_target_pairs={{0,4},{4,0},{8,12},{12,8},{16,20},{20,16},{24,28},{28,24},{1,5},{5... | collective-permute-start | bytes 3145736 | tf_op jit(solution)/shard_map/ppermute | solution.py:36
  12.0 46.2 %collective-permute-start.3 = (f32[64,32,128]{2,1,0:T(8,128)}, f32[64,32,128]{2,1,0:T(8,128)}, u32[]{:S(2)}, u32[]{:S(2)}) collective-permute-start(f32[64,32,128]{2,1,0:T(8,128)} %get-tuple-element.78), channel_id=1, source_target_pairs={{4,8},{8,4},{12,16},{16,12},{20,24},{24,20},{5,9},{9,5},{13,17},{1... | collective-permute-start | bytes 3145736 | tf_op jit(solution)/shard_map/ppermute | solution.py:36
  16.4 13.5 %collective-permute-start.5 = (f32[512,128]{1,0:T(8,128)S(1)}, f32[512,128]{1,0:T(8,128)S(1)}, u32[]{:S(2)}, u32[]{:S(2)}) collective-permute-start(f32[512,128]{1,0:T(8,128)S(1)} %bitcast.37), channel_id=1, source_target_pairs={{5,6},{6,5},{9,10},{10,9},{13,14},{14,13},{17,18},{18,17},{21,22},... | collective-permute-start | bytes 786440 | tf_op jit(solution)/shard_map/ppermute | solution.py:54
  31.4 8.0 %collective-permute-start.6 = (f32[512,128]{1,0:T(8,128)S(1)}, f32[512,128]{1,0:T(8,128)S(1)}, u32[]{:S(2)}, u32[]{:S(2)}) collective-permute-start(f32[512,128]{1,0:T(8,128)S(1)} %collective-permute-done.5.refs_8_), channel_id=1, source_target_pairs={{19,2},{16,1},{15,30},{12,29},{51,34},{48,33},{47,62},{44,61},{83,... | collective-permute-start | bytes 786440 | tf_op jit(solution)/shard_map/ppermute | solution.py:55
  39.4 15.3 %collective-permute-start = (f32[1,4,32,128]{3,2,1,0:T(8,128)S(1)}, f32[1,4,32,128]{3,2,1,0:T(8,128)S(1)}, u32[]{:S(2)}, u32[]{:S(2)}) collective-permute-start(f32[1,4,32,128]{3,2,1,0:T(8,128)S(1)} %get-tuple-element.151), channel_id=1, source_target_pairs={{0,32},{32,64},{64,96},{96,0},{1,33},{33,65},{65,97},{97,1},{2,34}... | collective-permute-start | bytes 196616 | tf_op jit(solution)/shard_map/ppermute | solution.py:19
  53.8 39.2 %collective-permute-start.16 = (f32[64,32,128]{2,1,0:T(8,128)S(1)}, f32[64,32,128]{2,1,0:T(8,128)S(1)}, u32[]{:S(2)}, u32[]{:S(2)}) collective-permute-start(f32[64,32,128]{2,1,0:T(8,128)S(1)} %get-tuple-element.91), channel_id=1, source_target_pairs={{0,4},{4,0},{8,12},{12,8},{16,20},{20,16},{24,28},{28,24},{1,5},{5... | collective-permute-start | bytes 3145736 | tf_op jit(solution)/shard_map/ppermute | solution.py:36
  53.9 39.1 %collective-permute-start.17 = (f32[64,32,128]{2,1,0:T(8,128)S(1)}, f32[64,32,128]{2,1,0:T(8,128)S(1)}, u32[]{:S(2)}, u32[]{:S(2)}) collective-permute-start(f32[64,32,128]{2,1,0:T(8,128)S(1)} %get-tuple-element.92), channel_id=1, source_target_pairs={{4,8},{8,4},{12,16},{16,12},{20,24},{24,20},{5,9},{9,5},{13,17},{1... | collective-permute-start | bytes 3145736 | tf_op jit(solution)/shard_map/ppermute | solution.py:36
  62.5 38.8 %collective-permute-start.11 = (f32[64,32,128]{2,1,0:T(8,128)S(1)}, f32[64,32,128]{2,1,0:T(8,128)S(1)}, u32[]{:S(2)}, u32[]{:S(2)}) collective-permute-start(f32[64,32,128]{2,1,0:T(8,128)S(1)} %get-tuple-element.87), channel_id=1, source_target_pairs={{0,4},{4,0},{8,12},{12,8},{16,20},{20,16},{24,28},{28,24},{1,5},{5... | collective-permute-start | bytes 3145736 | tf_op jit(solution)/shard_map/ppermute | solution.py:36
  65.2 36.1 %collective-permute-start.12 = (f32[64,32,128]{2,1,0:T(8,128)S(1)}, f32[64,32,128]{2,1,0:T(8,128)S(1)}, u32[]{:S(2)}, u32[]{:S(2)}) collective-permute-start(f32[64,32,128]{2,1,0:T(8,128)S(1)} %get-tuple-element.88), channel_id=1, source_target_pairs={{4,8},{8,4},{12,16},{16,12},{20,24},{24,20},{5,9},{9,5},{13,17},{1... | collective-permute-start | bytes 3145736 | tf_op jit(solution)/shard_map/ppermute | solution.py:36
  65.9 9.0 %collective-permute-start.14 = (f32[512,128]{1,0:T(8,128)S(1)}, f32[512,128]{1,0:T(8,128)S(1)}, u32[]{:S(2)}, u32[]{:S(2)}) collective-permute-start(f32[512,128]{1,0:T(8,128)S(1)} %get-tuple-element.90), channel_id=1, source_target_pairs={{5,6},{6,5},{9,10},{10,9},{13,14},{14,13},{17,18},{18,17},{21,22},... | collective-permute-start | bytes 786440 | tf_op jit(solution)/shard_map/ppermute | solution.py:54
  76.4 14.0 %collective-permute-start.15 = (f32[512,128]{1,0:T(8,128)S(1)}, f32[512,128]{1,0:T(8,128)S(1)}, u32[]{:S(2)}, u32[]{:S(2)}) collective-permute-start(f32[512,128]{1,0:T(8,128)S(1)} %collective-permute-done.14.refs_8_), channel_id=1, source_target_pairs={{19,2},{16,1},{15,30},{12,29},{51,34},{48,33},{47,62},{44,61},{83,... | collective-permute-start | bytes 786440 | tf_op jit(solution)/shard_map/ppermute | solution.py:55
  96.0 36.8 %collective-permute-start.25 = (f32[64,32,128]{2,1,0:T(8,128)S(1)}, f32[64,32,128]{2,1,0:T(8,128)S(1)}, u32[]{:S(2)}, u32[]{:S(2)}) collective-permute-start(f32[64,32,128]{2,1,0:T(8,128)S(1)} %get-tuple-element.103), channel_id=1, source_target_pairs={{0,4},{4,0},{8,12},{12,8},{16,20},{20,16},{24,28},{28,24},{1,5},{5... | collective-permute-start | bytes 3145736 | tf_op jit(solution)/shard_map/ppermute | solution.py:36
  96.1 36.7 %collective-permute-start.26 = (f32[64,32,128]{2,1,0:T(8,128)S(1)}, f32[64,32,128]{2,1,0:T(8,128)S(1)}, u32[]{:S(2)}, u32[]{:S(2)}) collective-permute-start(f32[64,32,128]{2,1,0:T(8,128)S(1)} %get-tuple-element.104), channel_id=1, source_target_pairs={{4,8},{8,4},{12,16},{16,12},{20,24},{24,20},{5,9},{9,5},{13,17},{1... | collective-permute-start | bytes 3145736 | tf_op jit(solution)/shard_map/ppermute | solution.py:36
  104.3 41.7 %collective-permute-start.20 = (f32[64,32,128]{2,1,0:T(8,128)S(1)}, f32[64,32,128]{2,1,0:T(8,128)S(1)}, u32[]{:S(2)}, u32[]{:S(2)}) collective-permute-start(f32[64,32,128]{2,1,0:T(8,128)S(1)} %get-tuple-element.99), channel_id=1, source_target_pairs={{0,4},{4,0},{8,12},{12,8},{16,20},{20,16},{24,28},{28,24},{1,5},{5... | collective-permute-start | bytes 3145736 | tf_op jit(solution)/shard_map/ppermute | solution.py:36
  107.3 38.7 %collective-permute-start.21 = (f32[64,32,128]{2,1,0:T(8,128)S(1)}, f32[64,32,128]{2,1,0:T(8,128)S(1)}, u32[]{:S(2)}, u32[]{:S(2)}) collective-permute-start(f32[64,32,128]{2,1,0:T(8,128)S(1)} %get-tuple-element.100), channel_id=1, source_target_pairs={{4,8},{8,4},{12,16},{16,12},{20,24},{24,20},{5,9},{9,5},{13,17},{1... | collective-permute-start | bytes 3145736 | tf_op jit(solution)/shard_map/ppermute | solution.py:36
  108.0 13.1 %collective-permute-start.23 = (f32[512,128]{1,0:T(8,128)S(1)}, f32[512,128]{1,0:T(8,128)S(1)}, u32[]{:S(2)}, u32[]{:S(2)}) collective-permute-start(f32[512,128]{1,0:T(8,128)S(1)} %get-tuple-element.102), channel_id=1, source_target_pairs={{5,6},{6,5},{9,10},{10,9},{13,14},{14,13},{17,18},{18,17},{21,22},... | collective-permute-start | bytes 786440 | tf_op jit(solution)/shard_map/ppermute | solution.py:54
  122.6 9.8 %collective-permute-start.24 = (f32[512,128]{1,0:T(8,128)S(1)}, f32[512,128]{1,0:T(8,128)S(1)}, u32[]{:S(2)}, u32[]{:S(2)}) collective-permute-start(f32[512,128]{1,0:T(8,128)S(1)} %collective-permute-done.23.refs_8_), channel_id=1, source_target_pairs={{19,2},{16,1},{15,30},{12,29},{51,34},{48,33},{47,62},{44,61},{83,... | collective-permute-start | bytes 786440 | tf_op jit(solution)/shard_map/ppermute | solution.py:55
  134.3 31.1 %collective-permute-start.38 = (f32[32,32,128]{2,1,0:T(8,128)S(1)}, f32[32,32,128]{2,1,0:T(8,128)S(1)}, u32[]{:S(2)}, u32[]{:S(2)}) collective-permute-start(f32[32,32,128]{2,1,0:T(8,128)S(1)} %get-tuple-element.126), channel_id=1, source_target_pairs={{0,4},{4,0},{8,12},{12,8},{16,20},{20,16},{24,28},{28,24},{1,5},{5... | collective-permute-start | bytes 1572872 | tf_op jit(solution)/shard_map/ppermute | solution.py:36
  134.4 36.2 %collective-permute-start.39 = (f32[32,32,128]{2,1,0:T(8,128)S(1)}, f32[32,32,128]{2,1,0:T(8,128)S(1)}, u32[]{:S(2)}, u32[]{:S(2)}) collective-permute-start(f32[32,32,128]{2,1,0:T(8,128)S(1)} %get-tuple-element.127), channel_id=1, source_target_pairs={{4,8},{8,4},{12,16},{16,12},{20,24},{24,20},{5,9},{9,5},{13,17},{1... | collective-permute-start | bytes 1572872 | tf_op jit(solution)/shard_map/ppermute | solution.py:36
  150.9 9.3 %collective-permute-start.28 = (f32[1,4,32,128]{3,2,1,0:T(8,128)S(1)}, f32[1,4,32,128]{3,2,1,0:T(8,128)S(1)}, u32[]{:S(2)}, u32[]{:S(2)}) collective-permute-start(f32[1,4,32,128]{3,2,1,0:T(8,128)S(1)} %get-tuple-element.116), channel_id=1, source_target_pairs={{0,96},{32,0},{64,32},{96,64},{1,97},{33,1},{65,33},{97,65},{2,98}... | collective-permute-start | bytes 196616 | tf_op jit(solution)/shard_map/ppermute | solution.py:19
  151.7 19.6 %collective-permute-start.36 = (f32[32,32,128]{2,1,0:T(8,128)S(1)}, f32[32,32,128]{2,1,0:T(8,128)S(1)}, u32[]{:S(2)}, u32[]{:S(2)}) collective-permute-start(f32[32,32,128]{2,1,0:T(8,128)S(1)} %get-tuple-element.124), channel_id=1, source_target_pairs={{0,4},{4,0},{8,12},{12,8},{16,20},{20,16},{24,28},{28,24},{1,5},{5... | collective-permute-start | bytes 1572872 | tf_op jit(solution)/shard_map/ppermute | solution.py:36
  154.8 8.6 %collective-permute-start.32 = (f32[512,128]{1,0:T(8,128)S(1)}, f32[512,128]{1,0:T(8,128)S(1)}, u32[]{:S(2)}, u32[]{:S(2)}) collective-permute-start(f32[512,128]{1,0:T(8,128)S(1)} %get-tuple-element.120), channel_id=1, source_target_pairs={{5,6},{6,5},{9,10},{10,9},{13,14},{14,13},{17,18},{18,17},{21,22},... | collective-permute-start | bytes 786440 | tf_op jit(solution)/shard_map/ppermute | solution.py:54
  163.4 12.9 %collective-permute-start.33 = (f32[512,128]{1,0:T(8,128)S(1)}, f32[512,128]{1,0:T(8,128)S(1)}, u32[]{:S(2)}, u32[]{:S(2)}) collective-permute-start(f32[512,128]{1,0:T(8,128)S(1)} %collective-permute-done.32.refs_8_), channel_id=1, source_target_pairs={{19,2},{16,1},{15,30},{12,29},{51,34},{48,33},{47,62},{44,61},{83,... | collective-permute-start | bytes 786440 | tf_op jit(solution)/shard_map/ppermute | solution.py:55
  164.7 16.3 %collective-permute-start.37 = (f32[32,32,128]{2,1,0:T(8,128)S(1)}, f32[32,32,128]{2,1,0:T(8,128)S(1)}, u32[]{:S(2)}, u32[]{:S(2)}) collective-permute-start(f32[32,32,128]{2,1,0:T(8,128)S(1)} %get-tuple-element.125), channel_id=1, source_target_pairs={{4,8},{8,4},{12,16},{16,12},{20,24},{24,20},{5,9},{9,5},{13,17},{1... | collective-permute-start | bytes 1572872 | tf_op jit(solution)/shard_map/ppermute | solution.py:36
  165.4 21.7 %collective-permute-start.34 = (f32[32,32,128]{2,1,0:T(8,128)S(1)}, f32[32,32,128]{2,1,0:T(8,128)S(1)}, u32[]{:S(2)}, u32[]{:S(2)}) collective-permute-start(f32[32,32,128]{2,1,0:T(8,128)S(1)} %get-tuple-element.122), channel_id=1, source_target_pairs={{0,4},{4,0},{8,12},{12,8},{16,20},{20,16},{24,28},{28,24},{1,5},{5... | collective-permute-start | bytes 1572872 | tf_op jit(solution)/shard_map/ppermute | solution.py:36
  170.7 16.5 %collective-permute-start.35 = (f32[32,32,128]{2,1,0:T(8,128)S(1)}, f32[32,32,128]{2,1,0:T(8,128)S(1)}, u32[]{:S(2)}, u32[]{:S(2)}) collective-permute-start(f32[32,32,128]{2,1,0:T(8,128)S(1)} %get-tuple-element.123), channel_id=1, source_target_pairs={{4,8},{8,4},{12,16},{16,12},{20,24},{24,20},{5,9},{9,5},{13,17},{1... | collective-permute-start | bytes 1572872 | tf_op jit(solution)/shard_map/ppermute | solution.py:36
  171.4 25.9 %collective-permute-start.29 = (f32[32,32,128]{2,1,0:T(8,128)S(1)}, f32[32,32,128]{2,1,0:T(8,128)S(1)}, u32[]{:S(2)}, u32[]{:S(2)}) collective-permute-start(f32[32,32,128]{2,1,0:T(8,128)S(1)} %get-tuple-element.117), channel_id=1, source_target_pairs={{0,4},{4,0},{8,12},{12,8},{16,20},{20,16},{24,28},{28,24},{1,5},{5... | collective-permute-start | bytes 1572872 | tf_op jit(solution)/shard_map/ppermute | solution.py:36
  176.3 20.9 %collective-permute-start.30 = (f32[32,32,128]{2,1,0:T(8,128)S(1)}, f32[32,32,128]{2,1,0:T(8,128)S(1)}, u32[]{:S(2)}, u32[]{:S(2)}) collective-permute-start(f32[32,32,128]{2,1,0:T(8,128)S(1)} %get-tuple-element.118), channel_id=1, source_target_pairs={{4,8},{8,4},{12,16},{16,12},{20,24},{24,20},{5,9},{9,5},{13,17},{1... | collective-permute-start | bytes 1572872 | tf_op jit(solution)/shard_map/ppermute | solution.py:36
  181.1 36.4 %collective-permute-start.55 = (f32[2,16,32,128]{3,2,1,0:T(8,128)S(1)}, f32[2,16,32,128]{3,2,1,0:T(8,128)S(1)}, u32[]{:S(2)}, u32[]{:S(2)}) collective-permute-start(f32[2,16,32,128]{3,2,1,0:T(8,128)S(1)} %get-tuple-element.145), channel_id=1, source_target_pairs={{0,16},{4,20},{8,24},{12,28},{16,0},{20,4},{24,8},{28,12},{1,17},{... | collective-permute-start | bytes 1572872 | tf_op jit(solution)/shard_map/ppermute | solution.py:31
  190.5 27.8 %collective-permute-start.50 = (f32[2,16,32,128]{3,2,1,0:T(8,128)S(1)}, f32[2,16,32,128]{3,2,1,0:T(8,128)S(1)}, u32[]{:S(2)}, u32[]{:S(2)}) collective-permute-start(f32[2,16,32,128]{3,2,1,0:T(8,128)S(1)} %get-tuple-element.141), channel_id=1, source_target_pairs={{0,12},{4,8},{8,4},{12,0},{16,28},{20,24},{24,20},{28,16},{1,13},{... | collective-permute-start | bytes 1572872 | tf_op jit(solution)/shard_map/ppermute | solution.py:31
  196.1 24.4 %collective-permute-start.45 = (f32[2,16,32,128]{3,2,1,0:T(8,128)S(1)}, f32[2,16,32,128]{3,2,1,0:T(8,128)S(1)}, u32[]{:S(2)}, u32[]{:S(2)}) collective-permute-start(f32[2,16,32,128]{3,2,1,0:T(8,128)S(1)} %get-tuple-element.137), channel_id=1, source_target_pairs={{0,4},{4,0},{8,12},{12,8},{16,20},{20,16},{24,28},{28,24},{1,5},{5... | collective-permute-start | bytes 1572872 | tf_op jit(solution)/shard_map/ppermute | solution.py:31
  200.6 28.0 %collective-permute-start.40 = (f32[2,16,32,128]{3,2,1,0:T(8,128)S(1)}, f32[2,16,32,128]{3,2,1,0:T(8,128)S(1)}, u32[]{:S(2)}, u32[]{:S(2)}) collective-permute-start(f32[2,16,32,128]{3,2,1,0:T(8,128)S(1)} %get-tuple-element.133), channel_id=1, source_target_pairs={{0,16},{4,20},{8,24},{12,28},{16,0},{20,4},{24,8},{28,12},{1,17},{... | collective-permute-start | bytes 1572872 | tf_op jit(solution)/shard_map/ppermute | solution.py:31
  218.2 11.2 %collective-permute-start.56 = (f32[2,8,32,128]{3,2,1,0:T(8,128)S(1)}, f32[2,8,32,128]{3,2,1,0:T(8,128)S(1)}, u32[]{:S(2)}, u32[]{:S(2)}) collective-permute-start(f32[2,8,32,128]{3,2,1,0:T(8,128)S(1)} %get-tuple-element.147), channel_id=1, source_target_pairs={{0,4},{4,0},{8,12},{12,8},{16,20},{20,16},{24,28},{28,24},{1,5},{5... | collective-permute-start | bytes 786440 | tf_op jit(solution)/shard_map/ppermute | solution.py:31
  219.0 12.7 %collective-permute-start.51 = (f32[2,8,32,128]{3,2,1,0:T(8,128)S(1)}, f32[2,8,32,128]{3,2,1,0:T(8,128)S(1)}, u32[]{:S(2)}, u32[]{:S(2)}) collective-permute-start(f32[2,8,32,128]{3,2,1,0:T(8,128)S(1)} %get-tuple-element.143), channel_id=1, source_target_pairs={{0,4},{4,0},{8,12},{12,8},{16,20},{20,16},{24,28},{28,24},{1,5},{5... | collective-permute-start | bytes 786440 | tf_op jit(solution)/shard_map/ppermute | solution.py:31
  221.2 12.2 %collective-permute-start.46 = (f32[2,8,32,128]{3,2,1,0:T(8,128)S(1)}, f32[2,8,32,128]{3,2,1,0:T(8,128)S(1)}, u32[]{:S(2)}, u32[]{:S(2)}) collective-permute-start(f32[2,8,32,128]{3,2,1,0:T(8,128)S(1)} %get-tuple-element.139), channel_id=1, source_target_pairs={{0,12},{4,8},{8,4},{12,0},{16,28},{20,24},{24,20},{28,16},{1,13},{... | collective-permute-start | bytes 786440 | tf_op jit(solution)/shard_map/ppermute | solution.py:31
  229.3 7.6 %collective-permute-start.41 = (f32[2,8,32,128]{3,2,1,0:T(8,128)S(1)}, f32[2,8,32,128]{3,2,1,0:T(8,128)S(1)}, u32[]{:S(2)}, u32[]{:S(2)}) collective-permute-start(f32[2,8,32,128]{3,2,1,0:T(8,128)S(1)} %get-tuple-element.135), channel_id=1, source_target_pairs={{0,4},{4,0},{8,12},{12,8},{16,20},{20,16},{24,28},{28,24},{1,5},{5... | collective-permute-start | bytes 786440 | tf_op jit(solution)/shard_map/ppermute | solution.py:31
  229.4 10.1 %collective-permute-start.57 = (f32[2,8,32,128]{3,2,1,0:T(8,128)S(1)}, f32[2,8,32,128]{3,2,1,0:T(8,128)S(1)}, u32[]{:S(2)}, u32[]{:S(2)}) collective-permute-start(f32[2,8,32,128]{3,2,1,0:T(8,128)S(1)} %add.35), channel_id=1, source_target_pairs={{0,12},{4,8},{8,4},{12,0},{16,28},{20,24},{24,20},{28,16},{1,13},{... | collective-permute-start | bytes 786440 | tf_op jit(solution)/shard_map/ppermute | solution.py:31
  231.7 7.9 %collective-permute-start.52 = (f32[2,8,32,128]{3,2,1,0:T(8,128)S(1)}, f32[2,8,32,128]{3,2,1,0:T(8,128)S(1)}, u32[]{:S(2)}, u32[]{:S(2)}) collective-permute-start(f32[2,8,32,128]{3,2,1,0:T(8,128)S(1)} %add.33), channel_id=1, source_target_pairs={{0,16},{4,20},{8,24},{12,28},{16,0},{20,4},{24,8},{28,12},{1,17},{... | collective-permute-start | bytes 786440 | tf_op jit(solution)/shard_map/ppermute | solution.py:31
  233.5 10.7 %collective-permute-start.47 = (f32[2,8,32,128]{3,2,1,0:T(8,128)S(1)}, f32[2,8,32,128]{3,2,1,0:T(8,128)S(1)}, u32[]{:S(2)}, u32[]{:S(2)}) collective-permute-start(f32[2,8,32,128]{3,2,1,0:T(8,128)S(1)} %add.31), channel_id=1, source_target_pairs={{0,16},{4,20},{8,24},{12,28},{16,0},{20,4},{24,8},{28,12},{1,17},{... | collective-permute-start | bytes 786440 | tf_op jit(solution)/shard_map/ppermute | solution.py:31
  236.9 8.6 %collective-permute-start.42 = (f32[2,8,32,128]{3,2,1,0:T(8,128)S(1)}, f32[2,8,32,128]{3,2,1,0:T(8,128)S(1)}, u32[]{:S(2)}, u32[]{:S(2)}) collective-permute-start(f32[2,8,32,128]{3,2,1,0:T(8,128)S(1)} %add.29), channel_id=1, source_target_pairs={{0,12},{4,8},{8,4},{12,0},{16,28},{20,24},{24,20},{28,16},{1,13},{... | collective-permute-start | bytes 786440 | tf_op jit(solution)/shard_map/ppermute | solution.py:31
  239.7 11.8 %collective-permute-start.53 = (f32[2,8,32,128]{3,2,1,0:T(8,128)S(1)}, f32[2,8,32,128]{3,2,1,0:T(8,128)S(1)}, u32[]{:S(2)}, u32[]{:S(2)}) collective-permute-start(f32[2,8,32,128]{3,2,1,0:T(8,128)S(1)} %add.34), channel_id=1, source_target_pairs={{0,4},{4,0},{8,12},{12,8},{16,20},{20,16},{24,28},{28,24},{1,5},{5... | collective-permute-start | bytes 786440 | tf_op jit(solution)/shard_map/ppermute | solution.py:31
  245.5 11.6 %collective-permute-start.43 = (f32[2,8,32,128]{3,2,1,0:T(8,128)S(1)}, f32[2,8,32,128]{3,2,1,0:T(8,128)S(1)}, u32[]{:S(2)}, u32[]{:S(2)}) collective-permute-start(f32[2,8,32,128]{3,2,1,0:T(8,128)S(1)} %add.30), channel_id=1, source_target_pairs={{0,4},{4,0},{8,12},{12,8},{16,20},{20,16},{24,28},{28,24},{1,5},{5... | collective-permute-start | bytes 786440 | tf_op jit(solution)/shard_map/ppermute | solution.py:31
  245.9 16.9 %collective-permute-start.59 = (f32[2,2,8,32,128]{4,3,2,1,0:T(8,128)S(1)}, f32[2,2,8,32,128]{4,3,2,1,0:T(8,128)S(1)}, u32[]{:S(2)}, u32[]{:S(2)}) collective-permute-start(f32[2,2,8,32,128]{4,3,2,1,0:T(8,128)S(1)} %pad_maximum_fusion.3.refs_0_), channel_id=1, source_target_pairs={{0,16},{4,20},{8,24},{12,28},{16,0},{20,4},{24,8},{28,12},{1,17},{... | collective-permute-start | bytes 1572872 | tf_op jit(solution)/shard_map/ppermute | solution.py:31
  251.5 16.0 %collective-permute-start.54 = (f32[2,2,8,32,128]{4,3,2,1,0:T(8,128)S(1)}, f32[2,2,8,32,128]{4,3,2,1,0:T(8,128)S(1)}, u32[]{:S(2)}, u32[]{:S(2)}) collective-permute-start(f32[2,2,8,32,128]{4,3,2,1,0:T(8,128)S(1)} %pad_maximum_fusion.2.refs_0_), channel_id=1, source_target_pairs={{0,12},{4,8},{8,4},{12,0},{16,28},{20,24},{24,20},{28,16},{1,13},{... | collective-permute-start | bytes 1572872 | tf_op jit(solution)/shard_map/ppermute | solution.py:31
  251.7 18.2 %collective-permute-start.49 = (f32[2,2,8,32,128]{4,3,2,1,0:T(8,128)S(1)}, f32[2,2,8,32,128]{4,3,2,1,0:T(8,128)S(1)}, u32[]{:S(2)}, u32[]{:S(2)}) collective-permute-start(f32[2,2,8,32,128]{4,3,2,1,0:T(8,128)S(1)} %pad_maximum_fusion.1.refs_0_), channel_id=1, source_target_pairs={{0,4},{4,0},{8,12},{12,8},{16,20},{20,16},{24,28},{28,24},{1,5},{5... | collective-permute-start | bytes 1572872 | tf_op jit(solution)/shard_map/ppermute | solution.py:31
  257.2 16.1 %collective-permute-start.44 = (f32[2,2,8,32,128]{4,3,2,1,0:T(8,128)S(1)}, f32[2,2,8,32,128]{4,3,2,1,0:T(8,128)S(1)}, u32[]{:S(2)}, u32[]{:S(2)}) collective-permute-start(f32[2,2,8,32,128]{4,3,2,1,0:T(8,128)S(1)} %pad_maximum_fusion.refs_0_), channel_id=1, source_target_pairs={{0,16},{4,20},{8,24},{12,28},{16,0},{20,4},{24,8},{28,12},{1,17},{... | collective-permute-start | bytes 1572872 | tf_op jit(solution)/shard_map/ppermute | solution.py:31
  (19 other events, 267.8 us)
